TPU v7x, 16 devices: a whole 2x2x2 slice. The times are simulated.
16 devices in a mesh: vp: 2 (over z), dp: 8 (over y, x, core).
Axes of the slice: x: 2, y: 2, z: 2, core: 2. Of those that a mesh axis runs over, the one named last changes fastest.
Arguments:
- hidden: bfloat16 [64, 512, 768], P('dp')
- mask_pos: int32 [64, 77], P('dp')
- labels: int32 [64, 77], P('dp')
- w_trans: bfloat16 [768, 768], replicated
- b_trans: float32 [768], replicated
- ln_gain: float32 [768], replicated
- ln_bias: float32 [768], replicated
- emb_table: bfloat16 [50304, 768], P('vp')
- b_vocab: float32 [50304], P('vp')
Outputs:
- output 1: float32 [], replicated
- output 2: bfloat16 [64, 512, 768], P('dp')
- output 3: float32 [768, 768], replicated
- output 4: float32 [768], replicated
- output 5: float32 [768], replicated
- output 6: float32 [768], replicated
- output 7: float32 [50304, 768], P('vp')
- output 8: float32 [50304], P('vp')
All inputs are finite; a program needn't handle non-finite values.
Results may differ from a plain program's by a relative error of at most 0.0106917.
Values sent between devices are 32-bit elements.
A program may use at most 1 GiB of HBM per device.

v0:
```python
import jax
import jax.numpy as jnp
from jax import lax
from jax.sharding import PartitionSpec as P

LN_EPS = 1e-5


def head_norm(pre_act, ln_gain, ln_bias):
    gelu_out = jax.nn.gelu(pre_act, approximate=False)
    row_mean = jnp.mean(gelu_out, axis=-1, keepdims=True)
    centered = gelu_out - row_mean
    row_var = jnp.mean(centered * centered, axis=-1, keepdims=True)
    return centered * lax.rsqrt(row_var + LN_EPS) * ln_gain + ln_bias


def solution(mesh):
    n_groups = mesh.shape["dp"]

    def local_step(hidden, mask_pos, labels, w_trans, b_trans, ln_gain, ln_bias, emb_table, b_vocab):
        n_rows, seq_len = hidden.shape[0], hidden.shape[1]
        n_masks = mask_pos.shape[1]
        shard_rows = emb_table.shape[0]
        n_tokens = n_rows * n_masks * n_groups
        row_start = lax.axis_index("vp") * shard_rows
        pos_onehot = (mask_pos[:, :, None] == jnp.arange(seq_len)[None, None, :]).astype(jnp.bfloat16)
        masked_h = jnp.einsum("clt,cte->cle", pos_onehot, hidden, preferred_element_type=jnp.float32).astype(jnp.bfloat16)
        pre_act = jnp.einsum("cle,ef->clf", masked_h, w_trans, preferred_element_type=jnp.float32) + b_trans
        u_norm, head_vjp = jax.vjp(head_norm, pre_act, ln_gain, ln_bias)
        u_bf16 = u_norm.astype(jnp.bfloat16)
        logits = jnp.einsum("cle,se->cls", u_bf16, emb_table, preferred_element_type=jnp.float32) + b_vocab
        local_max = jnp.max(logits, axis=-1)
        local_sum = jnp.sum(jnp.exp(logits - local_max[..., None]), axis=-1)
        is_label = (labels - row_start)[..., None] == jnp.arange(shard_rows)[None, None, :]
        label_logit = jnp.sum(jnp.where(is_label, logits, 0.0), axis=-1)
        tok_stats = lax.all_gather(jnp.stack([local_max, local_sum, label_logit]), "vp")
        global_max = jnp.max(tok_stats[:, 0], axis=0)
        log_norm = global_max + jnp.log(jnp.sum(tok_stats[:, 1] * jnp.exp(tok_stats[:, 0] - global_max), axis=0))
        target = jnp.sum(tok_stats[:, 2], axis=0)
        mlm_loss = lax.psum(jnp.sum(log_norm - target), "dp") / n_tokens
        d_logits = (jnp.exp(logits - log_norm[..., None]) - is_label.astype(jnp.float32)) / n_tokens
        d_logits_bf = d_logits.astype(jnp.bfloat16)
        d_emb_table = lax.psum(jnp.einsum("cls,cle->se", d_logits_bf, u_bf16, preferred_element_type=jnp.float32), "dp")
        d_b_vocab = lax.psum(jnp.sum(d_logits, axis=(0, 1)), "dp")
        du_part = jnp.einsum("cls,se->cle", d_logits_bf, emb_table, preferred_element_type=jnp.float32).astype(jnp.bfloat16)
        d_unorm = lax.psum(du_part.astype(jnp.float32), "vp")
        d_pre, d_ln_gain, d_ln_bias = head_vjp(d_unorm)
        d_pre_bf = d_pre.astype(jnp.bfloat16)
        d_w_trans = lax.psum(jnp.einsum("cle,clf->ef", masked_h, d_pre_bf, preferred_element_type=jnp.float32), "dp")
        vec_grads = lax.psum(jnp.stack([jnp.sum(d_pre, axis=(0, 1)), d_ln_gain, d_ln_bias]), "dp")
        d_masked = jnp.einsum("clf,ef->cle", d_pre_bf, w_trans, preferred_element_type=jnp.float32).astype(jnp.bfloat16)
        d_hidden = jnp.einsum("clt,cle->cte", pos_onehot, d_masked, preferred_element_type=jnp.float32).astype(jnp.bfloat16)
        return mlm_loss, d_hidden, d_w_trans, vec_grads[0], vec_grads[1], vec_grads[2], d_emb_table, d_b_vocab

    in_specs = (P("dp", None, None), P("dp", None), P("dp", None), P(None, None), P(None), P(None), P(None), P("vp", None), P("vp"))
    out_specs = (P(), P("dp", None, None), P(None, None), P(None), P(None), P(None), P("vp", None), P("vp"))
    return jax.shard_map(local_step, mesh=mesh, in_specs=in_specs, out_specs=out_specs, check_vma=False)
```

profile of v0, /device:TPU:0, one launch (start us, length us, event | category | flops | bytes accessed | tf_op | source)
XLA Modules:
  0.0 1189.7 jit_solution(3724499962667002747)
XLA Ops:
  7.2 0.0 copy-start
  7.2 0.0 all-reduce.5.cloned.1.call-start
  7.2 0.0 copy-start.15
  7.2 4.1 convolution_convert_fusion.2
  11.4 0.0 copy-done
  11.4 0.0 copy-done.15
  11.4 0.0 copy-start.7
  11.4 1.3 fusion.28
  12.7 0.0 copy-done.7
  12.7 0.0 copy-start.2
  12.7 5.6 fusion.37
  18.3 0.0 copy-done.2
  18.3 0.0 copy-start.18
  18.4 0.4 multiply_reduce_fusion.2
  18.7 0.0 copy-start.13
  18.7 0.6 copy-done.13
  19.3 0.0 copy-done.17
  19.3 0.0 copy-done.9
  19.3 0.0 copy-done.12
  19.4 41.3 %add_reduce_fusion = (f32[8,77]{1,0:T(8,128)S(1)}, f32[8,77,25152]{2,1,0:T(8,128)}) fusion(f32[25152]{0:T(1024)S(1)} %copy-done.9, bf16[25152,768]{1,0:T(8,128)(2,1)} %param.16, f32[8,77,768]{2,1,0:T(8,128)S(1)} %get-tuple-element.28, f32[768]{0:T(1024)S(1)} %copy-done.18, f32[768]{0:T(1024)S(1)} %copy-done.12, f32[8,77]{1,0:T(8,128)S(1)} %fusion.33, ...), kind=kOutput, calls=%fused_computation.4 | convolution fusion | flops 23831570432 | bytes 102614496 | tf_op jit(solution)/shard_map/cle,se->cls/dot_general | solution.py:31
  60.7 30.6 %exponential_reduce_fusion = (f32[8,77]{1,0:T(8,128)S(1)}, f32[8,77]{1,0:T(8,128)S(1)}) fusion(f32[8,77,25152]{2,1,0:T(8,128)} %get-tuple-element.32, f32[8,77]{1,0:T(8,128)S(1)} %get-tuple-element.31, f32[25152]{0:T(1024)S(1)} %copy-done.9, s32[8,77]{1,0:T(8,128)S(1)} %broadcast_subtract_fusion), kind=kLoop, calls=%fused_computation.3 | loop fusion | flops 92960560 | bytes 62084992 | tf_op jit(solution)/shard_map/reduce_sum | solution.py:33
  91.3 5.8 all-gather
  97.2 0.6 subtract_reduce_fusion
  97.8 46.7 %fusion.15 = f32[8,77,768]{2,1,0:T(8,128)} fusion(bf16[25152,768]{1,0:T(8,128)(2,1)} %param.16, f32[8,77,25152]{2,1,0:T(8,128)} %get-tuple-element.32, f32[8,77]{1,0:T(8,128)S(1)} %get-tuple-element.26, s32[8,77]{1,0:T(8,128)S(1)} %broadcast_subtract_fusion, f32[25152]{0:T(1024)S(1)} %copy-done.9), kind=kOutput, calls=%fused_computation.43 | convolution fusion | flops 23907620864 | bytes 102605888 | tf_op jit(solution)/shard_map/cls,se->cle/dot_general | solution.py:45
  144.5 0.0 all-reduce.5.cloned.1.call-update
  144.5 0.3 all-reduce.7.cloned.1.call-start
  144.8 57.7 %convolution_bitcast_fusion = f32[25152,768]{1,0:T(8,128)} fusion(f32[8,77,768]{2,1,0:T(8,128)S(1)} %get-tuple-element.28, f32[768]{0:T(1024)S(1)} %copy-done.18, f32[768]{0:T(1024)S(1)} %copy-done.12, f32[8,77]{1,0:T(8,128)S(1)} %fusion.33, f32[8,77]{1,0:T(8,128)S(1)} %broadcast_multiply_fusion, f32[8,77,25152]{2,1,0:T(8,128)} %get-tuple-element.32, ...), kind=kOutput, calls=%fused_computation.5 | convolution fusion | flops 23909040128 | bytes 141250432 | tf_op jit(solution)/shard_map/cls,cle->se/dot_general | solution.py:43
  202.5 26.5 %fusion = f32[25152]{0:T(1024)} fusion(f32[8,77,25152]{2,1,0:T(8,128)} %get-tuple-element.32, f32[8,77]{1,0:T(8,128)S(1)} %get-tuple-element.26, s32[8,77]{1,0:T(8,128)S(1)} %broadcast_subtract_fusion, f32[25152]{0:T(1024)S(1)} %copy-done.9), kind=kLoop, calls=%fused_computation.6 | loop fusion | flops 108430272 | bytes 62180672 | tf_op jit(solution)/shard_map/reduce_sum | solution.py:44
  229.0 2.1 multiply_reduce_fusion.1
  231.2 0.0 copy-done.1
  231.2 0.0 copy-start.3
  231.2 0.0 copy-start.4
  231.2 0.0 copy-start.16
  231.2 1.1 multiply_reduce_fusion
  232.3 0.4 copy-done.3
  232.7 0.6 copy-done.4
  233.3 1.8 fusion.36
  235.2 0.0 copy-start.5
  235.2 0.9 copy-done.5
  236.1 2.5 convolution_bitcast_fusion.1
  238.7 0.0 all-reduce.7.cloned.1.call-update
  238.7 24.5 %all-reduce = (f32[]{:T(128)}, f32[3,768]{1,0:T(4,128)S(1)}) all-reduce(f32[]{:T(128)} %get-tuple-element.25, f32[3,768]{1,0:T(4,128)S(1)} %pad_maximum_fusion.1), channel_id=1, replica_groups=mesh['vp'=2,'dp'=8] {'dp'}, use_global_device_ids=true, to_apply=%region_9.10 | all-reduce | flops 2305 | bytes 18440 | tf_op jit(solution)/shard_map/psum | solution.py:40
  263.9 0.6 slice_reduce_fusion.1
  264.6 4.6 convolution_convert_fusion
  269.2 858.2 %all-reduce.7.cloned.1.call-done = (f32[768,768]{1,0:T(8,128)}, f32[25152,768]{1,0:T(8,128)}, f32[25152]{0:T(1024)}) async-done(((f32[768,768]{1,0:T(8,128)}, f32[25152,768]{1,0:T(8,128)}, f32[25152]{0:T(1024)}), (f32[768,768]{1,0:T(8,128)}, f32[25152,768]{1,0:T(8,128)}, f32[25152]{0:T(1024)})) %all-reduce.7.cloned.1.call-update) | async-done | bytes 79726864 | tf_op jit(solution)/shard_map/psum | solution.py:49
  1127.4 3.2 copy.24
  1130.6 50.5 %copy.25 = f32[25152,768]{1,0:T(8,128)} copy(f32[25152,768]{1,0:T(8,128)} %get-tuple-element.41) | data formatting | bytes 154533888
  1181.1 0.7 copy.26
  (30 shorter events, 0.1 us)
Async XLA Ops:
  7.2 4.2 copy-start
  7.2 221.8 %all-reduce.5.cloned.1.call-start = ((), (), s32[]{:S(2)}) async-start(), calls=%async_computation | async-start | bytes 3932160 | tf_op jit(solution)/shard_map/psum | solution.py:46
  7.2 4.1 copy-start.15
  11.4 1.3 copy-start.7
  12.7 5.6 copy-start.2
  18.3 1.0 copy-start.17
  18.3 1.0 copy-start.9
  18.3 1.0 copy-start.12
  18.3 1.0 copy-start.18
  18.7 0.6 copy-start.13
  144.5 982.8 %all-reduce.7.cloned.1.call-start = ((), (), s32[]{:S(2)}) async-start(), calls=%async_computation.1 | async-start | bytes 159457280 | tf_op jit(solution)/shard_map/psum | solution.py:49
  229.0 2.1 copy-start.14
  229.0 2.2 copy-start.1
  231.2 1.5 copy-start.3
  231.2 2.1 copy-start.4
  231.2 2.1 copy-start.16
  233.3 2.8 copy-start.8
  235.2 0.9 copy-start.5
  238.7 25.9 %copy-start.6 = (bf16[8,77,768]{2,1,0:T(8,128)(2,1)S(1)}, bf16[8,77,768]{2,1,0:T(8,128)(2,1)}, u32[]{:S(2)}) copy-start(bf16[8,77,768]{2,1,0:T(8,128)(2,1)} %copy-done.5) | copy-start | bytes 2838532
  238.7 25.9 %copy-start.10 = (s32[8,77]{1,0:T(8,128)S(1)}, s32[8,77]{1,0:T(8,128)}, u32[]{:S(2)}) copy-start(s32[8,77]{1,0:T(8,128)} %param.10) | copy-start | bytes 7396
  1130.6 50.5 %copy-start.11 = (f32[25152]{0:T(1024)S(1)}, f32[25152]{0:T(1024)}, u32[]{:S(2)}) copy-start(f32[25152]{0:T(1024)} %get-tuple-element.42) | copy-start | bytes 301828
Sparse Core Ops, SparseCore 0:
  144.7 57.6 all-reduce.4
  238.8 888.5 all-reduce.6
where the time goes:
time: 1190 us
  waiting for transfers between devices  858 us (72%)
  matrix products  158 us (13%)
  other arithmetic  68.8 us (6%)
  local copies, waits for them, and re-layouts  57.6 us (5%)
  blocking collectives  30.4 us (3%)
  between operations  16.1 us (1%)
    psum x1, waiting for transfers between devices, local_step(): lax.psum(jnp.einsum('cle,clf->ef', masked_h, d_pre_bf, preferred_element_...  858 us
    dot_general x1, matrix products, local_step(): jnp.einsum('cls,cle->se', d_logits_bf, u_bf16, preferred_element_type=jnp...  57.7 us
    unnamed x41, local copies, waits for them, and re-layouts  57 us
    dot_general x1, matrix products, local_step(): jnp.einsum('cls,se->cle', d_logits_bf, emb_table, preferred_element_type=...  46.7 us
    dot_general x1, matrix products, local_step(): jnp.einsum('cle,se->cls', u_bf16, emb_table, preferred_element_type=jnp.f...  41.3 us
    reduce_sum x1, other arithmetic, local_step(): local_sum = jnp.sum(jnp.exp(logits - local_max[..., None]), axis=-1)  30.6 us
    reduce_sum x1, other arithmetic, local_step(): d_b_vocab = lax.psum(jnp.sum(d_logits, axis=(0, 1)), 'dp')  26.5 us
    psum x1, blocking collectives, local_step(): mlm_loss = lax.psum(jnp.sum(log_norm - target), 'dp') / n_tokens  24.5 us
  transfers between devices with their start and end apart: 2, of which 1 were waited for; matrix products, arithmetic and copies ran while one was open for 8% of the time, Pallas kernels for 0%

commit v1 on v0

v1 whole, which is shorter than its diff:
```python
import functools

import jax
import jax.numpy as jnp
from jax import lax
from jax.experimental import pallas as pl
from jax.experimental.pallas import tpu as pltpu
from jax.sharding import PartitionSpec as P


LN_EPS = 1e-5

BF16, F32, I32 = jnp.bfloat16, jnp.float32, jnp.int32
SLOTS = 80
VT = 2304
CHUNK, ROWS = 768, 128
SHARE_CHUNKS, SHARE_TILE = 4, 528
LOCAL_TILES, LOCAL_TILE = 6, 688
LOCAL_CALLS = 3
TOK_CHUNK = 1280
VMEM_ROWS = 44
COST_SCALE = 4
OFF = 1e30
MIB = 2 ** 20


def head_norm(pre_act, ln_gain, ln_bias):
    gelu_out = jax.nn.gelu(pre_act, approximate=False)
    row_mean = jnp.mean(gelu_out, axis=-1, keepdims=True)
    centered = gelu_out - row_mean
    row_var = jnp.mean(centered * centered, axis=-1, keepdims=True)
    return centered * lax.rsqrt(row_var + LN_EPS) * ln_gain + ln_bias


def dot_nt(a, b):
    return lax.dot_general(a, b, (((1,), (1,)), ((), ())), preferred_element_type=F32)


def to_lanes(row):
    return jnp.broadcast_to(row, (128, row.shape[1])).T


def stats_kernel(n_steps, u_ref, emb_ref, bias_ref, col_ref, lab_row_ref, logit_ref, stat_ref, m_ref, s_ref, t_ref, lab_ref):
    step = pl.program_id(0)
    n_own = u_ref.shape[0]

    @pl.when(step == 0)
    def _():
        m_ref[...] = jnp.full_like(m_ref, -1e38)
        s_ref[...] = jnp.zeros_like(s_ref)
        t_ref[...] = jnp.zeros_like(t_ref)
        lab_ref[...] = to_lanes(lab_row_ref[...])

    for q in range(VT // CHUNK):
        cs = slice(q * CHUNK, (q + 1) * CHUNK)
        block = dot_nt(u_ref[...], emb_ref[cs, :]) + bias_ref[0, :, cs]
        logit_ref[0, :, cs] = block
        for r in range(n_own // ROWS):
            rs = slice(r * ROWS, (r + 1) * ROWS)
            cols = [block[rs, k * 128:(k + 1) * 128] for k in range(CHUNK // 128)]
            m_old = m_ref[rs, :]
            m_new = functools.reduce(jnp.maximum, cols, m_old)
            total = s_ref[rs, :] * jnp.exp(m_old - m_new)
            label = t_ref[rs, :]
            lab = lab_ref[rs, :]
            for k, col in enumerate(cols):
                total += jnp.exp(col - m_new)
                ids = col_ref[0, :, q * CHUNK + k * 128:q * CHUNK + (k + 1) * 128]
                label += jnp.where(ids == lab, col, 0.0)
            m_ref[rs, :] = m_new
            s_ref[rs, :] = total
            t_ref[rs, :] = label

    @pl.when(step == n_steps - 1)
    def _():
        m_new = m_ref[...]
        top = jnp.max(m_new, axis=1, keepdims=True)
        mass = jnp.sum(s_ref[...] * jnp.exp(m_new - top), axis=1, keepdims=True)
        target = jnp.sum(t_ref[...], axis=1, keepdims=True)
        lane = lax.broadcasted_iota(I32, m_new.shape, 1)
        stat_ref[...] = jnp.where(lane == 0, top, jnp.where(lane == 1, mass, target)).T[:8]


def du_kernel(n_steps, inv_n, logit_ref, emb_ref, col_ref, norm_row_ref, lab_row_ref, du_ref, db_ref, acc_ref, gb_ref, norm_ref, lab_ref):
    step = pl.program_id(0)
    n_own = acc_ref.shape[0]

    @pl.when(step == 0)
    def _():
        acc_ref[...] = jnp.zeros_like(acc_ref)
        norm_ref[...] = to_lanes(norm_row_ref[...])
        lab_ref[...] = to_lanes(lab_row_ref[...])

    wide = lambda x: jnp.concatenate([x] * (CHUNK // 128), axis=1)
    for q in range(VT // CHUNK):
        cs = slice(q * CHUNK, (q + 1) * CHUNK)
        db = jnp.zeros((1, CHUNK), F32)
        for r in range(n_own // ROWS):
            rs = slice(r * ROWS, (r + 1) * ROWS)
            prob = jnp.exp(logit_ref[0, rs, cs] - wide(norm_ref[rs, :]))
            hot = jnp.where(col_ref[0, :, cs] == wide(lab_ref[rs, :]), 1.0, 0.0)
            grad = (prob - hot) * inv_n
            db += jnp.sum(grad, axis=0, keepdims=True)
            gb_ref[rs, cs] = grad.astype(BF16)
        db_ref[0, :, cs] = db
        acc_ref[...] += jnp.dot(gb_ref[:, cs], emb_ref[cs, :], preferred_element_type=F32)

    @pl.when(step == n_steps - 1)
    def _():
        du_ref[...] = acc_ref[...].astype(BF16).astype(F32)


def place_kernel(n_pieces, n_tok, start_ref, *refs):
    pieces, toks, refs = refs[:n_pieces], refs[n_pieces:n_pieces + n_tok], refs[n_pieces + n_tok:]
    bufs, sems = refs[-n_pieces - 1:-1], refs[-1]
    outs = refs[:-n_pieces - 1]
    out_ref = outs[-3] if n_tok else outs[-1]
    copies = []
    for k in range(n_pieces):
        bufs[k][...] = pieces[k][...].astype(BF16)
        rows = pl.ds(pl.multiple_of(start_ref[k] * 16, 16), pieces[k].shape[0])
        copies.append(pltpu.make_async_copy(bufs[k], out_ref.at[rows, :], sems.at[k]))
        copies[-1].start()
    for k in range(n_tok):
        row = pl.ds(start_ref[n_pieces + k], 1)
        outs[-2][row, :] = toks[k][0:1, :]
        outs[-1][row, :] = toks[k][1:2, :]
    for copy in copies:
        copy.wait()


def place(pieces, starts, n_all, table=None, toks=()):
    n = len(pieces)
    width = pieces[0].shape[1]
    extra = [] if table is None else [table]
    shapes = [jax.ShapeDtypeStruct((n_all, width), BF16)]
    specs = [pl.BlockSpec(memory_space=pl.ANY)]
    if toks:
        shapes += [jax.ShapeDtypeStruct((len(toks), toks[0].shape[1]), F32)] * 2
        specs += [pl.BlockSpec(shapes[-1].shape, lambda i, s: (0, 0))] * 2
    whole = lambda p: pl.BlockSpec(p.shape, lambda i, s: (0, 0))
    return pl.pallas_call(
        functools.partial(place_kernel, n, len(toks)),
        grid_spec=pltpu.PrefetchScalarGridSpec(
            num_scalar_prefetch=1,
            grid=(1,),
            in_specs=[whole(p) for p in pieces] + [whole(t) for t in toks] + [pl.BlockSpec(memory_space=pl.ANY)] * len(extra),
            out_specs=specs,
            scratch_shapes=[pltpu.VMEM(p.shape, BF16) for p in pieces] + [pltpu.SemaphoreType.DMA((n,))],
        ),
        out_shape=shapes,
        input_output_aliases={n + len(toks) + 1: 0} if extra else {},
        compiler_params=pltpu.CompilerParams(vmem_limit_bytes=40 * MIB),
        cost_estimate=pl.CostEstimate(flops=5 * 10 ** 9, bytes_accessed=6 * sum(p.size for p in pieces), transcendentals=0),
    )(starts, *pieces, *toks, *extra)


def rows_kernel(cfg, start_ref, emb_ref, bias_ref, u_ref, norm_ref, lab_ref, *refs):
    n_steps, tile, inv_n, n_send, n_copy, aliased = cfg
    arrived, refs = refs[:n_copy], refs[n_copy + (1 if aliased else 0):]
    out_ref, sends, refs = refs[0], refs[1:1 + n_send], refs[1 + n_send:]
    acc_ref, out_sem, send_sem = refs[:3]
    stage, load_sem, store_sem = (refs[3:3 + n_copy], refs[3 + n_copy], refs[4 + n_copy]) if n_copy else ((), None, None)
    step = pl.program_id(0)
    slot = lax.rem(step, 2)
    n_tok = u_ref.shape[0]

    def load(k):
        return pltpu.make_async_copy(arrived[k], stage[k], load_sem.at[k])

    def store(k):
        rows = pl.ds(pl.multiple_of(start_ref[2 * n_steps + k] * 16, 16), arrived[k].shape[0])
        return pltpu.make_async_copy(stage[k], out_ref.at[rows, :], store_sem.at[k])

    @pl.when(step == 0)
    def _():
        for k in range(n_copy):
            load(k).start()

    @pl.when(step == 1)
    def _():
        for k in range(n_copy):
            load(k).wait()
            store(k).start()

    def out_copy(t, which):
        rows = pl.ds(pl.multiple_of(start_ref[t] * 16, 16), tile)
        return pltpu.make_async_copy(acc_ref.at[which], out_ref.at[rows, :], out_sem.at[which])

    def send_copy(t, which):
        rows = pl.ds(pl.multiple_of(t * tile, 16), tile) if n_send == 1 else pl.ds(0, tile)
        target = sends[0] if n_send == 1 else sends[t]
        return pltpu.make_async_copy(acc_ref.at[which], target.at[rows, :], send_sem.at[which])

    @pl.when(step >= 2)
    def _():
        out_copy(step - 2, slot).wait()
        pltpu.make_async_copy(acc_ref.at[slot], sends[0].at[pl.ds(0, tile), :], send_sem.at[slot]).wait()

    row_id = lax.broadcasted_iota(I32, (tile, 1), 0).astype(F32) + (start_ref[step] * 16).astype(F32)
    bias = jnp.concatenate([to_lanes(bias_ref[0])[:tile]] * (TOK_CHUNK // 128), axis=1)
    per = TOK_CHUNK // norm_ref.shape[1]
    for j in range(n_tok // TOK_CHUNK):
        s = slice(j * TOK_CHUNK, (j + 1) * TOK_CHUNK)
        norm = jnp.concatenate([norm_ref[i:i + 1, :] for i in range(j * per, (j + 1) * per)], axis=1)
        lab = jnp.concatenate([lab_ref[i:i + 1, :] for i in range(j * per, (j + 1) * per)], axis=1)
        logit = dot_nt(emb_ref[...], u_ref[s, :]) + bias
        prob = jnp.exp(logit - norm)
        grad = (prob - jnp.where(lab == row_id, 1.0, 0.0)) * inv_n
        part = jnp.dot(grad.astype(BF16), u_ref[s, :], preferred_element_type=F32)
        if j == 0:
            acc_ref[slot] = part
        else:
            acc_ref[slot] += part

    out_copy(step, slot).start()
    if n_send == 1:
        send_copy(step, slot).start()
    else:
        for t in range(n_send):
            @pl.when(step == t)
            def _():
                send_copy(t, t % 2).start()

    @pl.when(step == n_steps - 1)
    def _():
        for k in range(n_copy):
            store(k).wait()
        for t in range(max(0, n_steps - 2), n_steps):
            out_copy(t, t % 2).wait()
            pltpu.make_async_copy(acc_ref.at[t % 2], sends[0].at[pl.ds(0, tile), :], send_sem.at[t % 2]).wait()


def emb_rows(out, starts, blocks, emb, bias, u_all, norm, lab, inv_n, tile, n_steps, n_send, arrived, copy_starts):
    n_tok, width = u_all.shape
    n_rows = emb.shape[0]
    n_copy = len(arrived)
    aliased = out is not None
    cfg = (n_steps, tile, inv_n, n_send, n_copy, aliased)
    table = jnp.concatenate([starts, blocks] + list(copy_starts)).astype(I32)
    any_space = pl.BlockSpec(memory_space=pl.ANY)
    whole = lambda a: pl.BlockSpec(a.shape, lambda i, s: (0, 0))
    send_rows = n_steps * tile if n_send == 1 else tile
    scratch = [pltpu.VMEM((2, tile, width), F32), pltpu.SemaphoreType.DMA((2,)), pltpu.SemaphoreType.DMA((2,))]
    if n_copy:
        scratch += [pltpu.VMEM(a.shape, F32) for a in arrived] + [pltpu.SemaphoreType.DMA((n_copy,))] * 2
    return pl.pallas_call(
        functools.partial(rows_kernel, cfg),
        grid_spec=pltpu.PrefetchScalarGridSpec(
            num_scalar_prefetch=1,
            grid=(n_steps,),
            in_specs=[
                pl.BlockSpec((pl.Element(tile), pl.Element(width)), lambda i, s: (pl.multiple_of(s[i] * 16, 16), 0)),
                pl.BlockSpec((1, 1, bias.shape[2]), lambda i, s: (s[n_steps + i], 0, 0)),
                pl.BlockSpec(memory_space=pltpu.VMEM), whole(norm), whole(lab),
            ] + [any_space] * (n_copy + aliased),
            out_specs=[any_space] * (1 + n_send),
            scratch_shapes=scratch,
        ),
        out_shape=[jax.ShapeDtypeStruct((n_rows, width), F32)] + [jax.ShapeDtypeStruct((send_rows, width), F32)] * n_send,
        input_output_aliases={6 + n_copy: 0} if aliased else {},
        compiler_params=pltpu.CompilerParams(vmem_limit_bytes=VMEM_ROWS * MIB),
        cost_estimate=pl.CostEstimate(
            flops=n_steps * tile * n_tok * width // COST_SCALE, bytes_accessed=n_steps * tile * width * 10, transcendentals=n_steps * tile * n_tok
        ),
    )(table, emb, bias, u_all, norm, lab, *arrived, *([out] if aliased else []))


def copy_kernel(n, start_ref, *refs):
    arrived, out_ref, stage, load_sem, store_sem = refs[:n], refs[n + 1], refs[n + 2:-2], refs[-2], refs[-1]
    loads = [pltpu.make_async_copy(arrived[k], stage[k], load_sem.at[k]) for k in range(n)]
    for load in loads:
        load.start()
    stores = []
    for k in range(n):
        loads[k].wait()
        rows = pl.ds(pl.multiple_of(start_ref[k] * 16, 16), arrived[k].shape[0])
        stores.append(pltpu.make_async_copy(stage[k], out_ref.at[rows, :], store_sem.at[k]))
        stores[-1].start()
    for store in stores:
        store.wait()


def copy_rows(out, arrived, starts):
    n = len(arrived)
    return pl.pallas_call(
        functools.partial(copy_kernel, n),
        grid_spec=pltpu.PrefetchScalarGridSpec(
            num_scalar_prefetch=1,
            grid=(1,),
            in_specs=[pl.BlockSpec(memory_space=pl.ANY)] * (n + 1),
            out_specs=pl.BlockSpec(memory_space=pl.ANY),
            scratch_shapes=[pltpu.VMEM(a.shape, F32) for a in arrived] + [pltpu.SemaphoreType.DMA((n,))] * 2,
        ),
        out_shape=jax.ShapeDtypeStruct(out.shape, F32),
        input_output_aliases={n + 1: 0},
        compiler_params=pltpu.CompilerParams(vmem_limit_bytes=48 * MIB),
        cost_estimate=pl.CostEstimate(flops=5 * 10 ** 9, bytes_accessed=8 * sum(a.size for a in arrived), transcendentals=0),
    )(jnp.concatenate(starts).astype(I32), *arrived, out)


def swap(x, mask, axis="dp"):
    n = 8 if axis == "dp" else 2
    return lax.ppermute(x, axis, [(i, i ^ mask) for i in range(n)])


def solution(mesh):
    n_groups = mesh.shape["dp"]

    def local_step(hidden, mask_pos, labels, w_trans, b_trans, ln_gain, ln_bias, emb_table, b_vocab):
        n_rows, seq_len, width = hidden.shape
        n_masks = mask_pos.shape[1]
        shard_rows = emb_table.shape[0]
        inv_n = 1.0 / (n_rows * n_masks * n_groups)
        n_own = n_rows * SLOTS
        n_all = n_own * n_groups
        me, plane = lax.axis_index("dp"), lax.axis_index("vp")
        core, par = me & 1, ((me >> 1) ^ (me >> 2)) & 1
        row_start = plane * shard_rows
        valid = (jnp.arange(n_own) % SLOTS < n_masks)[None]

        pos = jnp.pad(mask_pos, ((0, 0), (0, SLOTS - n_masks)), constant_values=-1)
        pos_onehot = (pos[:, :, None] == jnp.arange(seq_len)[None, None, :]).astype(BF16)
        masked_h = jnp.einsum("clt,cte->cle", pos_onehot, hidden, preferred_element_type=F32).astype(BF16).reshape(n_own, width)
        pre_act = jnp.dot(masked_h, w_trans, preferred_element_type=F32) + b_trans
        u_norm, head_vjp = jax.vjp(head_norm, pre_act, ln_gain, ln_bias)
        u_own = u_norm.astype(BF16)

        half = n_own // 2
        u_f = u_own.astype(F32)
        u_sib, u_x, u_y = swap(u_f, 1), swap(u_f, 2), swap(u_f, 4)
        u_d0, u_d1 = swap(u_x[:half], 4), swap(u_y[half:], 2)
        u_xs, u_ys = swap(u_x, 1), swap(u_y, 1)
        blk = n_own // 16
        at = lambda m, o=0: ((me ^ m) * blk + o)[None]

        n_steps = -(-shard_rows // VT)
        last = shard_rows - VT
        dup = n_steps * VT - shard_rows
        b_pad = jnp.concatenate([b_vocab[:shard_rows - (VT - dup)], jnp.full((dup,), -OFF, F32), b_vocab[shard_rows - (VT - dup):]]).reshape(n_steps, 1, VT)
        ids = jnp.arange(shard_rows, dtype=F32)
        cols = jnp.concatenate([ids[:shard_rows - (VT - dup)], jnp.full((dup,), -7.0, F32), ids[shard_rows - (VT - dup):]]).reshape(n_steps, 1, VT)
        lab_pad = jnp.pad(labels, ((0, 0), (0, SLOTS - n_masks)), constant_values=-1000000).reshape(n_own)
        lab_rel = (lab_pad - row_start).astype(F32)
        lab_row = lab_rel[None]
        row_block = pl.BlockSpec((1, n_own), lambda i: (0, 0))
        own_block = pl.BlockSpec((n_own, width), lambda i: (0, 0))
        emb_block = pl.BlockSpec((pl.Element(VT), pl.Element(width)), lambda i: (pl.multiple_of(jnp.minimum(i * (VT // 16), last // 16) * 16, 16), 0))
        col_block = pl.BlockSpec((1, 1, VT), lambda i: (i, 0, 0))
        logit_block = pl.BlockSpec((1, n_own, VT), lambda i: (i, 0, 0))
        lane_block = pl.BlockSpec((n_own, 128), lambda i: (0, 0))
        flops = 2 * n_own * shard_rows * width
        cost = pl.CostEstimate(flops=flops, bytes_accessed=4 * n_own * shard_rows, transcendentals=n_own * shard_rows)
        params = pltpu.CompilerParams(vmem_limit_bytes=60 * MIB)
        logits, stats = pl.pallas_call(
            functools.partial(stats_kernel, n_steps),
            grid=(n_steps,),
            in_specs=[own_block, emb_block, col_block, col_block, row_block],
            out_specs=[logit_block, pl.BlockSpec((8, n_own), lambda i: (0, 0))],
            out_shape=[jax.ShapeDtypeStruct((n_steps, n_own, VT), F32), jax.ShapeDtypeStruct((8, n_own), F32)],
            scratch_shapes=[pltpu.VMEM((n_own, 128), F32)] * 4,
            compiler_params=params,
            cost_estimate=cost,
        )(u_own, emb_table, b_pad, cols, lab_row)
        other = swap(stats, 1, "vp")
        lo, hi = jnp.where(plane == 0, stats, other), jnp.where(plane == 0, other, stats)
        top = jnp.maximum(lo[0:1], hi[0:1])
        log_norm = top + jnp.log(lo[1:2] * jnp.exp(lo[0:1] - top) + hi[1:2] * jnp.exp(hi[0:1] - top))
        loss_part = jnp.sum(jnp.where(valid, log_norm - (lo[2:3] + hi[2:3]), 0.0)) * inv_n
        norm_own = jnp.where(valid, log_norm, OFF)

        tok = jnp.concatenate([norm_own, lab_row])
        toks = [tok] + [swap(tok, m) for m in range(1, n_groups)]
        own_du = pl.pallas_call(
            functools.partial(du_kernel, n_steps, inv_n),
            grid=(n_steps,),
            in_specs=[logit_block, emb_block, col_block, row_block, row_block],
            out_specs=[own_block, col_block],
            out_shape=[jax.ShapeDtypeStruct((n_own, width), F32), jax.ShapeDtypeStruct((n_steps, 1, VT), F32)],
            scratch_shapes=[pltpu.VMEM((n_own, width), F32), pltpu.VMEM((n_own, VT), BF16)] + [pltpu.VMEM((n_own, 128), F32)] * 2,
            compiler_params=params,
            cost_estimate=cost,
        )
        du_part, db_tiles = own_du(logits, emb_table, cols, norm_own, lab_row)
        du_other = swap(du_part, 1, "vp")

        (u_d0, u_d1), du_part, db_tiles = lax.optimization_barrier(((u_d0, u_d1), du_part, db_tiles))
        u_ds0, u_ds1 = swap(u_d0, 1), swap(u_d1, 1)
        u_all, = place([u_f, u_sib, u_x, u_y, u_xs, u_ys], jnp.concatenate([at(0), at(1), at(2), at(4), at(3), at(5)]).astype(I32), n_all)
        ranks = [(me ^ m)[None] for m in range(n_groups)]
        (u_all, *toks), du_part, db_tiles = lax.optimization_barrier(((u_all, *toks), du_part, db_tiles))
        u_all, norm_all, lab_all = place(
            [u_d0, u_d1, u_ds0, u_ds1], jnp.concatenate([at(6), at(6, blk // 2), at(7), at(7, blk // 2)] + ranks).astype(I32), n_all, u_all, toks)

        nx, nl = SHARE_CHUNKS * SHARE_TILE // 16, LOCAL_TILES * LOCAL_TILE // 16
        assert 16 * (8 * nx + 2 * nl) == shard_rows
        st = SHARE_TILE // 16
        x_at = lambda p, c, k: ((2 * p + c) * nx + k * st)[None]
        y_at = lambda p, c, k: (4 * nx + (2 * p + c) * nx + k * st)[None]
        pad128 = lambda x: jnp.pad(x, ((0, 0), (0, -x.shape[1] % 128)))[:, None, :]
        bias_share = pad128(b_vocab[:16 * 8 * nx].reshape(-1, SHARE_TILE))
        bias_local = pad128(b_vocab[16 * 8 * nx:].reshape(-1, LOCAL_TILE))
        lt = LOCAL_TILE // 16
        out = None

        def rows_call(out, starts, blocks, bias, tile, n_steps, n_send, take):
            return emb_rows(out, starts, blocks, emb_table, bias, u_all, norm_all, lab_all, inv_n, tile, n_steps, n_send,
                            [a for a, _ in take], [s[:1] for _, s in take])

        per = LOCAL_TILES // LOCAL_CALLS
        l_at = lambda c, k: jnp.stack([8 * nx + c * nl + (k * per + i) * lt for i in range(per)])

        def shared_rows(out, k, take):
            starts = jnp.concatenate([x_at(par, core, k), y_at(par, core, k)])
            return rows_call(out, starts, starts // st, bias_share, SHARE_TILE, 2, 2, take)

        def local_rows(out, k, take):
            starts = l_at(core, k)
            out, rows = rows_call(out, starts, (starts - 8 * nx) // lt, bias_local, LOCAL_TILE, per, 1, take)
            return out, (swap(rows, 1), l_at(1 - core, k))

        def near(k, sx, sy):
            return [(swap(sx, 1), x_at(par, 1 - core, k)), (swap(sy, 1), y_at(par, 1 - core, k))]

        def far(k, rx, ry):
            return [(rx, x_at(1 - par, core, k)), (ry, y_at(1 - par, core, k)),
                    (swap(rx, 1), x_at(1 - par, 1 - core, k)),
                    (swap(ry, 1), y_at(1 - par, 1 - core, k))]

        after = lax.optimization_barrier
        out, sx0, sy0 = shared_rows(out, 0, [])
        rx0, ry0 = swap(sx0, 2), swap(sy0, 4)
        near0 = near(0, sx0, sy0)
        out, sx1, sy1 = shared_rows(out, 1, [])
        rx1, ry1 = swap(sx1, 2), swap(sy1, 4)
        near1 = near(1, sx1, sy1)

        du_other, out = after((du_other, out))
        d_pre, d_ln_gain, d_ln_bias = head_vjp(du_part + du_other)
        d_pre_bf = d_pre.astype(BF16)
        d_w_part = lax.dot_general(masked_h, d_pre_bf, (((0,), (0,)), ((), ())), preferred_element_type=F32)
        hw = width // 2
        db_flat = db_tiles.reshape(n_steps * VT)
        db_own = jnp.concatenate([db_flat[:shard_rows - (VT - dup)], db_flat[shard_rows - (VT - dup) + dup:]])
        db_rows = -(-shard_rows // width)
        small = jnp.concatenate([jnp.sum(d_pre, axis=0), d_ln_gain, d_ln_bias, jnp.pad(loss_part[None], (0, width - 1)),
                                 jnp.pad(db_own, (0, db_rows * width - shard_rows))]).reshape(4 + db_rows, width)
        total = hw + 4 + db_rows
        padded = -(-total // 64) * 64
        part = padded // n_groups
        mine = jnp.concatenate([lax.dynamic_slice(d_w_part, (plane * hw, 0), (hw, width)), small, jnp.zeros((padded - total, width), F32)])
        mine = mine.reshape(n_groups, part, width)
        mine, out, d_pre_bf = after((mine, out, d_pre_bf))
        piece = lambda a, m: lax.dynamic_index_in_dim(a, me ^ m, 0, keepdims=False)
        got = [swap(piece(mine, m), m) for m in range(1, n_groups)]

        out, sx2, sy2 = shared_rows(out, 2, [])
        near2 = near(2, sx2, sy2)
        out, sx3, sy3 = shared_rows(out, 3, [])
        near3 = near(3, sx3, sy3)
        out, rx0, ry0, sx2, sy2 = after((out, rx0, ry0, sx2, sy2))
        rx2, ry2 = swap(sx2, 2), swap(sy2, 4)
        far0 = far(0, rx0, ry0)
        d_masked = dot_nt(d_pre_bf, w_trans).astype(BF16).reshape(n_rows, SLOTS, width)
        out, got0 = local_rows(out, 0, near0 + near1 + near2)
        out, got, d_masked = after((out, got, d_masked))
        parts = [piece(mine, 0)] + got
        order = [parts[m] for m in range(n_groups)]
        level = lambda v: [v[i] + v[i + 1] for i in range(0, len(v), 2)]
        acc = level(level(level(order)))[0]
        acc, out = after((acc, out))
        sums = [acc] + [swap(acc, m) for m in range(1, n_groups)]
        out, got1 = local_rows(out, 1, near3 + far0)
        out, rx1, ry1, sx3, sy3 = after((out, rx1, ry1, sx3, sy3))
        rx3, ry3 = swap(sx3, 2), swap(sy3, 4)
        far1 = far(1, rx1, ry1)
        (sums, out) = after((sums, out))
        grads = jnp.zeros((n_groups, part, width), F32)
        for m in range(n_groups):
            grads = lax.dynamic_update_index_in_dim(grads, sums[m], me ^ m, 0)
        grads = grads.reshape(padded, width)
        w_other = swap(grads[:hw], 1, "vp")
        out, got2 = local_rows(out, 2, far1[:2] + [got0])
        d_hidden = jnp.einsum("clt,cle->cte", pos_onehot, d_masked, preferred_element_type=F32).astype(BF16)
        out, rx2, ry2, d_hidden = after((out, rx2, ry2, d_hidden))
        far2 = far(2, rx2, ry2)
        put = lambda out, items: copy_rows(out, [a for a, _ in items], [s[:1] for _, s in items])
        out = put(out, far1[2:] + [got1, got2] + far2)
        out, rx3, ry3 = after((out, rx3, ry3))
        far3 = far(3, rx3, ry3)
        d_emb_table = put(out, far3)
        w_half = grads[:hw]
        d_w_trans = jnp.where(plane == 0, jnp.concatenate([w_half, w_other]), jnp.concatenate([w_other, w_half]))
        vec = grads[hw:hw + 3]
        mlm_loss = grads[hw + 3, 0]
        d_b_vocab = grads[hw + 4:total].reshape(db_rows * width)[:shard_rows]
        return mlm_loss, d_hidden, d_w_trans, vec[0], vec[1], vec[2], d_emb_table, d_b_vocab

    in_specs = (P("dp", None, None), P("dp", None), P("dp", None), P(None, None), P(None), P(None), P(None), P("vp", None), P("vp"))
    out_specs = (P(), P("dp", None, None), P(None, None), P(None), P(None), P(None), P("vp", None), P("vp"))

    return jax.shard_map(local_step, mesh=mesh, in_specs=in_specs, out_specs=out_specs, check_vma=False)
```

time: 1190 us -> 577 us (0.48)
  waiting for transfers between devices: 858 us -> 132 us
  Pallas kernels: 0 us -> 304 us
  matrix products: 158 us -> 27.8 us
  other arithmetic: 68.8 us -> 17.9 us
  starting transfers between devices: 0.3 us -> 49.9 us
  blocking collectives: 30.4 us -> 0 us
  local copies, waits for them, and re-layouts: 57.6 us -> 32.5 us
  between operations: 16.1 us -> 2.59 us
    psum x2 -> x0, waiting for transfers between devices: 858 us -> none  [the longest x1 858 us: local_step(): lax.psum(jnp.einsum('cle,clf->ef', masked_h, d_pre_bf, preferred_element_...]
    pallas_call x0 -> x13, Pallas kernels: none -> 304 us  [the longest x7 185 us: emb_rows(): pl.pallas_call(functools.partial(rows_kernel, cfg), grid_spec=pltpu.Prefe...]
    ppermute x0 -> x60, waiting for transfers between devices: none -> 132 us  [swap(): return lax.ppermute(x, axis, [(i, i ^ mask) for i in range(n)])]
    dot_general x7 -> x5, matrix products: 158 us -> 27.8 us  [the longest x1 13.4 us: local_step(): pre_act = jnp.dot(masked_h, w_trans, preferred_element_type=F32) + b_trans]
    reduce_sum x7 -> x2, other arithmetic: 65.2 us -> 2.41 us  [the longest x1 1.75 us: local_step(): jnp.sum(d_pre, axis=0)]
    ppermute x0 -> x60, starting transfers between devices: none -> 49.9 us  [swap(): return lax.ppermute(x, axis, [(i, i ^ mask) for i in range(n)])]
    unnamed x41 -> x94, local copies, waits for them, and re-layouts: 57 us -> 12.7 us
    psum x1 -> x0, blocking collectives: 24.5 us -> none  [local_step(): mlm_loss = lax.psum(jnp.sum(log_norm - target), 'dp') / n_tokens]
  transfers between devices with their start and end apart: 2 -> 60, of which waited for: 1 -> 19; matrix products, arithmetic and copies ran while one was open for 8% -> 6% of each run, Pallas kernels for 0% -> 47%
where the time goes in v1:
time: 577 us; the launch traced here: 567 us
  Pallas kernels  304 us (53%)
  waiting for transfers between devices  132 us (23%)
  starting transfers between devices  49.9 us (9%)
  local copies, waits for them, and re-layouts  32.5 us (6%)
  matrix products  27.8 us (5%)
  other arithmetic  17.9 us (3%)
    pallas_call x7, Pallas kernels, emb_rows(): pl.pallas_call(functools.partial(rows_kernel, cfg), grid_spec=pltpu.Prefe...  185 us
    ppermute x60, waiting for transfers between devices, swap(): return lax.ppermute(x, axis, [(i, i ^ mask) for i in range(n)])  132 us
    ppermute x60, starting transfers between devices, swap(): return lax.ppermute(x, axis, [(i, i ^ mask) for i in range(n)])  49.9 us
    pallas_call x1, Pallas kernels, local_step(): pl.pallas_call(functools.partial(stats_kernel, n_steps), grid=(n_steps,),...  46.9 us
    pallas_call x1, Pallas kernels, local_step(): du_part, db_tiles = own_du(logits, emb_table, cols, norm_own, lab_row)  42.9 us
    pallas_call x2, Pallas kernels, copy_rows(): pl.pallas_call(functools.partial(copy_kernel, n), grid_spec=pltpu.Prefetc...  17.7 us
    dot_general x1, matrix products, local_step(): pre_act = jnp.dot(masked_h, w_trans, preferred_element_type=F32) + b_trans  13.4 us
    unnamed x94, local copies, waits for them, and re-layouts  12.7 us
  transfers between devices with their start and end apart: 60, of which 19 were waited for; matrix products, arithmetic and copies ran while one was open for 6% of the time, Pallas kernels for 47%

profile of v1, /device:TPU:0, one launch (start us, length us, event | category | flops | bytes accessed | tf_op | source)
XLA Modules:
  0.0 566.6 jit_solution(17431894146921489345)
XLA Ops:
  1.4 4.0 convolution_convert_fusion.2
  5.5 13.4 %fusion.20 = (f32[640]{0:T(1024)S(1)}, f32[640,768]{1,0:T(8,128)S(1)}, f32[640,768]{1,0:T(8,128)}, f32[640,768]{1,0:T(8,128)}) fusion(f32[768]{0:T(1024)S(1)} %copy-done.43, bf16[640,768]{1,0:T(8,128)(2,1)S(1)} %bitcast.116, bf16[768,768]{1,0:T(8,128)(2,1)S(1)} %copy-done), kind=kOutput, calls=%fused_computation.106 | convolution fusion | flops 787414400 | bytes 8066560 | tf_op jit(solution)/shard_map/dot_general | solution.py:325
  21.1 3.2 collective-permute-start.1
  29.7 46.9 %shard_map.153 = (f32[11,640,2304]{2,1,0:T(8,128)}, f32[8,640]{1,0:T(8,128)}) custom-call(bf16[640,768]{1,0:T(8,128)(2,1)} %get-tuple-element.185.u_ref, bf16[25152,768]{1,0:T(8,128)(2,1)} %emb_ref.17, f32[11,1,2304]{2,1,0:T(1,128)} %reshape.127.bias_ref, f32[11,1,2304]{2,1,0:T(1,128)} %reshape.128.col_ref, f32[1,640]{1,0:T(1,128)} %convert_element_type.44.lab_row_ref), custom_call_target="tpu_custom_call" | custom-call | flops 24725422080 | bytes 64389120 | tf_op jit(solution)/shard_map/pallas_call | solution.py:355
  78.3 2.4 collective-permute-done.5
  82.3 2.8 collective-permute-start.12
  85.3 2.2 slice.107
  87.8 2.3 slice.108
  92.6 42.9 %shard_map.154 = (f32[640,768]{1,0:T(8,128)}, f32[11,1,2304]{2,1,0:T(1,128)}) custom-call(f32[11,640,2304]{2,1,0:T(8,128)} %get-tuple-element.91.logit_ref, bf16[25152,768]{1,0:T(8,128)(2,1)} %emb_ref.17, f32[11,1,2304]{2,1,0:T(1,128)} %reshape.128.col_ref, f32[1,640]{1,0:T(1,128)} %copy-done.41, f32[1,640]{1,0:T(1,128)} %convert_element_type.44.lab_row_ref), custom_call_target="tpu_custom_call" | custom-call | flops 24725422080 | bytes 64389120 | tf_op jit(solution)/shard_map/pallas_call | solution.py:384
  135.5 1.6 collective-permute-start.15
  139.1 1.7 collective-permute-done.7.refs_6_
  143.9 7.1 %shard_map.152.refs_12_ = bf16[5120,768]{1,0:T(8,128)(2,1)} custom-call(s32[6]{0:T(128)S(1)} %concatenate.76.start_ref, f32[640,768]{1,0:T(8,128)S(1)} %get-tuple-element.184.refs_0_, f32[640,768]{1,0:T(8,128)} %collective-permute-done.refs_1_, f32[640,768]{1,0:T(8,128)} %collective-permute-done.1.refs_2_, f32[640,768]{1,0:T(8,128)} %collective-permute-done.2.refs_3_, ...), custom_call_target="tpu_custom_call" | custom-call | flops 5000000000 | bytes 17694720 | tf_op jit(solution)/shard_map/pallas_call | solution.py:142
  151.1 3.2 copy-done.2
  154.3 4.1 shard_map.155
  158.5 3.1 copy-done.3
  161.6 23.6 %shard_map.156 = (f32[25152,768]{1,0:T(8,128)}, f32[528,768]{1,0:T(8,128)}, f32[528,768]{1,0:T(8,128)}) custom-call(s32[4]{0:T(128)S(1)} %pad_add_fusion.3.start_ref, bf16[25152,768]{1,0:T(8,128)(2,1)} %emb_ref.17, f32[32,1,640]{2,1,0:T(1,128)S(1)} %broadcast_in_dim.230.bias_ref, bf16[5120,768]{1,0:T(8,128)(2,1)} %copy-done.3, ...), custom_call_target="tpu_custom_call" | custom-call | flops 1038090240 | bytes 8110080 | tf_op jit(solution)/shard_map/pallas_call | solution.py:247
  185.3 24.2 %shard_map.157 = (f32[25152,768]{1,0:T(8,128)}, f32[528,768]{1,0:T(8,128)}, f32[528,768]{1,0:T(8,128)}) custom-call(s32[4]{0:T(128)S(1)} %pad_add_fusion.1.start_ref, bf16[25152,768]{1,0:T(8,128)(2,1)} %emb_ref.17, f32[32,1,640]{2,1,0:T(1,128)S(1)} %broadcast_in_dim.230.bias_ref, bf16[5120,768]{1,0:T(8,128)(2,1)} %copy-done.3, ...), custom_call_target="tpu_custom_call", output_to_operand_aliasing={{0}: (6, {})} | custom-call | flops 1038090240 | bytes 8110080 | tf_op jit(solution)/shard_map/pallas_call | solution.py:247
  209.5 2.1 fusion.17
  213.7 2.5 fusion.18
  216.3 2.5 fusion.22
  218.8 1.7 reduce_sum.77
  226.0 24.0 %shard_map.158 = (f32[25152,768]{1,0:T(8,128)}, f32[528,768]{1,0:T(8,128)S(1)}, f32[528,768]{1,0:T(8,128)}) custom-call(s32[4]{0:T(128)S(1)} %pad_add_fusion.5.start_ref, bf16[25152,768]{1,0:T(8,128)(2,1)} %emb_ref.17, f32[32,1,640]{2,1,0:T(1,128)S(1)} %broadcast_in_dim.230.bias_ref, bf16[5120,768]{1,0:T(8,128)(2,1)} %copy-done.3, ...), custom_call_target="tpu_custom_call", output_to_operand_aliasing={{0}: (6, {})} | custom-call | flops 1038090240 | bytes 8110080 | tf_op jit(solution)/shard_map/pallas_call | solution.py:247
  250.6 11.2 %collective-permute-done.24.refs_2_ = f32[528,768]{1,0:T(8,128)S(1)} collective-permute-done((f32[528,768]{1,0:T(8,128)}, f32[528,768]{1,0:T(8,128)S(1)}, u32[]{:S(2)}, u32[]{:S(2)}) %collective-permute-start.24) | collective-permute-done | bytes 1622048 | tf_op jit(solution)/shard_map/ppermute | solution.py:304
  264.2 23.6 %shard_map.159 = (f32[25152,768]{1,0:T(8,128)}, f32[528,768]{1,0:T(8,128)}, f32[528,768]{1,0:T(8,128)}) custom-call(s32[4]{0:T(128)S(1)} %pad_add_fusion.7.start_ref, bf16[25152,768]{1,0:T(8,128)(2,1)} %emb_ref.17, f32[32,1,640]{2,1,0:T(1,128)S(1)} %broadcast_in_dim.230.bias_ref, bf16[5120,768]{1,0:T(8,128)(2,1)} %copy-done.3, ...), custom_call_target="tpu_custom_call", output_to_operand_aliasing={{0}: (6, {})} | custom-call | flops 1038090240 | bytes 8110080 | tf_op jit(solution)/shard_map/pallas_call | solution.py:247
  287.9 30.1 %shard_map.160 = (f32[25152,768]{1,0:T(8,128)}, f32[1376,768]{1,0:T(8,128)}) custom-call(s32[10]{0:T(128)S(1)} %concatenate.88.start_ref, bf16[25152,768]{1,0:T(8,128)(2,1)} %emb_ref.17, f32[12,1,768]{2,1,0:T(1,128)S(1)} %broadcast_in_dim.256.bias_ref, bf16[5120,768]{1,0:T(8,128)(2,1)} %copy-done.3, ...), custom_call_target="tpu_custom_call", output_to_operand_aliasing={{0}: (12, {})} | custom-call | flops 1352663040 | bytes 10567680 | tf_op jit(solution)/shard_map/pallas_call | solution.py:247
  322.0 8.3 %collective-permute-done.26 = f32[56,768]{1,0:T(8,128)S(1)} collective-permute-done((f32[56,768]{1,0:T(8,128)S(1)}, f32[56,768]{1,0:T(8,128)S(1)}, u32[]{:S(2)}, u32[]{:S(2)}) %collective-permute-start.26) | collective-permute-done | bytes 172064 | tf_op jit(solution)/shard_map/ppermute | solution.py:304
  333.1 3.6 collective-permute-done.28
  339.7 6.7 %collective-permute-done.30 = f32[56,768]{1,0:T(8,128)S(1)} collective-permute-done((f32[56,768]{1,0:T(8,128)S(1)}, f32[56,768]{1,0:T(8,128)S(1)}, u32[]{:S(2)}, u32[]{:S(2)}) %collective-permute-start.30) | collective-permute-done | bytes 172064 | tf_op jit(solution)/shard_map/ppermute | solution.py:304
  346.4 2.5 collective-permute-start.32
  349.5 4.2 collective-permute-done.32
  355.8 3.2 convolution_convert_fusion.1
  360.1 28.8 %collective-permute-done.44.refs_0_ = f32[528,768]{1,0:T(8,128)} collective-permute-done((f32[528,768]{1,0:T(8,128)}, f32[528,768]{1,0:T(8,128)}, u32[]{:S(2)}, u32[]{:S(2)}) %collective-permute-start.44) | collective-permute-done | bytes 1622048 | tf_op jit(solution)/shard_map/ppermute | solution.py:304
  388.9 3.2 collective-permute-done.45.refs_1_
  393.5 5.9 %collective-permute-done.34 = f32[56,768]{1,0:T(8,128)S(1)} collective-permute-done((f32[56,768]{1,0:T(8,128)S(1)}, f32[56,768]{1,0:T(8,128)S(1)}, u32[]{:S(2)}, u32[]{:S(2)}) %collective-permute-start.34) | collective-permute-done | bytes 172064 | tf_op jit(solution)/shard_map/ppermute | solution.py:304
  401.0 1.9 collective-permute-start.37
  403.0 2.4 collective-permute-done.36
  405.4 2.1 collective-permute-start.38
  407.5 3.5 collective-permute-done.37
  411.0 2.9 collective-permute-start.39
  415.4 29.9 %shard_map.161 = (f32[25152,768]{1,0:T(8,128)}, f32[1376,768]{1,0:T(8,128)}) custom-call(s32[10]{0:T(128)S(1)} %concatenate.93.start_ref, bf16[25152,768]{1,0:T(8,128)(2,1)} %emb_ref.17, f32[12,1,768]{2,1,0:T(1,128)S(1)} %broadcast_in_dim.256.bias_ref, bf16[5120,768]{1,0:T(8,128)(2,1)} %copy-done.3, ...), custom_call_target="tpu_custom_call", output_to_operand_aliasing={{0}: (12, {})} | custom-call | flops 1352663040 | bytes 10567680 | tf_op jit(solution)/shard_map/pallas_call | solution.py:247
  445.4 29.9 %shard_map.162 = (f32[25152,768]{1,0:T(8,128)}, f32[1376,768]{1,0:T(8,128)}) custom-call(s32[7]{0:T(128)S(1)} %concatenate.94.start_ref, bf16[25152,768]{1,0:T(8,128)(2,1)} %emb_ref.17, f32[12,1,768]{2,1,0:T(1,128)S(1)} %broadcast_in_dim.256.bias_ref, bf16[5120,768]{1,0:T(8,128)(2,1)} %copy-done.3, ...), custom_call_target="tpu_custom_call", output_to_operand_aliasing={{0}: (9, {})} | custom-call | flops 1352663040 | bytes 10567680 | tf_op jit(solution)/shard_map/pallas_call | solution.py:247
  475.9 4.6 convolution_convert_fusion
  481.1 4.1 collective-permute-done.50.refs_0_
  494.5 12.7 %shard_map.163.refs_4_ = f32[25152,768]{1,0:T(8,128)} custom-call(s32[8]{0:T(128)S(1)} %concatenate.98.start_ref, f32[528,768]{1,0:T(8,128)S(1)} %copy-done.5, f32[528,768]{1,0:T(8,128)S(1)} %copy-done.7, f32[1376,768]{1,0:T(8,128)} %collective-permute-done.52.refs_2_, f32[1376,768]{1,0:T(8,128)} %collective-permute-done.53.refs_3_, ...), custom_call_target="tpu_custom_call", output_to_operand_aliasing={{}: (9, {})} | custom-call | flops 5000000000 | bytes 36372480 | tf_op jit(solution)/shard_map/pallas_call | solution.py:286
  507.2 19.4 %collective-permute-done.56.refs_0_ = f32[528,768]{1,0:T(8,128)S(1)} collective-permute-done((f32[528,768]{1,0:T(8,128)}, f32[528,768]{1,0:T(8,128)S(1)}, u32[]{:S(2)}, u32[]{:S(2)}) %collective-permute-start.56) | collective-permute-done | bytes 1622048 | tf_op jit(solution)/shard_map/ppermute | solution.py:304
  534.4 23.4 %collective-permute-done.49 = f32[384,768]{1,0:T(8,128)} collective-permute-done((f32[384,768]{1,0:T(8,128)S(1)}, f32[384,768]{1,0:T(8,128)}, u32[]{:S(2)}, u32[]{:S(2)}) %collective-permute-start.49) | collective-permute-done | bytes 1179680 | tf_op jit(solution)/shard_map/ppermute | solution.py:304
  557.8 3.4 maximum_select_fusion
  561.1 5.0 shard_map.164
  (268 shorter events, 65.7 us)
Async XLA Ops:
  21.1 64.0 %collective-permute-start.1 = (f32[640,768]{1,0:T(8,128)S(1)}, f32[640,768]{1,0:T(8,128)}, u32[]{:S(2)}, u32[]{:S(2)}) collective-permute-start(f32[640,768]{1,0:T(8,128)S(1)} %get-tuple-element.184.refs_0_), channel_id=1, source_target_pairs={{0,2},{1,3},{2,0},{3,1},{4,6},{5,7},{6,4},{7,5},{8,10},{9,11},{10,... | collective-permute-start | bytes 5898248 | tf_op jit(solution)/shard_map/ppermute | solution.py:304
  24.3 63.2 %collective-permute-start.2 = (f32[640,768]{1,0:T(8,128)S(1)}, f32[640,768]{1,0:T(8,128)}, u32[]{:S(2)}, u32[]{:S(2)}) collective-permute-start(f32[640,768]{1,0:T(8,128)S(1)} %get-tuple-element.184.refs_0_), channel_id=1, source_target_pairs={{0,4},{1,5},{2,6},{3,7},{4,0},{5,1},{6,2},{7,3},{8,12},{9,13},{10,... | collective-permute-start | bytes 5898248 | tf_op jit(solution)/shard_map/ppermute | solution.py:304
  82.1 7.9 %collective-permute-start.10 = (f32[2,640]{1,0:T(2,128)S(1)}, f32[2,640]{1,0:T(2,128)S(1)}, u32[]{:S(2)}, u32[]{:S(2)}) collective-permute-start(f32[2,640]{1,0:T(2,128)S(1)} %pad_maximum_fusion.refs_4_), channel_id=1, source_target_pairs={{0,5},{1,4},{2,7},{3,6},{4,1},{5,0},{6,3},{7,2},{8,13},{9,12},{10,... | collective-permute-start | bytes 15368 | tf_op jit(solution)/shard_map/ppermute | solution.py:304
  82.2 9.4 %collective-permute-start.11 = (f32[2,640]{1,0:T(2,128)S(1)}, f32[2,640]{1,0:T(2,128)S(1)}, u32[]{:S(2)}, u32[]{:S(2)}) collective-permute-start(f32[2,640]{1,0:T(2,128)S(1)} %pad_maximum_fusion.refs_4_), channel_id=1, source_target_pairs={{0,6},{1,7},{2,4},{3,5},{4,2},{5,3},{6,0},{7,1},{8,14},{9,15},{10,... | collective-permute-start | bytes 15368 | tf_op jit(solution)/shard_map/ppermute | solution.py:304
  82.3 9.8 %collective-permute-start.12 = (f32[2,640]{1,0:T(2,128)S(1)}, f32[2,640]{1,0:T(2,128)S(1)}, u32[]{:S(2)}, u32[]{:S(2)}) collective-permute-start(f32[2,640]{1,0:T(2,128)S(1)} %pad_maximum_fusion.refs_4_), channel_id=1, source_target_pairs={{0,7},{1,6},{2,5},{3,4},{4,3},{5,2},{6,1},{7,0},{8,15},{9,14},{10,... | collective-permute-start | bytes 15368 | tf_op jit(solution)/shard_map/ppermute | solution.py:304
  87.5 53.3 %collective-permute-start = (f32[640,768]{1,0:T(8,128)S(1)}, f32[640,768]{1,0:T(8,128)}, u32[]{:S(2)}, u32[]{:S(2)}) collective-permute-start(f32[640,768]{1,0:T(8,128)S(1)} %get-tuple-element.184.refs_0_), channel_id=1, source_target_pairs={{0,1},{1,0},{2,3},{3,2},{4,5},{5,4},{6,7},{7,6},{8,9},{9,8},{10,11... | collective-permute-start | bytes 5898248 | tf_op jit(solution)/shard_map/ppermute | solution.py:304
  90.0 45.5 %collective-permute-start.13 = (f32[320,768]{1,0:T(8,128)}, f32[320,768]{1,0:T(8,128)}, u32[]{:S(2)}, u32[]{:S(2)}) collective-permute-start(f32[320,768]{1,0:T(8,128)} %slice.107), channel_id=1, source_target_pairs={{0,4},{1,5},{2,6},{3,7},{4,0},{5,1},{6,2},{7,3},{8,12},{9,13},{10,... | collective-permute-start | bytes 2949128 | tf_op jit(solution)/shard_map/ppermute | solution.py:304
  91.5 45.6 %collective-permute-start.14 = (f32[320,768]{1,0:T(8,128)}, f32[320,768]{1,0:T(8,128)}, u32[]{:S(2)}, u32[]{:S(2)}) collective-permute-start(f32[320,768]{1,0:T(8,128)} %slice.108), channel_id=1, source_target_pairs={{0,2},{1,3},{2,0},{3,1},{4,6},{5,7},{6,4},{7,5},{8,10},{9,11},{10,... | collective-permute-start | bytes 2949128 | tf_op jit(solution)/shard_map/ppermute | solution.py:304
  92.1 50.2 %collective-permute-start.3 = (f32[640,768]{1,0:T(8,128)}, f32[640,768]{1,0:T(8,128)}, u32[]{:S(2)}, u32[]{:S(2)}) collective-permute-start(f32[640,768]{1,0:T(8,128)} %collective-permute-done.1.refs_2_), channel_id=1, source_target_pairs={{0,1},{1,0},{2,3},{3,2},{4,5},{5,4},{6,7},{7,6},{8,9},{9,8},{10,11... | collective-permute-start | bytes 5898248 | tf_op jit(solution)/shard_map/ppermute | solution.py:304
  92.1 51.3 %collective-permute-start.4 = (f32[640,768]{1,0:T(8,128)}, f32[640,768]{1,0:T(8,128)}, u32[]{:S(2)}, u32[]{:S(2)}) collective-permute-start(f32[640,768]{1,0:T(8,128)} %collective-permute-done.2.refs_3_), channel_id=1, source_target_pairs={{0,1},{1,0},{2,3},{3,2},{4,5},{5,4},{6,7},{7,6},{8,9},{9,8},{10,11... | collective-permute-start | bytes 5898248 | tf_op jit(solution)/shard_map/ppermute | solution.py:304
  135.5 73.9 %collective-permute-start.15 = (f32[640,768]{1,0:T(8,128)}, f32[640,768]{1,0:T(8,128)}, u32[]{:S(2)}, u32[]{:S(2)}) collective-permute-start(f32[640,768]{1,0:T(8,128)} %get-tuple-element.96), channel_id=1, source_target_pairs={{0,8},{8,0},{1,9},{9,1},{2,10},{10,2},{3,11},{11,3},{4,12},{12,4},... | collective-permute-start | bytes 5898248 | tf_op jit(solution)/shard_map/ppermute | solution.py:304
  140.7 10.4 %collective-permute-start.16 = (f32[320,768]{1,0:T(8,128)}, f32[320,768]{1,0:T(8,128)}, u32[]{:S(2)}, u32[]{:S(2)}) collective-permute-start(f32[320,768]{1,0:T(8,128)} %collective-permute-done.13.refs_0_), channel_id=1, source_target_pairs={{0,1},{1,0},{2,3},{3,2},{4,5},{5,4},{6,7},{7,6},{8,9},{9,8},{10,11... | collective-permute-start | bytes 2949128 | tf_op jit(solution)/shard_map/ppermute | solution.py:304
  140.7 10.4 %collective-permute-start.17 = (f32[320,768]{1,0:T(8,128)}, f32[320,768]{1,0:T(8,128)}, u32[]{:S(2)}, u32[]{:S(2)}) collective-permute-start(f32[320,768]{1,0:T(8,128)} %collective-permute-done.14.refs_1_), channel_id=1, source_target_pairs={{0,1},{1,0},{2,3},{3,2},{4,5},{5,4},{6,7},{7,6},{8,9},{9,8},{10,11... | collective-permute-start | bytes 2949128 | tf_op jit(solution)/shard_map/ppermute | solution.py:304
  142.3 8.8 %collective-permute-start.8 = (f32[2,640]{1,0:T(2,128)S(1)}, f32[2,640]{1,0:T(2,128)S(1)}, u32[]{:S(2)}, u32[]{:S(2)}) collective-permute-start(f32[2,640]{1,0:T(2,128)S(1)} %pad_maximum_fusion.refs_4_), channel_id=1, source_target_pairs={{0,3},{1,2},{2,1},{3,0},{4,7},{5,6},{6,5},{7,4},{8,11},{9,10},{10,... | collective-permute-start | bytes 15368 | tf_op jit(solution)/shard_map/ppermute | solution.py:304
  223.9 37.8 %collective-permute-start.24 = (f32[528,768]{1,0:T(8,128)}, f32[528,768]{1,0:T(8,128)S(1)}, u32[]{:S(2)}, u32[]{:S(2)}) collective-permute-start(f32[528,768]{1,0:T(8,128)} %get-tuple-element.117), channel_id=1, source_target_pairs={{0,2},{1,3},{2,0},{3,1},{4,6},{5,7},{6,4},{7,5},{8,10},{9,11},{10,... | collective-permute-start | bytes 4866056 | tf_op jit(solution)/shard_map/ppermute | solution.py:304
  224.5 37.6 %collective-permute-start.25 = (f32[528,768]{1,0:T(8,128)}, f32[528,768]{1,0:T(8,128)}, u32[]{:S(2)}, u32[]{:S(2)}) collective-permute-start(f32[528,768]{1,0:T(8,128)} %get-tuple-element.118), channel_id=1, source_target_pairs={{0,4},{1,5},{2,6},{3,7},{4,0},{5,1},{6,2},{7,3},{8,12},{9,13},{10,... | collective-permute-start | bytes 4866056 | tf_op jit(solution)/shard_map/ppermute | solution.py:304
  250.0 12.3 %collective-permute-start.22 = (f32[528,768]{1,0:T(8,128)S(1)}, f32[528,768]{1,0:T(8,128)S(1)}, u32[]{:S(2)}, u32[]{:S(2)}) collective-permute-start(f32[528,768]{1,0:T(8,128)S(1)} %get-tuple-element.158), channel_id=1, source_target_pairs={{0,1},{1,0},{2,3},{3,2},{4,5},{5,4},{6,7},{7,6},{8,9},{9,8},{10,11... | collective-permute-start | bytes 4866056 | tf_op jit(solution)/shard_map/ppermute | solution.py:304
  250.0 37.8 %collective-permute-start.18 = (f32[528,768]{1,0:T(8,128)}, f32[528,768]{1,0:T(8,128)}, u32[]{:S(2)}, u32[]{:S(2)}) collective-permute-start(f32[528,768]{1,0:T(8,128)} %get-tuple-element.117), channel_id=1, source_target_pairs={{0,1},{1,0},{2,3},{3,2},{4,5},{5,4},{6,7},{7,6},{8,9},{9,8},{10,11... | collective-permute-start | bytes 4866056 | tf_op jit(solution)/shard_map/ppermute | solution.py:304
  250.5 37.3 %collective-permute-start.23 = (f32[528,768]{1,0:T(8,128)}, f32[528,768]{1,0:T(8,128)}, u32[]{:S(2)}, u32[]{:S(2)}) collective-permute-start(f32[528,768]{1,0:T(8,128)} %get-tuple-element.159), channel_id=1, source_target_pairs={{0,1},{1,0},{2,3},{3,2},{4,5},{5,4},{6,7},{7,6},{8,9},{9,8},{10,11... | collective-permute-start | bytes 4866056 | tf_op jit(solution)/shard_map/ppermute | solution.py:304
  261.7 26.1 %collective-permute-start.20 = (f32[528,768]{1,0:T(8,128)}, f32[528,768]{1,0:T(8,128)}, u32[]{:S(2)}, u32[]{:S(2)}) collective-permute-start(f32[528,768]{1,0:T(8,128)} %get-tuple-element.119), channel_id=1, source_target_pairs={{0,1},{1,0},{2,3},{3,2},{4,5},{5,4},{6,7},{7,6},{8,9},{9,8},{10,11... | collective-permute-start | bytes 4866056 | tf_op jit(solution)/shard_map/ppermute | solution.py:304
  262.1 25.7 %collective-permute-start.21 = (f32[528,768]{1,0:T(8,128)}, f32[528,768]{1,0:T(8,128)}, u32[]{:S(2)}, u32[]{:S(2)}) collective-permute-start(f32[528,768]{1,0:T(8,128)} %get-tuple-element.120), channel_id=1, source_target_pairs={{0,1},{1,0},{2,3},{3,2},{4,5},{5,4},{6,7},{7,6},{8,9},{9,8},{10,11... | collective-permute-start | bytes 4866056 | tf_op jit(solution)/shard_map/ppermute | solution.py:304
  263.4 24.5 %collective-permute-start.19 = (f32[528,768]{1,0:T(8,128)}, f32[528,768]{1,0:T(8,128)}, u32[]{:S(2)}, u32[]{:S(2)}) collective-permute-start(f32[528,768]{1,0:T(8,128)} %get-tuple-element.118), channel_id=1, source_target_pairs={{0,1},{1,0},{2,3},{3,2},{4,5},{5,4},{6,7},{7,6},{8,9},{9,8},{10,11... | collective-permute-start | bytes 4866056 | tf_op jit(solution)/shard_map/ppermute | solution.py:304
  318.0 127.4 %collective-permute-start.46 = (f32[1376,768]{1,0:T(8,128)}, f32[1376,768]{1,0:T(8,128)}, u32[]{:S(2)}, u32[]{:S(2)}) collective-permute-start(f32[1376,768]{1,0:T(8,128)} %get-tuple-element.155), channel_id=1, source_target_pairs={{0,1},{1,0},{2,3},{3,2},{4,5},{5,4},{6,7},{7,6},{8,9},{9,8},{10,11... | collective-permute-start | bytes 12681224 | tf_op jit(solution)/shard_map/ppermute | solution.py:304
  318.2 36.7 %collective-permute-start.40 = (f32[528,768]{1,0:T(8,128)}, f32[528,768]{1,0:T(8,128)}, u32[]{:S(2)}, u32[]{:S(2)}) collective-permute-start(f32[528,768]{1,0:T(8,128)} %get-tuple-element.167), channel_id=1, source_target_pairs={{0,1},{1,0},{2,3},{3,2},{4,5},{5,4},{6,7},{7,6},{8,9},{9,8},{10,11... | collective-permute-start | bytes 4866056 | tf_op jit(solution)/shard_map/ppermute | solution.py:304
  318.6 37.2 %collective-permute-start.41 = (f32[528,768]{1,0:T(8,128)}, f32[528,768]{1,0:T(8,128)}, u32[]{:S(2)}, u32[]{:S(2)}) collective-permute-start(f32[528,768]{1,0:T(8,128)} %get-tuple-element.168), channel_id=1, source_target_pairs={{0,1},{1,0},{2,3},{3,2},{4,5},{5,4},{6,7},{7,6},{8,9},{9,8},{10,11... | collective-permute-start | bytes 4866056 | tf_op jit(solution)/shard_map/ppermute | solution.py:304
  320.1 10.2 %collective-permute-start.26 = (f32[56,768]{1,0:T(8,128)S(1)}, f32[56,768]{1,0:T(8,128)S(1)}, u32[]{:S(2)}, u32[]{:S(2)}) collective-permute-start(f32[56,768]{1,0:T(8,128)S(1)} %get-tuple-element.195), channel_id=1, source_target_pairs={{0,1},{1,0},{2,3},{3,2},{4,5},{5,4},{6,7},{7,6},{8,9},{9,8},{10,11... | collective-permute-start | bytes 516104 | tf_op jit(solution)/shard_map/ppermute | solution.py:304
  320.5 11.0 %collective-permute-start.27 = (f32[56,768]{1,0:T(8,128)S(1)}, f32[56,768]{1,0:T(8,128)S(1)}, u32[]{:S(2)}, u32[]{:S(2)}) collective-permute-start(f32[56,768]{1,0:T(8,128)S(1)} %get-tuple-element.194), channel_id=1, source_target_pairs={{0,2},{1,3},{2,0},{3,1},{4,6},{5,7},{6,4},{7,5},{8,10},{9,11},{10,... | collective-permute-start | bytes 516104 | tf_op jit(solution)/shard_map/ppermute | solution.py:304
  336.7 9.7 %collective-permute-start.30 = (f32[56,768]{1,0:T(8,128)S(1)}, f32[56,768]{1,0:T(8,128)S(1)}, u32[]{:S(2)}, u32[]{:S(2)}) collective-permute-start(f32[56,768]{1,0:T(8,128)S(1)} %get-tuple-element.191), channel_id=1, source_target_pairs={{0,5},{1,4},{2,7},{3,6},{4,1},{5,0},{6,3},{7,2},{8,13},{9,12},{10,... | collective-permute-start | bytes 516104 | tf_op jit(solution)/shard_map/ppermute | solution.py:304
  338.3 10.7 %collective-permute-start.31 = (f32[56,768]{1,0:T(8,128)S(1)}, f32[56,768]{1,0:T(8,128)S(1)}, u32[]{:S(2)}, u32[]{:S(2)}) collective-permute-start(f32[56,768]{1,0:T(8,128)S(1)} %get-tuple-element.190), channel_id=1, source_target_pairs={{0,6},{1,7},{2,4},{3,5},{4,2},{5,3},{6,0},{7,1},{8,14},{9,15},{10,... | collective-permute-start | bytes 516104 | tf_op jit(solution)/shard_map/ppermute | solution.py:304
  348.9 40.0 %collective-permute-start.44 = (f32[528,768]{1,0:T(8,128)}, f32[528,768]{1,0:T(8,128)}, u32[]{:S(2)}, u32[]{:S(2)}) collective-permute-start(f32[528,768]{1,0:T(8,128)} %get-tuple-element.119), channel_id=1, source_target_pairs={{0,2},{1,3},{2,0},{3,1},{4,6},{5,7},{6,4},{7,5},{8,10},{9,11},{10,... | collective-permute-start | bytes 4866056 | tf_op jit(solution)/shard_map/ppermute | solution.py:304
  353.7 38.4 %collective-permute-start.45 = (f32[528,768]{1,0:T(8,128)}, f32[528,768]{1,0:T(8,128)}, u32[]{:S(2)}, u32[]{:S(2)}) collective-permute-start(f32[528,768]{1,0:T(8,128)} %get-tuple-element.120), channel_id=1, source_target_pairs={{0,4},{1,5},{2,6},{3,7},{4,0},{5,1},{6,2},{7,3},{8,12},{9,13},{10,... | collective-permute-start | bytes 4866056 | tf_op jit(solution)/shard_map/ppermute | solution.py:304
  354.9 59.2 %collective-permute-start.42 = (f32[528,768]{1,0:T(8,128)S(1)}, f32[528,768]{1,0:T(8,128)}, u32[]{:S(2)}, u32[]{:S(2)}) collective-permute-start(f32[528,768]{1,0:T(8,128)S(1)} %collective-permute-done.24.refs_2_), channel_id=1, source_target_pairs={{0,1},{1,0},{2,3},{3,2},{4,5},{5,4},{6,7},{7,6},{8,9},{9,8},{10,11... | collective-permute-start | bytes 4866056 | tf_op jit(solution)/shard_map/ppermute | solution.py:304
  355.7 58.9 %collective-permute-start.43 = (f32[528,768]{1,0:T(8,128)}, f32[528,768]{1,0:T(8,128)}, u32[]{:S(2)}, u32[]{:S(2)}) collective-permute-start(f32[528,768]{1,0:T(8,128)} %collective-permute-done.25.refs_3_), channel_id=1, source_target_pairs={{0,1},{1,0},{2,3},{3,2},{4,5},{5,4},{6,7},{7,6},{8,9},{9,8},{10,11... | collective-permute-start | bytes 4866056 | tf_op jit(solution)/shard_map/ppermute | solution.py:304
  401.0 9.9 %collective-permute-start.37 = (f32[56,768]{1,0:T(8,128)S(1)}, f32[56,768]{1,0:T(8,128)S(1)}, u32[]{:S(2)}, u32[]{:S(2)}) collective-permute-start(f32[56,768]{1,0:T(8,128)S(1)} %fusion.10), channel_id=1, source_target_pairs={{0,5},{1,4},{2,7},{3,6},{4,1},{5,0},{6,3},{7,2},{8,13},{9,12},{10,... | collective-permute-start | bytes 516104 | tf_op jit(solution)/shard_map/ppermute | solution.py:304
  405.4 39.9 %collective-permute-start.38 = (f32[56,768]{1,0:T(8,128)S(1)}, f32[56,768]{1,0:T(8,128)S(1)}, u32[]{:S(2)}, u32[]{:S(2)}) collective-permute-start(f32[56,768]{1,0:T(8,128)S(1)} %fusion.10), channel_id=1, source_target_pairs={{0,6},{1,7},{2,4},{3,5},{4,2},{5,3},{6,0},{7,1},{8,14},{9,15},{10,... | collective-permute-start | bytes 516104 | tf_op jit(solution)/shard_map/ppermute | solution.py:304
  411.0 34.3 %collective-permute-start.39 = (f32[56,768]{1,0:T(8,128)S(1)}, f32[56,768]{1,0:T(8,128)S(1)}, u32[]{:S(2)}, u32[]{:S(2)}) collective-permute-start(f32[56,768]{1,0:T(8,128)S(1)} %fusion.10), channel_id=1, source_target_pairs={{0,7},{1,6},{2,5},{3,4},{4,3},{5,2},{6,1},{7,0},{8,15},{9,14},{10,... | collective-permute-start | bytes 516104 | tf_op jit(solution)/shard_map/ppermute | solution.py:304
  414.1 66.4 %collective-permute-start.47 = (f32[528,768]{1,0:T(8,128)}, f32[528,768]{1,0:T(8,128)}, u32[]{:S(2)}, u32[]{:S(2)}) collective-permute-start(f32[528,768]{1,0:T(8,128)} %copy-done.10), channel_id=1, source_target_pairs={{0,2},{1,3},{2,0},{3,1},{4,6},{5,7},{6,4},{7,5},{8,10},{9,11},{10,... | collective-permute-start | bytes 4866056 | tf_op jit(solution)/shard_map/ppermute | solution.py:304
  414.6 66.4 %collective-permute-start.48 = (f32[528,768]{1,0:T(8,128)}, f32[528,768]{1,0:T(8,128)}, u32[]{:S(2)}, u32[]{:S(2)}) collective-permute-start(f32[528,768]{1,0:T(8,128)} %get-tuple-element.159), channel_id=1, source_target_pairs={{0,4},{1,5},{2,6},{3,7},{4,0},{5,1},{6,2},{7,3},{8,12},{9,13},{10,... | collective-permute-start | bytes 4866056 | tf_op jit(solution)/shard_map/ppermute | solution.py:304
  445.3 49.1 %collective-permute-start.52 = (f32[1376,768]{1,0:T(8,128)}, f32[1376,768]{1,0:T(8,128)}, u32[]{:S(2)}, u32[]{:S(2)}) collective-permute-start(f32[1376,768]{1,0:T(8,128)} %get-tuple-element.162), channel_id=1, source_target_pairs={{0,1},{1,0},{2,3},{3,2},{4,5},{5,4},{6,7},{7,6},{8,9},{9,8},{10,11... | collective-permute-start | bytes 12681224 | tf_op jit(solution)/shard_map/ppermute | solution.py:304
  475.3 19.1 %collective-permute-start.53 = (f32[1376,768]{1,0:T(8,128)}, f32[1376,768]{1,0:T(8,128)}, u32[]{:S(2)}, u32[]{:S(2)}) collective-permute-start(f32[1376,768]{1,0:T(8,128)} %get-tuple-element.163), channel_id=1, source_target_pairs={{0,1},{1,0},{2,3},{3,2},{4,5},{5,4},{6,7},{7,6},{8,9},{9,8},{10,11... | collective-permute-start | bytes 12681224 | tf_op jit(solution)/shard_map/ppermute | solution.py:304
  475.9 9.4 %collective-permute-start.50 = (f32[528,768]{1,0:T(8,128)}, f32[528,768]{1,0:T(8,128)S(1)}, u32[]{:S(2)}, u32[]{:S(2)}) collective-permute-start(f32[528,768]{1,0:T(8,128)} %collective-permute-done.44.refs_0_), channel_id=1, source_target_pairs={{0,1},{1,0},{2,3},{3,2},{4,5},{5,4},{6,7},{7,6},{8,9},{9,8},{10,11... | collective-permute-start | bytes 4866056 | tf_op jit(solution)/shard_map/ppermute | solution.py:304
  481.0 9.0 %collective-permute-start.54 = (f32[528,768]{1,0:T(8,128)}, f32[528,768]{1,0:T(8,128)}, u32[]{:S(2)}, u32[]{:S(2)}) collective-permute-start(f32[528,768]{1,0:T(8,128)} %collective-permute-done.47.refs_4_), channel_id=1, source_target_pairs={{0,1},{1,0},{2,3},{3,2},{4,5},{5,4},{6,7},{7,6},{8,9},{9,8},{10,11... | collective-permute-start | bytes 4866056 | tf_op jit(solution)/shard_map/ppermute | solution.py:304
  486.4 8.1 %collective-permute-start.55 = (f32[528,768]{1,0:T(8,128)}, f32[528,768]{1,0:T(8,128)}, u32[]{:S(2)}, u32[]{:S(2)}) collective-permute-start(f32[528,768]{1,0:T(8,128)} %collective-permute-done.48.refs_5_), channel_id=1, source_target_pairs={{0,1},{1,0},{2,3},{3,2},{4,5},{5,4},{6,7},{7,6},{8,9},{9,8},{10,11... | collective-permute-start | bytes 4866056 | tf_op jit(solution)/shard_map/ppermute | solution.py:304
  488.7 37.9 %collective-permute-start.56 = (f32[528,768]{1,0:T(8,128)}, f32[528,768]{1,0:T(8,128)S(1)}, u32[]{:S(2)}, u32[]{:S(2)}) collective-permute-start(f32[528,768]{1,0:T(8,128)} %get-tuple-element.167), channel_id=1, source_target_pairs={{0,2},{1,3},{2,0},{3,1},{4,6},{5,7},{6,4},{7,5},{8,10},{9,11},{10,... | collective-permute-start | bytes 4866056 | tf_op jit(solution)/shard_map/ppermute | solution.py:304
  490.0 38.0 %collective-permute-start.57 = (f32[528,768]{1,0:T(8,128)}, f32[528,768]{1,0:T(8,128)}, u32[]{:S(2)}, u32[]{:S(2)}) collective-permute-start(f32[528,768]{1,0:T(8,128)} %get-tuple-element.168), channel_id=1, source_target_pairs={{0,4},{1,5},{2,6},{3,7},{4,0},{5,1},{6,2},{7,3},{8,12},{9,13},{10,... | collective-permute-start | bytes 4866056 | tf_op jit(solution)/shard_map/ppermute | solution.py:304
  528.0 33.1 %collective-permute-start.58 = (f32[528,768]{1,0:T(8,128)S(1)}, f32[528,768]{1,0:T(8,128)}, u32[]{:S(2)}, u32[]{:S(2)}) collective-permute-start(f32[528,768]{1,0:T(8,128)S(1)} %collective-permute-done.56.refs_0_), channel_id=1, source_target_pairs={{0,1},{1,0},{2,3},{3,2},{4,5},{5,4},{6,7},{7,6},{8,9},{9,8},{10,11... | collective-permute-start | bytes 4866056 | tf_op jit(solution)/shard_map/ppermute | solution.py:304
  528.0 33.1 %collective-permute-start.59 = (f32[528,768]{1,0:T(8,128)}, f32[528,768]{1,0:T(8,128)}, u32[]{:S(2)}, u32[]{:S(2)}) collective-permute-start(f32[528,768]{1,0:T(8,128)} %collective-permute-done.57.refs_1_), channel_id=1, source_target_pairs={{0,1},{1,0},{2,3},{3,2},{4,5},{5,4},{6,7},{7,6},{8,9},{9,8},{10,11... | collective-permute-start | bytes 4866056 | tf_op jit(solution)/shard_map/ppermute | solution.py:304
  529.8 28.0 %collective-permute-start.49 = (f32[384,768]{1,0:T(8,128)S(1)}, f32[384,768]{1,0:T(8,128)}, u32[]{:S(2)}, u32[]{:S(2)}) collective-permute-start(f32[384,768]{1,0:T(8,128)S(1)} %slice.113), channel_id=1, source_target_pairs={{0,8},{8,0},{1,9},{9,1},{2,10},{10,2},{3,11},{11,3},{4,12},{12,4},... | collective-permute-start | bytes 3538952 | tf_op jit(solution)/shard_map/ppermute | solution.py:304
  (59 other events, 531.3 us)

commit v2 on v1

v2 whole, which is shorter than its diff:
```python
import functools

import jax
import jax.numpy as jnp
from jax import lax
from jax.experimental import pallas as pl
from jax.experimental.pallas import tpu as pltpu
from jax.sharding import PartitionSpec as P


LN_EPS = 1e-5

BF16, F32, I32 = jnp.bfloat16, jnp.float32, jnp.int32
SLOTS = 80
OWN_SPLIT = 7
VT = 2304
CHUNK = 768
SHARE_CHUNKS, SHARE_TILE = 4, 624
LOCAL_TILES, LOCAL_TILE = 6, 432
LOCAL_CALLS = 2
TOK_CHUNK = 1280
VMEM_ROWS = 44
COST_SCALE = 4
OFF = 1e30
MIB = 2 ** 20


def head_norm(pre_act, ln_gain, ln_bias):
    gelu_out = jax.nn.gelu(pre_act, approximate=False)
    row_mean = jnp.mean(gelu_out, axis=-1, keepdims=True)
    centered = gelu_out - row_mean
    row_var = jnp.mean(centered * centered, axis=-1, keepdims=True)
    return centered * lax.rsqrt(row_var + LN_EPS) * ln_gain + ln_bias


def dot_nt(a, b):
    return lax.dot_general(a, b, (((1,), (1,)), ((), ())), preferred_element_type=F32)


def to_lanes(row):
    return jnp.broadcast_to(row, (128, row.shape[1])).T


def front_kernel(n_steps, hid_ref, pos_ref, w_ref, vec_ref, z_ref, pre_ref, u_ref, uf_ref):
    step = pl.program_id(0)
    pos = to_lanes(pos_ref[0])[:SLOTS]
    lane = lax.broadcasted_iota(I32, (SLOTS, 128), 1).astype(F32)
    hot = jnp.concatenate([jnp.where(pos == lane + k * 128.0, 1.0, 0.0) for k in range(hid_ref.shape[1] // 128)], axis=1)
    rows = pl.ds(pl.multiple_of(step * SLOTS, 16), SLOTS)
    z_ref[rows, :] = jnp.dot(hot.astype(BF16), hid_ref[0], preferred_element_type=F32).astype(BF16)

    @pl.when(step == n_steps - 1)
    def _():
        pre = jnp.dot(z_ref[...], w_ref[...], preferred_element_type=F32) + vec_ref[0:1, :]
        pre_ref[...] = pre
        act = 0.5 * pre * (1.0 + lax.erf(pre * 0.7071067811865476))
        cen = act - jnp.mean(act, axis=1, keepdims=True)
        var = jnp.mean(cen * cen, axis=1, keepdims=True)
        u = (cen * lax.rsqrt(var + LN_EPS) * vec_ref[1:2, :] + vec_ref[2:3, :]).astype(BF16)
        u_ref[...] = u
        uf_ref[...] = u.astype(F32)


def own_kernel(n_steps, first, u_ref, emb_ref, bias_ref, col_ref, lab_row_ref, *refs):
    acc_in, state_in = (None, None) if first else refs[:2]
    acc_ref, stat_ref, m_ref, s_ref, t_ref, lab_ref = refs if first else refs[2:]
    step = pl.program_id(0)

    @pl.when(step == 0)
    def _():
        lab_ref[...] = to_lanes(lab_row_ref[...])
        if first:
            m_ref[...] = jnp.full_like(m_ref, -1e38)
            s_ref[...] = jnp.zeros_like(s_ref)
            t_ref[...] = jnp.zeros_like(t_ref)
            acc_ref[...] = jnp.zeros_like(acc_ref)
        else:
            m_ref[...], s_ref[...], t_ref[...] = state_in[0], state_in[1], state_in[2]
            acc_ref[...] = acc_in[...]

    wide = lambda x, n: jnp.concatenate([x] * (n // 128), axis=1)
    fold = lambda x: functools.reduce(jnp.add, [x[:, k * 128:(k + 1) * 128] for k in range(CHUNK // 128)])
    logit = lambda q: dot_nt(u_ref[...], emb_ref[q * CHUNK:(q + 1) * CHUNK, :]) + bias_ref[0, :, q * CHUNK:(q + 1) * CHUNK]
    following = logit(0)
    for q in range(VT // CHUNK):
        block, cs = following, slice(q * CHUNK, (q + 1) * CHUNK)
        if q + 1 < VT // CHUNK:
            following = logit(q + 1)
        hot = col_ref[0, :, cs] == wide(lab_ref[...], CHUNK)
        m_old = m_ref[...]
        m_new = jnp.maximum(m_old, jnp.max(block, axis=1, keepdims=True))
        scale = jnp.exp(m_old - m_new)
        prob = jnp.exp(block - wide(m_new, CHUNK))
        m_ref[...] = m_new
        s_ref[...] = s_ref[...] * scale + fold(prob)
        t_ref[...] += fold(jnp.where(hot, block, 0.0))
        rest = jnp.where(hot, 0.0, prob).astype(BF16)
        acc_ref[...] = acc_ref[...] * wide(scale, acc_ref.shape[1]) + jnp.dot(rest, emb_ref[cs, :], preferred_element_type=F32)

    @pl.when(step == n_steps - 1)
    def _():
        if first:
            for k, ref in enumerate((m_ref, s_ref, t_ref)):
                stat_ref[k] = ref[...]
            return
        mass = jnp.sum(s_ref[...], axis=1, keepdims=True)
        target = jnp.sum(t_ref[...], axis=1, keepdims=True)
        lane = lax.broadcasted_iota(I32, m_ref.shape, 1)
        stat_ref[...] = jnp.where(lane == 0, m_ref[...], jnp.where(lane == 1, mass, target)).T[:8]


def norm_kernel(n_masks, inv_n, shard_rows, plane_ref, mine_ref, other_ref, lab_ref, tok_ref, coef_ref, loss_ref):
    low = plane_ref[0] == 0
    mine, other = mine_ref[...], other_ref[...]
    lo, hi = jnp.where(low, mine, other), jnp.where(low, other, mine)
    top = jnp.maximum(lo[0:1], hi[0:1])
    log_norm = top + jnp.log(lo[1:2] * jnp.exp(lo[0:1] - top) + hi[1:2] * jnp.exp(hi[0:1] - top))
    valid = lax.rem(lax.broadcasted_iota(I32, log_norm.shape, 1), SLOTS) < n_masks
    norm = jnp.where(valid, log_norm, OFF)
    lab = lab_ref[...]
    tok_ref[0:1, :] = norm
    tok_ref[1:2, :] = lab
    here = (lab >= 0.0) & (lab < shard_rows)
    coef_ref[0:1, :] = jnp.exp(mine[0:1] - norm) * inv_n
    coef_ref[1:2, :] = jnp.where(here, (jnp.exp(mine[2:3] - norm) - 1.0) * inv_n, 0.0)
    loss = jnp.sum(jnp.where(valid, log_norm - (lo[2:3] + hi[2:3]), 0.0), axis=1, keepdims=True) * inv_n
    loss_ref[...] = jnp.broadcast_to(loss, loss_ref.shape)


def du_kernel(acc_ref, row_ref, coef_ref, du_ref):
    wide = lambda x: jnp.concatenate([x] * (acc_ref.shape[1] // 128), axis=1)
    hot = to_lanes(coef_ref[1:2, :]).astype(BF16).astype(F32)
    du = acc_ref[...] * wide(to_lanes(coef_ref[0:1, :])) + row_ref[...].astype(F32) * wide(hot)
    du_ref[...] = du.astype(BF16).astype(F32)


def place_kernel(n, start_ref, *refs):
    pieces, out_ref, bufs, sems = refs[:n], refs[n], refs[n + 1:-1], refs[-1]
    loads = [pltpu.make_async_copy(pieces[k], bufs[k], sems.at[k]) for k in range(n)]
    for load in loads:
        load.start()
    for k in range(n):
        loads[k].wait()
        out_ref[pl.ds(pl.multiple_of(start_ref[k] * 16, 16), pieces[k].shape[0]), :] = bufs[k][...].astype(BF16)


def place(pieces, starts, n_all):
    n, width = len(pieces), pieces[0].shape[1]
    return pl.pallas_call(
        functools.partial(place_kernel, n),
        grid_spec=pltpu.PrefetchScalarGridSpec(
            num_scalar_prefetch=1,
            grid=(1,),
            in_specs=[pl.BlockSpec(memory_space=pl.ANY)] * n,
            out_specs=pl.BlockSpec(memory_space=pltpu.VMEM),
            scratch_shapes=[pltpu.VMEM(p.shape, F32) for p in pieces] + [pltpu.SemaphoreType.DMA((n,))],
        ),
        out_shape=jax.ShapeDtypeStruct((n_all, width), BF16),
        compiler_params=pltpu.CompilerParams(vmem_limit_bytes=40 * MIB),
        cost_estimate=pl.CostEstimate(flops=5 * 10 ** 9, bytes_accessed=6 * n_all * width, transcendentals=0),
    )(starts, *pieces)


def tok_kernel(n, start_ref, *refs):
    for k in range(n):
        row = pl.ds(start_ref[k], 1)
        refs[n][row, :] = refs[k][0:1, :]
        refs[n + 1][row, :] = refs[k][1:2, :]


def place_toks(toks, ranks):
    n, width = len(toks), toks[0].shape[1]
    return pl.pallas_call(
        functools.partial(tok_kernel, n),
        grid_spec=pltpu.PrefetchScalarGridSpec(
            num_scalar_prefetch=1,
            grid=(1,),
            in_specs=[pl.BlockSpec(t.shape, lambda i, s: (0, 0)) for t in toks],
            out_specs=[pl.BlockSpec((n, width), lambda i, s: (0, 0))] * 2,
        ),
        out_shape=[jax.ShapeDtypeStruct((n, width), F32)] * 2,
    )(ranks, *toks)


def piece_kernel(n, start_ref, *refs):
    for k in range(n):
        refs[n][start_ref[k]] = refs[k][...]


def gather_pieces(pieces, ranks):
    n = len(pieces)
    shape = (n,) + pieces[0].shape
    return pl.pallas_call(
        functools.partial(piece_kernel, n),
        grid_spec=pltpu.PrefetchScalarGridSpec(
            num_scalar_prefetch=1,
            grid=(1,),
            in_specs=[pl.BlockSpec(p.shape, lambda i, s: (0, 0)) for p in pieces],
            out_specs=pl.BlockSpec(shape, lambda i, s: (0, 0, 0)),
        ),
        out_shape=jax.ShapeDtypeStruct(shape, F32),
    )(ranks, *pieces)


def rows_kernel(cfg, start_ref, emb_ref, bias_ref, u_ref, norm_ref, lab_ref, *refs):
    n_steps, tile, inv_n, n_send, n_copy, aliased = cfg
    arrived, refs = refs[:n_copy], refs[n_copy + (1 if aliased else 0):]
    out_ref, db_ref, sends, refs = refs[0], refs[1], refs[2:2 + n_send], refs[2 + n_send:]
    acc_ref, out_sem, send_sem = refs[:3]
    stage, load_sem, store_sem = (refs[3:3 + n_copy], refs[3 + n_copy], refs[4 + n_copy]) if n_copy else ((), None, None)
    step = pl.program_id(0)
    slot = lax.rem(step, 2)
    n_tok = u_ref.shape[0]

    def load(k):
        return pltpu.make_async_copy(arrived[k], stage[k], load_sem.at[k])

    def store(k):
        rows = pl.ds(pl.multiple_of(start_ref[2 * n_steps + k] * 16, 16), arrived[k].shape[0])
        return pltpu.make_async_copy(stage[k], out_ref.at[rows, :], store_sem.at[k])

    @pl.when(step == 0)
    def _():
        for k in range(n_copy):
            load(k).start()

    @pl.when(step == 1)
    def _():
        for k in range(n_copy):
            load(k).wait()
            store(k).start()

    def out_copy(t, which):
        rows = pl.ds(pl.multiple_of(start_ref[t] * 16, 16), tile)
        return pltpu.make_async_copy(acc_ref.at[which], out_ref.at[rows, :], out_sem.at[which])

    def send_copy(t, which):
        rows = pl.ds(pl.multiple_of(t * tile, 16), tile) if n_send == 1 else pl.ds(0, tile)
        target = sends[0] if n_send == 1 else sends[t]
        return pltpu.make_async_copy(acc_ref.at[which], target.at[rows, :], send_sem.at[which])

    @pl.when(step >= 2)
    def _():
        out_copy(step - 2, slot).wait()
        pltpu.make_async_copy(acc_ref.at[slot], sends[0].at[pl.ds(0, tile), :], send_sem.at[slot]).wait()

    row_id = lax.broadcasted_iota(I32, (tile, 1), 0).astype(F32) + (start_ref[step] * 16).astype(F32)
    bias = jnp.concatenate([to_lanes(bias_ref[0])[:tile]] * (TOK_CHUNK // 128), axis=1)
    per = TOK_CHUNK // norm_ref.shape[1]
    for j in range(n_tok // TOK_CHUNK):
        s = slice(j * TOK_CHUNK, (j + 1) * TOK_CHUNK)
        norm = jnp.concatenate([norm_ref[i:i + 1, :] for i in range(j * per, (j + 1) * per)], axis=1)
        lab = jnp.concatenate([lab_ref[i:i + 1, :] for i in range(j * per, (j + 1) * per)], axis=1)
        logit = dot_nt(emb_ref[...], u_ref[s, :]) + bias
        prob = jnp.exp(logit - norm)
        grad = (prob - jnp.where(lab == row_id, 1.0, 0.0)) * inv_n
        part = jnp.dot(grad.astype(BF16), u_ref[s, :], preferred_element_type=F32)
        lanes = functools.reduce(jnp.add, [grad[:, k * 128:(k + 1) * 128] for k in range(TOK_CHUNK // 128)])
        db = lanes if j == 0 else db + lanes
        if j == 0:
            acc_ref[slot] = part
        else:
            acc_ref[slot] += part

    db = jnp.concatenate([db, jnp.zeros((db_ref.shape[2] - tile, 128), F32)])
    db_ref[0] = jnp.sum(db.T, axis=0, keepdims=True)
    out_copy(step, slot).start()
    if n_send == 1:
        send_copy(step, slot).start()
    else:
        for t in range(n_send):
            @pl.when(step == t)
            def _():
                send_copy(t, t % 2).start()

    @pl.when(step == n_steps - 1)
    def _():
        for k in range(n_copy):
            store(k).wait()
        for t in range(max(0, n_steps - 2), n_steps):
            out_copy(t, t % 2).wait()
            pltpu.make_async_copy(acc_ref.at[t % 2], sends[0].at[pl.ds(0, tile), :], send_sem.at[t % 2]).wait()


def emb_rows(out, starts, blocks, emb, bias, u_all, norm, lab, inv_n, tile, n_steps, n_send, arrived, copy_starts):
    n_tok, width = u_all.shape
    n_rows = emb.shape[0]
    n_copy = len(arrived)
    aliased = out is not None
    cfg = (n_steps, tile, inv_n, n_send, n_copy, aliased)
    table = jnp.concatenate([starts, blocks] + list(copy_starts)).astype(I32)
    any_space = pl.BlockSpec(memory_space=pl.ANY)
    whole = lambda a: pl.BlockSpec(a.shape, lambda i, s: (0, 0))
    send_rows = n_steps * tile if n_send == 1 else tile
    scratch = [pltpu.VMEM((2, tile, width), F32), pltpu.SemaphoreType.DMA((2,)), pltpu.SemaphoreType.DMA((2,))]
    if n_copy:
        scratch += [pltpu.VMEM(a.shape, F32) for a in arrived] + [pltpu.SemaphoreType.DMA((n_copy,))] * 2
    return pl.pallas_call(
        functools.partial(rows_kernel, cfg),
        grid_spec=pltpu.PrefetchScalarGridSpec(
            num_scalar_prefetch=1,
            grid=(n_steps,),
            in_specs=[
                pl.BlockSpec((pl.Element(tile), pl.Element(width)), lambda i, s: (pl.multiple_of(s[i] * 16, 16), 0)),
                pl.BlockSpec((1, 1, bias.shape[2]), lambda i, s: (s[n_steps + i], 0, 0)),
                pl.BlockSpec(memory_space=pltpu.VMEM), whole(norm), whole(lab),
            ] + [any_space] * (n_copy + aliased),
            out_specs=[any_space, pl.BlockSpec((1, 1, bias.shape[2]), lambda i, s: (i, 0, 0))] + [any_space] * n_send,
            scratch_shapes=scratch,
        ),
        out_shape=[jax.ShapeDtypeStruct((n_rows, width), F32), jax.ShapeDtypeStruct((n_steps, 1, bias.shape[2]), F32)] + [jax.ShapeDtypeStruct((send_rows, width), F32)] * n_send,
        input_output_aliases={6 + n_copy: 0} if aliased else {},
        compiler_params=pltpu.CompilerParams(vmem_limit_bytes=VMEM_ROWS * MIB),
        cost_estimate=pl.CostEstimate(
            flops=n_steps * tile * n_tok * width // COST_SCALE, bytes_accessed=n_steps * tile * width * 10, transcendentals=n_steps * tile * n_tok
        ),
    )(table, emb, bias, u_all, norm, lab, *arrived, *([out] if aliased else []))


def copy_kernel(n, start_ref, *refs):
    arrived, out_ref, stage, load_sem, store_sem = refs[:n], refs[n + 1], refs[n + 2:-2], refs[-2], refs[-1]
    loads = [pltpu.make_async_copy(arrived[k], stage[k], load_sem.at[k]) for k in range(n)]
    for load in loads:
        load.start()
    stores = []
    for k in range(n):
        loads[k].wait()
        rows = pl.ds(pl.multiple_of(start_ref[k] * 16, 16), arrived[k].shape[0])
        stores.append(pltpu.make_async_copy(stage[k], out_ref.at[rows, :], store_sem.at[k]))
        stores[-1].start()
    for store in stores:
        store.wait()


def copy_rows(out, arrived, starts):
    n = len(arrived)
    return pl.pallas_call(
        functools.partial(copy_kernel, n),
        grid_spec=pltpu.PrefetchScalarGridSpec(
            num_scalar_prefetch=1,
            grid=(1,),
            in_specs=[pl.BlockSpec(memory_space=pl.ANY)] * (n + 1),
            out_specs=pl.BlockSpec(memory_space=pl.ANY),
            scratch_shapes=[pltpu.VMEM(a.shape, F32) for a in arrived] + [pltpu.SemaphoreType.DMA((n,))] * 2,
        ),
        out_shape=jax.ShapeDtypeStruct(out.shape, F32),
        input_output_aliases={n + 1: 0},
        compiler_params=pltpu.CompilerParams(vmem_limit_bytes=48 * MIB),
        cost_estimate=pl.CostEstimate(flops=5 * 10 ** 9, bytes_accessed=8 * sum(a.size for a in arrived), transcendentals=0),
    )(jnp.concatenate(starts).astype(I32), *arrived, out)


def swap(x, mask, axis="dp"):
    n = 8 if axis == "dp" else 2
    return lax.ppermute(x, axis, [(i, i ^ mask) for i in range(n)])


def solution(mesh):
    n_groups = mesh.shape["dp"]

    def local_step(hidden, mask_pos, labels, w_trans, b_trans, ln_gain, ln_bias, emb_table, b_vocab):
        n_rows, seq_len, width = hidden.shape
        n_masks = mask_pos.shape[1]
        shard_rows = emb_table.shape[0]
        inv_n = 1.0 / (n_rows * n_masks * n_groups)
        n_own = n_rows * SLOTS
        n_all = n_own * n_groups
        me, plane = lax.axis_index("dp"), lax.axis_index("vp")
        core, par = me & 1, ((me >> 1) ^ (me >> 2)) & 1
        row_start = plane * shard_rows

        pos = jnp.pad(mask_pos, ((0, 0), (0, SLOTS - n_masks)), constant_values=-1)
        pos_onehot = (pos[:, :, None] == jnp.arange(seq_len)[None, None, :]).astype(BF16)
        pos_row = jnp.pad(mask_pos, ((0, 0), (0, 128 - n_masks)), constant_values=-1).astype(F32)[:, None, :]
        tok_f32, tok_bf16 = jax.ShapeDtypeStruct((n_own, width), F32), jax.ShapeDtypeStruct((n_own, width), BF16)
        own_block = pl.BlockSpec((n_own, width), lambda i: (0, 0))
        masked_h, pre_act, u_own, u_f = pl.pallas_call(
            functools.partial(front_kernel, n_rows),
            grid=(n_rows,),
            in_specs=[
                pl.BlockSpec((1, seq_len, width), lambda i: (i, 0, 0)), pl.BlockSpec((1, 1, 128), lambda i: (i, 0, 0)),
                pl.BlockSpec((width, width), lambda i: (0, 0)), pl.BlockSpec((3, width), lambda i: (0, 0)),
            ],
            out_specs=[own_block] * 4,
            out_shape=[tok_bf16, tok_f32, tok_bf16, tok_f32],
            compiler_params=pltpu.CompilerParams(vmem_limit_bytes=48 * MIB),
            cost_estimate=pl.CostEstimate(flops=2 * n_own * width * (width + seq_len), bytes_accessed=2 * hidden.size, transcendentals=0),
        )(hidden, pos_row, w_trans, jnp.stack([b_trans, ln_gain, ln_bias]))

        _, head_vjp = jax.vjp(head_norm, pre_act, ln_gain, ln_bias)

        half = n_own // 2
        u_sib, u_x, u_y = swap(u_f, 1), swap(u_f, 2), swap(u_f, 4)
        blk = n_own // 16
        at = lambda m, o=0: ((me ^ m) * blk + o)[None]

        n_steps = -(-shard_rows // VT)
        last = shard_rows - VT
        dup = n_steps * VT - shard_rows
        b_pad = jnp.concatenate([b_vocab[:shard_rows - (VT - dup)], jnp.full((dup,), -OFF, F32), b_vocab[shard_rows - (VT - dup):]]).reshape(n_steps, 1, VT)
        ids = jnp.arange(shard_rows, dtype=F32)
        cols = jnp.concatenate([ids[:shard_rows - (VT - dup)], jnp.full((dup,), -7.0, F32), ids[shard_rows - (VT - dup):]]).reshape(n_steps, 1, VT)
        lab_pad = jnp.pad(labels, ((0, 0), (0, SLOTS - n_masks)), constant_values=-1000000).reshape(n_own)
        lab_rel = (lab_pad - row_start).astype(F32)
        lab_row = lab_rel[None]
        row_block = pl.BlockSpec((1, n_own), lambda i: (0, 0))
        emb_block = pl.BlockSpec((pl.Element(VT), pl.Element(width)), lambda i: (pl.multiple_of(jnp.minimum(i * (VT // 16), last // 16) * 16, 16), 0))
        col_block = pl.BlockSpec((1, 1, VT), lambda i: (i, 0, 0))
        state = jax.ShapeDtypeStruct((3, n_own, 128), F32)
        state_block = pl.BlockSpec(state.shape, lambda i: (0, 0, 0))

        def own_call(begin, end, carry):
            first = not carry
            skip = lambda i: i + begin
            last_shape = state if first else jax.ShapeDtypeStruct((8, n_own), F32)
            return pl.pallas_call(
                functools.partial(own_kernel, end - begin, first),
                grid=(end - begin,),
                in_specs=[
                    own_block,
                    pl.BlockSpec((pl.Element(VT), pl.Element(width)), lambda i: (pl.multiple_of(jnp.minimum(skip(i) * (VT // 16), last // 16) * 16, 16), 0)),
                    pl.BlockSpec((1, 1, VT), lambda i: (skip(i), 0, 0)), pl.BlockSpec((1, 1, VT), lambda i: (skip(i), 0, 0)), row_block,
                ] + ([] if first else [own_block, state_block]),
                out_specs=[own_block, state_block if first else pl.BlockSpec((8, n_own), lambda i: (0, 0))],
                out_shape=[tok_f32, last_shape],
                scratch_shapes=[pltpu.VMEM((n_own, 128), F32)] * 4,
                compiler_params=pltpu.CompilerParams(vmem_limit_bytes=56 * MIB),
                cost_estimate=pl.CostEstimate(
                    flops=4 * n_own * (end - begin) * VT * width // COST_SCALE, bytes_accessed=2 * (end - begin) * VT * width, transcendentals=n_own * shard_rows),
            )(u_own, emb_table, b_pad, cols, lab_row, *carry)

        carry = own_call(0, OWN_SPLIT, ())
        u_x, u_y, carry = lax.optimization_barrier((u_x, u_y, carry))
        u_d0, u_d1 = swap(u_x[:half], 4), swap(u_y[half:], 2)
        u_xs, u_ys = swap(u_x, 1), swap(u_y, 1)
        du_sum, stats = own_call(OWN_SPLIT, n_steps, carry)
        lab_local = lab_pad - row_start
        spread = jnp.arange(n_own, dtype=I32) * (shard_rows // n_own)
        label_rows = jnp.take(emb_table, jnp.where((lab_local >= 0) & (lab_local < shard_rows), lab_local, spread), axis=0)
        other = swap(stats, 1, "vp")
        (u_d0, u_d1), du_sum = lax.optimization_barrier(((u_d0, u_d1), du_sum))
        u_ds0, u_ds1 = swap(u_d0, 1), swap(u_d1, 1)

        u_all = place(
            [u_f, u_sib, u_x, u_y, u_xs, u_ys, u_d0, u_d1, u_ds0, u_ds1],
            jnp.concatenate([at(0), at(1), at(2), at(4), at(3), at(5), at(6), at(6, blk // 2), at(7), at(7, blk // 2)]).astype(I32), n_all)
        tok, coef, loss_row = pl.pallas_call(
            functools.partial(norm_kernel, n_masks, inv_n, shard_rows),
            in_specs=[pl.BlockSpec(memory_space=pltpu.SMEM)] + [pl.BlockSpec(memory_space=pltpu.VMEM)] * 3,
            out_shape=[jax.ShapeDtypeStruct((2, n_own), F32)] * 2 + [jax.ShapeDtypeStruct((1, width), F32)],
        )(plane[None], stats, other, lab_row)
        toks = [tok] + [swap(tok, m) for m in range(1, n_groups)]
        du_part = pl.pallas_call(
            du_kernel, out_shape=tok_f32, compiler_params=pltpu.CompilerParams(vmem_limit_bytes=32 * MIB),
            cost_estimate=pl.CostEstimate(flops=10 ** 9, bytes_accessed=10 * n_own * width, transcendentals=0),
        )(du_sum, label_rows, coef)
        du_other = swap(du_part, 1, "vp")
        ranks = jnp.stack([me ^ m for m in range(n_groups)]).astype(I32)
        norm_all, lab_all = place_toks(toks, ranks)

        nx, nl = SHARE_CHUNKS * SHARE_TILE // 16, LOCAL_TILES * LOCAL_TILE // 16
        assert 16 * (8 * nx + 2 * nl) == shard_rows
        st = SHARE_TILE // 16
        x_at = lambda p, c, k: ((2 * p + c) * nx + k * st)[None]
        y_at = lambda p, c, k: (4 * nx + (2 * p + c) * nx + k * st)[None]
        pad128 = lambda x: jnp.pad(x, ((0, 0), (0, -x.shape[1] % 128)))[:, None, :]
        bias_share = pad128(b_vocab[:16 * 8 * nx].reshape(-1, SHARE_TILE))
        bias_local = pad128(b_vocab[16 * 8 * nx:].reshape(-1, LOCAL_TILE))
        lt = LOCAL_TILE // 16
        out = None

        def rows_call(out, starts, blocks, bias, tile, n_steps, n_send, take):
            return emb_rows(out, starts, blocks, emb_table, bias, u_all, norm_all, lab_all, inv_n, tile, n_steps, n_send,
                            [a for a, _ in take], [s[:1] for _, s in take])

        per = LOCAL_TILES // LOCAL_CALLS
        l_at = lambda c, k: jnp.stack([8 * nx + c * nl + (k * per + i) * lt for i in range(per)])

        def shared_rows(out, k, take):
            starts = jnp.concatenate([x_at(par, core, k), y_at(par, core, k)])
            return rows_call(out, starts, starts // st, bias_share, SHARE_TILE, 2, 2, take)

        def local_rows(out, k, take):
            starts = l_at(core, k)
            out, db, rows = rows_call(out, starts, (starts - 8 * nx) // lt, bias_local, LOCAL_TILE, per, 1, take)
            return out, (swap(rows, 1), l_at(1 - core, k)), db[:, 0, :LOCAL_TILE]

        def near(k, sx, sy):
            return [(swap(sx, 1), x_at(par, 1 - core, k)), (swap(sy, 1), y_at(par, 1 - core, k))]

        def far(k, rx, ry):
            return [(rx, x_at(1 - par, core, k)), (ry, y_at(1 - par, core, k)),
                    (swap(rx, 1), x_at(1 - par, 1 - core, k)),
                    (swap(ry, 1), y_at(1 - par, 1 - core, k))]

        after = lax.optimization_barrier
        out, db0, sx0, sy0 = shared_rows(out, 0, [])
        rx0, ry0 = swap(sx0, 2), swap(sy0, 4)
        near0 = near(0, sx0, sy0)
        out, db1, sx1, sy1 = shared_rows(out, 1, [])
        rx1, ry1 = swap(sx1, 2), swap(sy1, 4)
        near1 = near(1, sx1, sy1)

        du_other, out = after((du_other, out))
        d_pre, d_ln_gain, d_ln_bias = head_vjp(du_part + du_other)
        d_pre_bf = d_pre.astype(BF16)
        d_w_part = lax.dot_general(masked_h, d_pre_bf, (((0,), (0,)), ((), ())), preferred_element_type=F32)
        hw = width // 2
        small = jnp.concatenate([jnp.sum(d_pre, axis=0), d_ln_gain, d_ln_bias, loss_row[0]]).reshape(4, width)
        total = hw + 4
        padded = -(-total // 64) * 64
        part = padded // n_groups
        mine = jnp.concatenate([lax.dynamic_slice(d_w_part, (plane * hw, 0), (hw, width)), small, jnp.zeros((padded - total, width), F32)])
        mine = mine.reshape(n_groups, part, width)
        mine, out, d_pre_bf = after((mine, out, d_pre_bf))
        piece = lambda a, m: lax.dynamic_index_in_dim(a, me ^ m, 0, keepdims=False)
        got = [swap(piece(mine, m), m) for m in range(1, n_groups)]

        out, db2, sx2, sy2 = shared_rows(out, 2, [])
        near2 = near(2, sx2, sy2)
        out, rx0, ry0, sx2, sy2 = after((out, rx0, ry0, sx2, sy2))
        rx2, ry2 = swap(sx2, 2), swap(sy2, 4)
        far0 = far(0, rx0, ry0)
        out, db3, sx3, sy3 = shared_rows(out, 3, near0 + near1)
        near3 = near(3, sx3, sy3)
        out, rx1, ry1, sx3, sy3, got = after((out, rx1, ry1, sx3, sy3, got))
        rx3, ry3 = swap(sx3, 2), swap(sy3, 4)
        far1 = far(1, rx1, ry1)
        parts = [piece(mine, 0)] + got
        level = lambda v: [v[i] + v[i + 1] for i in range(0, len(v), 2)]
        acc = level(level(level(parts)))[0]
        db_mine = jnp.stack([jnp.concatenate([d[i, 0, :SHARE_TILE] for d in (db0, db1, db2, db3)]) for i in range(2)])
        acc, db_mine, out = after((acc, db_mine, out))
        sums = [acc] + [swap(acc, m) for m in range(1, n_groups)]
        db_rel = [db_mine] + [swap(db_mine, m) for m in (1, 2, 3)]
        out, got0, dl0 = local_rows(out, 0, near2 + far0)
        sums, out = after((sums, out))
        grads = gather_pieces(sums, ranks).reshape(padded, width)
        w_half, out = after((grads[:hw], out))
        w_other = swap(w_half, 1, "vp")
        d_masked = dot_nt(d_pre_bf, w_trans).astype(BF16).reshape(n_rows, SLOTS, width)
        out, rx2, ry2, d_masked, db_rel = after((out, rx2, ry2, d_masked, db_rel))
        far2 = far(2, rx2, ry2)
        db_sh = jnp.stack(db_rel, 1).reshape(2, 2, 2, 16 * nx)
        db_sh = jnp.where(par == 1, jnp.flip(db_sh, 1), db_sh)
        db_sh = jnp.where(core == 1, jnp.flip(db_sh, 2), db_sh).reshape(2 * 4 * 16 * nx)
        out, got1, dl1 = local_rows(out, 1, near3 + far1 + far2[:2])
        out, rx3, ry3 = after((out, rx3, ry3))
        far3 = far(3, rx3, ry3)
        dl_mine = jnp.concatenate([dl0, dl1]).reshape(16 * nl)
        dl_other = swap(dl_mine, 1)
        d_hidden = jnp.einsum("clt,cle->cte", pos_onehot, d_masked, preferred_element_type=F32).astype(BF16)
        put = lambda out, items: copy_rows(out, [a for a, _ in items], [s[:1] for _, s in items])
        out = put(out, far2[2:] + [got0] + far3[:2])
        d_emb_table = put(out, [got1] + far3[2:])
        d_w_trans = gather_pieces([w_half, w_other], jnp.stack([plane, 1 - plane]).astype(I32)).reshape(width, width)
        vec = grads[hw:hw + 3]
        mlm_loss = grads[hw + 3, 0]
        d_b_vocab = jnp.concatenate([db_sh, jnp.where(core == 0, dl_mine, dl_other), jnp.where(core == 0, dl_other, dl_mine)])
        return mlm_loss, d_hidden, d_w_trans, vec[0], vec[1], vec[2], d_emb_table, d_b_vocab

    in_specs = (P("dp", None, None), P("dp", None), P("dp", None), P(None, None), P(None), P(None), P(None), P("vp", None), P("vp"))
    out_specs = (P(), P("dp", None, None), P(None, None), P(None), P(None), P(None), P("vp", None), P("vp"))

    return jax.shard_map(local_step, mesh=mesh, in_specs=in_specs, out_specs=out_specs, check_vma=False)
```

time: 577 us -> 521 us (0.903)
  waiting for transfers between devices: 132 us -> 112 us
  Pallas kernels: 304 us -> 286 us
  matrix products: 27.8 us -> 10.2 us
  local copies, waits for them, and re-layouts: 32.5 us -> 43.9 us
  starting transfers between devices: 49.9 us -> 40.4 us
    ppermute x60 -> x63, waiting for transfers between devices: 132 us -> 112 us  [swap(): return lax.ppermute(x, axis, [(i, i ^ mask) for i in range(n)])]
    pallas_call x7 -> x6, Pallas kernels: 185 us -> 166 us  [emb_rows(): pl.pallas_call(functools.partial(rows_kernel, cfg), grid_spec=pltpu.Prefe...]
    dot_general x2 -> x0, matrix products: 17.4 us -> none  [the longest x1 13.4 us: local_step(): pre_act = jnp.dot(masked_h, w_trans, preferred_element_type=F32) + b_trans]
    gather x0 -> x1, local copies, waits for them, and re-layouts: none -> 11 us  [local_step(): jnp.take(emb_table, jnp.where((lab_local >= 0) & (lab_local < shard_rows)...]
    ppermute x60 -> x63, starting transfers between devices: 49.9 us -> 40.4 us  [swap(): return lax.ppermute(x, axis, [(i, i ^ mask) for i in range(n)])]
    pallas_call x4 -> x9, Pallas kernels: 101 us -> 106 us  [the longest x2 75.1 us: own_call(): pl.pallas_call(functools.partial(own_kernel, end - begin, first), grid=(e...]
    unnamed x94 -> x97, local copies, waits for them, and re-layouts: 12.7 us -> 14.5 us
  transfers between devices with their start and end apart: 60 -> 63, of which waited for: 19 -> 20; matrix products, arithmetic and copies ran while one was open for 6% -> 11% of each run, Pallas kernels for 47% -> 53%
where the time goes in v2:
time: 521 us; the launch traced here: 512 us
  Pallas kernels  286 us (55%)
  waiting for transfers between devices  112 us (21%)
  local copies, waits for them, and re-layouts  43.9 us (8%)
  starting transfers between devices  40.4 us (8%)
  other arithmetic  18.4 us (4%)
  matrix products  10.2 us (2%)
    pallas_call x6, Pallas kernels, emb_rows(): pl.pallas_call(functools.partial(rows_kernel, cfg), grid_spec=pltpu.Prefe...  166 us
    ppermute x63, waiting for transfers between devices, swap(): return lax.ppermute(x, axis, [(i, i ^ mask) for i in range(n)])  112 us
    pallas_call x2, Pallas kernels, own_call(): pl.pallas_call(functools.partial(own_kernel, end - begin, first), grid=(e...  75.1 us
    ppermute x63, starting transfers between devices, swap(): return lax.ppermute(x, axis, [(i, i ^ mask) for i in range(n)])  40.4 us
    unnamed x97, local copies, waits for them, and re-layouts  14.5 us
    pallas_call x2, Pallas kernels, copy_rows(): pl.pallas_call(functools.partial(copy_kernel, n), grid_spec=pltpu.Prefetc...  14.4 us
    gather x1, local copies, waits for them, and re-layouts, local_step(): jnp.take(emb_table, jnp.where((lab_local >= 0) & (lab_local < shard_rows)...  11 us
  transfers between devices with their start and end apart: 63, of which 20 were waited for; matrix products, arithmetic and copies ran while one was open for 11% of the time, Pallas kernels for 53%

profile of v2, /device:TPU:0, one launch (start us, length us, event | category | flops | bytes accessed | tf_op | source)
XLA Modules:
  0.0 512.2 jit_solution(854593036098149936)
XLA Ops:
  4.7 9.3 %shard_map.152 = (bf16[640,768]{1,0:T(8,128)(2,1)S(1)}, f32[640,768]{1,0:T(8,128)S(1)}, bf16[640,768]{1,0:T(8,128)(2,1)S(1)}, f32[640,768]{1,0:T(8,128)}) custom-call(bf16[8,512,768]{2,1,0:T(8,128)(2,1)} %hid_ref.1, f32[8,1,128]{2,1,0:T(1,128)S(1)} %bitcast.100, bf16[768,768]{1,0:T(8,128)(2,1)S(1)} %copy-done.7, f32[3,768]{1,0:T(4,128)S(1)} %pad_maximum_fusion.3.vec_ref), custom_call_target="tpu_custom_call" | custom-call | flops 1258291200 | bytes 6291456 | tf_op jit(solution)/shard_map/pallas_call | solution.py:377
  15.9 3.2 collective-permute-start
  19.1 1.5 collective-permute-start.1
  23.2 11.0 %gather_fusion = bf16[640,768]{1,0:T(8,128)(2,1)} fusion(bf16[25152,768]{1,0:T(8,128)(2,1)} %emb_ref.15, s32[1024]{0:T(1024)S(1)} %pad_clamp_fusion), kind=kCustom, calls=%fused_computation | custom fusion | bytes 1968640 | tf_op jit(solution)/shard_map/jit(_take)/gather | solution.py:439
  34.2 46.0 %shard_map.153 = (f32[640,768]{1,0:T(8,128)}, f32[3,640,128]{2,1,0:T(8,128)}) custom-call(bf16[640,768]{1,0:T(8,128)(2,1)} %copy-done, bf16[25152,768]{1,0:T(8,128)(2,1)} %emb_ref.15, f32[11,1,2304]{2,1,0:T(1,128)} %reshape.150.bias_ref, f32[11,1,2304]{2,1,0:T(1,128)} %reshape.151.col_ref, f32[1,640]{1,0:T(1,128)} %convert_element_type.32.lab_row_ref.lab_ref), custom_call_target="tpu_custom_call" | custom-call | flops 7927234560 | bytes 24772608 | tf_op jit(solution)/shard_map/pallas_call | solution.py:416
  80.2 2.2 slice.77
  83.3 2.2 slice.78
  85.5 29.1 %shard_map.154 = (f32[640,768]{1,0:T(8,128)}, f32[8,640]{1,0:T(8,128)}) custom-call(bf16[640,768]{1,0:T(8,128)(2,1)} %copy-done, bf16[25152,768]{1,0:T(8,128)(2,1)} %emb_ref.15, f32[11,1,2304]{2,1,0:T(1,128)} %reshape.150.bias_ref, f32[11,1,2304]{2,1,0:T(1,128)} %reshape.151.col_ref, f32[1,640]{1,0:T(1,128)} %convert_element_type.32.lab_row_ref.lab_ref, ...), custom_call_target="tpu_custom_call" | custom-call | flops 4529848320 | bytes 14155776 | tf_op jit(solution)/shard_map/pallas_call | solution.py:416
  115.7 3.0 collective-permute-done.4.other_ref
  120.8 2.1 collective-permute-done.11.refs_1_
  122.9 1.9 collective-permute-start.12
  128.1 1.9 collective-permute-start.16
  130.5 1.5 copy-done.2
  132.8 1.7 shard_map.156
  136.4 5.9 %fusion.13 = (f32[640]{0:T(1024)S(1)}, f32[640,768]{1,0:T(8,128)}, f32[640,768]{1,0:T(8,128)}) fusion(f32[640,768]{1,0:T(8,128)S(1)} %get-tuple-element.98), kind=kLoop, calls=%fused_computation.95 | loop fusion | flops 31948160 | bytes 5900800 | tf_op jit(solution)/shard_map/jvp()/reduce_sum | solution.py:30
  142.3 2.1 shard_map.158
  144.4 1.5 copy-done.1
  146.0 8.8 %shard_map.157.u_ref = bf16[5120,768]{1,0:T(8,128)(2,1)} custom-call(s32[10]{0:T(128)S(1)} %concatenate.73.start_ref, f32[640,768]{1,0:T(8,128)S(1)} %copy-done.1, f32[640,768]{1,0:T(8,128)} %collective-permute-done.6.refs_1_, f32[640,768]{1,0:T(8,128)} %collective-permute-done.refs_2_, f32[640,768]{1,0:T(8,128)} %collective-permute-done.1.refs_3_, ...), custom_call_target="tpu_custom_call" | custom-call | flops 5000000000 | bytes 23592960 | tf_op jit(solution)/shard_map/pallas_call | solution.py:149
  154.8 27.3 %shard_map.159 = (f32[25152,768]{1,0:T(8,128)}, f32[2,1,640]{2,1,0:T(1,128)S(1)}, f32[624,768]{1,0:T(8,128)}, f32[624,768]{1,0:T(8,128)}) custom-call(s32[4]{0:T(128)S(1)} %pad_add_fusion.3.start_ref, bf16[25152,768]{1,0:T(8,128)(2,1)} %emb_ref.15, f32[32,1,640]{2,1,0:T(1,128)S(1)} %broadcast_in_dim.177.bias_ref, bf16[5120,768]{1,0:T(8,128)(2,1)} %shard_map.157.u_ref, ...), custom_call_target="tpu_custom_call" | custom-call | flops 1226833920 | bytes 9584640 | tf_op jit(solution)/shard_map/pallas_call | solution.py:298
  182.1 1.5 collective-permute-start.22
  184.6 27.5 %shard_map.160 = (f32[25152,768]{1,0:T(8,128)}, f32[2,1,640]{2,1,0:T(1,128)S(1)}, f32[624,768]{1,0:T(8,128)}, f32[624,768]{1,0:T(8,128)}) custom-call(s32[4]{0:T(128)S(1)} %pad_add_fusion.1.start_ref, bf16[25152,768]{1,0:T(8,128)(2,1)} %emb_ref.15, f32[32,1,640]{2,1,0:T(1,128)S(1)} %broadcast_in_dim.177.bias_ref, ...), custom_call_target="tpu_custom_call", output_to_operand_aliasing={{0}: (6, {})} | custom-call | flops 1226833920 | bytes 9584640 | tf_op jit(solution)/shard_map/pallas_call | solution.py:298
  212.2 2.8 multiply_reduce_fusion.1
  216.6 2.6 fusion.12
  219.2 2.1 reduce_sum.69
  226.0 5.5 %collective-permute-done.27 = f32[56,768]{1,0:T(8,128)S(1)} collective-permute-done((f32[56,768]{1,0:T(8,128)S(1)}, f32[56,768]{1,0:T(8,128)S(1)}, u32[]{:S(2)}, u32[]{:S(2)}) %collective-permute-start.27) | collective-permute-done | bytes 172064 | tf_op jit(solution)/shard_map/ppermute | solution.py:355
  234.7 2.8 collective-permute-done.29
  237.5 2.5 collective-permute-done.30
  242.5 26.5 %shard_map.161 = (f32[25152,768]{1,0:T(8,128)}, f32[2,1,640]{2,1,0:T(1,128)S(1)}, f32[624,768]{1,0:T(8,128)}, f32[624,768]{1,0:T(8,128)S(1)}) custom-call(s32[4]{0:T(128)S(1)} %pad_add_fusion.6.start_ref, bf16[25152,768]{1,0:T(8,128)(2,1)} %emb_ref.15, f32[32,1,640]{2,1,0:T(1,128)S(1)} %broadcast_in_dim.177.bias_ref, ...), custom_call_target="tpu_custom_call", output_to_operand_aliasing={{0}: (6, {})} | custom-call | flops 1226833920 | bytes 9584640 | tf_op jit(solution)/shard_map/pallas_call | solution.py:298
  270.3 1.9 collective-permute-start.31
  273.1 27.1 %shard_map.162 = (f32[25152,768]{1,0:T(8,128)}, f32[2,1,640]{2,1,0:T(1,128)S(1)}, f32[624,768]{1,0:T(8,128)S(1)}, f32[624,768]{1,0:T(8,128)S(1)}) custom-call(s32[8]{0:T(128)S(1)} %concatenate.79.start_ref, bf16[25152,768]{1,0:T(8,128)(2,1)} %emb_ref.15, f32[32,1,640]{2,1,0:T(1,128)S(1)} %broadcast_in_dim.177.bias_ref, ...), custom_call_target="tpu_custom_call", output_to_operand_aliasing={{0}: (10, {})} | custom-call | flops 1226833920 | bytes 9584640 | tf_op jit(solution)/shard_map/pallas_call | solution.py:298
  308.8 3.3 collective-permute-done.47
  312.5 2.9 collective-permute-done.48
  318.2 3.8 collective-permute-done.35.refs_3_
  323.0 3.7 collective-permute-done.37.refs_5_
  327.5 6.3 %collective-permute-done.38.refs_6_ = f32[56,768]{1,0:T(8,128)S(1)} collective-permute-done((f32[56,768]{1,0:T(8,128)S(1)}, f32[56,768]{1,0:T(8,128)S(1)}, u32[]{:S(2)}, u32[]{:S(2)}) %collective-permute-start.38) | collective-permute-done | bytes 172064 | tf_op jit(solution)/shard_map/ppermute | solution.py:355
  334.0 6.7 %collective-permute-done.39.refs_7_ = f32[56,768]{1,0:T(8,128)S(1)} collective-permute-done((f32[56,768]{1,0:T(8,128)S(1)}, f32[56,768]{1,0:T(8,128)S(1)}, u32[]{:S(2)}, u32[]{:S(2)}) %collective-permute-start.39) | collective-permute-done | bytes 172064 | tf_op jit(solution)/shard_map/ppermute | solution.py:355
  345.9 38.3 %collective-permute-done.44.refs_6_ = f32[624,768]{1,0:T(8,128)} collective-permute-done((f32[624,768]{1,0:T(8,128)}, f32[624,768]{1,0:T(8,128)}, u32[]{:S(2)}, u32[]{:S(2)}) %collective-permute-start.44) | collective-permute-done | bytes 1916960 | tf_op jit(solution)/shard_map/ppermute | solution.py:355
  387.3 3.3 convolution_convert_fusion.1
  390.6 29.0 %shard_map.163 = (f32[25152,768]{1,0:T(8,128)}, f32[3,1,512]{2,1,0:T(1,128)S(1)}, f32[1296,768]{1,0:T(8,128)}) custom-call(s32[12]{0:T(128)S(1)} %concatenate.84.start_ref, bf16[25152,768]{1,0:T(8,128)(2,1)} %emb_ref.15, f32[12,1,512]{2,1,0:T(1,128)S(1)} %broadcast_in_dim.207.bias_ref, ...), custom_call_target="tpu_custom_call", output_to_operand_aliasing={{0}: (12, {})} | custom-call | flops 1274019840 | bytes 9953280 | tf_op jit(solution)/shard_map/pallas_call | solution.py:298
  419.5 3.2 shard_map.164
  422.8 2.4 slice.99.refs_0_
  425.9 28.5 %shard_map.166 = (f32[25152,768]{1,0:T(8,128)}, f32[3,1,512]{2,1,0:T(1,128)S(1)}, f32[1296,768]{1,0:T(8,128)}) custom-call(s32[14]{0:T(128)S(1)} %concatenate.86.start_ref, bf16[25152,768]{1,0:T(8,128)(2,1)} %emb_ref.15, f32[12,1,512]{2,1,0:T(1,128)S(1)} %broadcast_in_dim.207.bias_ref, ...), custom_call_target="tpu_custom_call", output_to_operand_aliasing={{0}: (14, {})} | custom-call | flops 1274019840 | bytes 9953280 | tf_op jit(solution)/shard_map/pallas_call | solution.py:298
  456.8 4.8 collective-permute-done.62
  461.8 21.3 %collective-permute-done.49.refs_1_ = f32[384,768]{1,0:T(8,128)S(1)} collective-permute-done((f32[384,768]{1,0:T(8,128)}, f32[384,768]{1,0:T(8,128)S(1)}, u32[]{:S(2)}, u32[]{:S(2)}) %collective-permute-start.49) | collective-permute-done | bytes 1179680 | tf_op jit(solution)/shard_map/ppermute | solution.py:355
  487.1 5.8 %convolution_convert_fusion = bf16[8,512,768]{2,1,0:T(8,128)(2,1)} fusion(bf16[8,80,768]{2,1,0:T(8,128)(2,1)} %bitcast.108, s32[8,80]{1,0:T(8,128)S(1)} %pad.23), kind=kOutput, calls=%fused_computation.1 | convolution fusion | flops 506789888 | bytes 7277056 | tf_op jit(solution)/shard_map/clt,cle->cte/dot_general | solution.py:552
  493.7 3.8 shard_map.165
  497.5 8.5 %shard_map.167.refs_3_ = f32[25152,768]{1,0:T(8,128)} custom-call(s32[5]{0:T(128)S(1)} %concatenate.87.start_ref, f32[624,768]{1,0:T(8,128)} %collective-permute-done.59.refs_0_, f32[624,768]{1,0:T(8,128)} %collective-permute-done.60.refs_1_, f32[1296,768]{1,0:T(8,128)} %collective-permute-done.61.refs_2_, ...), custom_call_target="tpu_custom_call", output_to_operand_aliasing={{}: (6, {})} | custom-call | flops 5000000000 | bytes 23298048 | tf_op jit(solution)/shard_map/pallas_call | solution.py:337
  506.1 5.9 %shard_map.168 = f32[25152,768]{1,0:T(8,128)} custom-call(s32[3]{0:T(128)S(1)} %pad_add_fusion.8.start_ref, f32[1296,768]{1,0:T(8,128)} %collective-permute-done.54.refs_0_, f32[624,768]{1,0:T(8,128)S(1)} %collective-permute-done.57.refs_1_, f32[624,768]{1,0:T(8,128)} %collective-permute-done.58.refs_2_, ...), custom_call_target="tpu_custom_call", output_to_operand_aliasing={{}: (4, {})} | custom-call | flops 5000000000 | bytes 15630336 | tf_op jit(solution)/shard_map/pallas_call | solution.py:337
  (293 shorter events, 64.0 us)
Async XLA Ops:
  15.9 64.2 %collective-permute-start = (f32[640,768]{1,0:T(8,128)}, f32[640,768]{1,0:T(8,128)}, u32[]{:S(2)}, u32[]{:S(2)}) collective-permute-start(f32[640,768]{1,0:T(8,128)} %get-tuple-element.99.refs_0_), channel_id=1, source_target_pairs={{0,2},{1,3},{2,0},{3,1},{4,6},{5,7},{6,4},{7,5},{8,10},{9,11},{10,... | collective-permute-start | bytes 5898248 | tf_op jit(solution)/shard_map/ppermute | solution.py:355
  19.1 61.1 %collective-permute-start.1 = (f32[640,768]{1,0:T(8,128)}, f32[640,768]{1,0:T(8,128)}, u32[]{:S(2)}, u32[]{:S(2)}) collective-permute-start(f32[640,768]{1,0:T(8,128)} %get-tuple-element.99.refs_0_), channel_id=1, source_target_pairs={{0,4},{1,5},{2,6},{3,7},{4,0},{5,1},{6,2},{7,3},{8,12},{9,13},{10,... | collective-permute-start | bytes 5898248 | tf_op jit(solution)/shard_map/ppermute | solution.py:355
  20.6 100.1 %collective-permute-start.6 = (f32[640,768]{1,0:T(8,128)}, f32[640,768]{1,0:T(8,128)}, u32[]{:S(2)}, u32[]{:S(2)}) collective-permute-start(f32[640,768]{1,0:T(8,128)} %get-tuple-element.99.refs_0_), channel_id=1, source_target_pairs={{0,1},{1,0},{2,3},{3,2},{4,5},{5,4},{6,7},{7,6},{8,9},{9,8},{10,11... | collective-permute-start | bytes 5898248 | tf_op jit(solution)/shard_map/ppermute | solution.py:355
  82.4 42.5 %collective-permute-start.2 = (f32[320,768]{1,0:T(8,128)}, f32[320,768]{1,0:T(8,128)}, u32[]{:S(2)}, u32[]{:S(2)}) collective-permute-start(f32[320,768]{1,0:T(8,128)} %slice.77), channel_id=1, source_target_pairs={{0,4},{1,5},{2,6},{3,7},{4,0},{5,1},{6,2},{7,3},{8,12},{9,13},{10,... | collective-permute-start | bytes 2949128 | tf_op jit(solution)/shard_map/ppermute | solution.py:355
  85.5 39.4 %collective-permute-start.3 = (f32[320,768]{1,0:T(8,128)}, f32[320,768]{1,0:T(8,128)}, u32[]{:S(2)}, u32[]{:S(2)}) collective-permute-start(f32[320,768]{1,0:T(8,128)} %slice.78), channel_id=1, source_target_pairs={{0,2},{1,3},{2,0},{3,1},{4,6},{5,7},{6,4},{7,5},{8,10},{9,11},{10,... | collective-permute-start | bytes 2949128 | tf_op jit(solution)/shard_map/ppermute | solution.py:355
  115.6 28.8 %collective-permute-start.7 = (f32[640,768]{1,0:T(8,128)}, f32[640,768]{1,0:T(8,128)}, u32[]{:S(2)}, u32[]{:S(2)}) collective-permute-start(f32[640,768]{1,0:T(8,128)} %collective-permute-done.refs_2_), channel_id=1, source_target_pairs={{0,1},{1,0},{2,3},{3,2},{4,5},{5,4},{6,7},{7,6},{8,9},{9,8},{10,11... | collective-permute-start | bytes 5898248 | tf_op jit(solution)/shard_map/ppermute | solution.py:355
  118.6 25.8 %collective-permute-start.8 = (f32[640,768]{1,0:T(8,128)}, f32[640,768]{1,0:T(8,128)}, u32[]{:S(2)}, u32[]{:S(2)}) collective-permute-start(f32[640,768]{1,0:T(8,128)} %collective-permute-done.1.refs_3_), channel_id=1, source_target_pairs={{0,1},{1,0},{2,3},{3,2},{4,5},{5,4},{6,7},{7,6},{8,9},{9,8},{10,11... | collective-permute-start | bytes 5898248 | tf_op jit(solution)/shard_map/ppermute | solution.py:355
  127.1 7.4 %collective-permute-start.15 = (f32[2,640]{1,0:T(2,128)}, f32[2,640]{1,0:T(2,128)S(1)}, u32[]{:S(2)}, u32[]{:S(2)}) collective-permute-start(f32[2,640]{1,0:T(2,128)} %get-tuple-element.113.refs_0_), channel_id=1, source_target_pairs={{0,5},{1,4},{2,7},{3,6},{4,1},{5,0},{6,3},{7,2},{8,13},{9,12},{10,... | collective-permute-start | bytes 15368 | tf_op jit(solution)/shard_map/ppermute | solution.py:355
  128.1 7.1 %collective-permute-start.16 = (f32[2,640]{1,0:T(2,128)}, f32[2,640]{1,0:T(2,128)S(1)}, u32[]{:S(2)}, u32[]{:S(2)}) collective-permute-start(f32[2,640]{1,0:T(2,128)} %get-tuple-element.113.refs_0_), channel_id=1, source_target_pairs={{0,6},{1,7},{2,4},{3,5},{4,2},{5,3},{6,0},{7,1},{8,14},{9,15},{10,... | collective-permute-start | bytes 15368 | tf_op jit(solution)/shard_map/ppermute | solution.py:355
  134.5 9.9 %collective-permute-start.10 = (f32[320,768]{1,0:T(8,128)}, f32[320,768]{1,0:T(8,128)S(1)}, u32[]{:S(2)}, u32[]{:S(2)}) collective-permute-start(f32[320,768]{1,0:T(8,128)} %collective-permute-done.3.refs_7_), channel_id=1, source_target_pairs={{0,1},{1,0},{2,3},{3,2},{4,5},{5,4},{6,7},{7,6},{8,9},{9,8},{10,11... | collective-permute-start | bytes 2949128 | tf_op jit(solution)/shard_map/ppermute | solution.py:355
  135.2 9.2 %collective-permute-start.9 = (f32[320,768]{1,0:T(8,128)}, f32[320,768]{1,0:T(8,128)}, u32[]{:S(2)}, u32[]{:S(2)}) collective-permute-start(f32[320,768]{1,0:T(8,128)} %collective-permute-done.2.refs_6_), channel_id=1, source_target_pairs={{0,1},{1,0},{2,3},{3,2},{4,5},{5,4},{6,7},{7,6},{8,9},{9,8},{10,11... | collective-permute-start | bytes 2949128 | tf_op jit(solution)/shard_map/ppermute | solution.py:355
  135.3 76.9 %collective-permute-start.5 = (f32[640,768]{1,0:T(8,128)}, f32[640,768]{1,0:T(8,128)}, u32[]{:S(2)}, u32[]{:S(2)}) collective-permute-start(f32[640,768]{1,0:T(8,128)} %shard_map.156), channel_id=1, source_target_pairs={{0,8},{8,0},{1,9},{9,1},{2,10},{10,2},{3,11},{11,3},{4,12},{12,4},... | collective-permute-start | bytes 5898248 | tf_op jit(solution)/shard_map/ppermute | solution.py:355
  182.1 58.3 %collective-permute-start.22 = (f32[624,768]{1,0:T(8,128)}, f32[624,768]{1,0:T(8,128)}, u32[]{:S(2)}, u32[]{:S(2)}) collective-permute-start(f32[624,768]{1,0:T(8,128)} %get-tuple-element.122), channel_id=1, source_target_pairs={{0,2},{1,3},{2,0},{3,1},{4,6},{5,7},{6,4},{7,5},{8,10},{9,11},{10,... | collective-permute-start | bytes 5750792 | tf_op jit(solution)/shard_map/ppermute | solution.py:355
  183.6 56.9 %collective-permute-start.23 = (f32[624,768]{1,0:T(8,128)}, f32[624,768]{1,0:T(8,128)}, u32[]{:S(2)}, u32[]{:S(2)}) collective-permute-start(f32[624,768]{1,0:T(8,128)} %get-tuple-element.123), channel_id=1, source_target_pairs={{0,4},{1,5},{2,6},{3,7},{4,0},{5,1},{6,2},{7,3},{8,12},{9,13},{10,... | collective-permute-start | bytes 5750792 | tf_op jit(solution)/shard_map/ppermute | solution.py:355
  212.2 29.1 %collective-permute-start.20 = (f32[624,768]{1,0:T(8,128)}, f32[624,768]{1,0:T(8,128)}, u32[]{:S(2)}, u32[]{:S(2)}) collective-permute-start(f32[624,768]{1,0:T(8,128)} %get-tuple-element.124), channel_id=1, source_target_pairs={{0,1},{1,0},{2,3},{3,2},{4,5},{5,4},{6,7},{7,6},{8,9},{9,8},{10,11... | collective-permute-start | bytes 5750792 | tf_op jit(solution)/shard_map/ppermute | solution.py:355
  224.2 7.2 %collective-permute-start.27 = (f32[56,768]{1,0:T(8,128)S(1)}, f32[56,768]{1,0:T(8,128)S(1)}, u32[]{:S(2)}, u32[]{:S(2)}) collective-permute-start(f32[56,768]{1,0:T(8,128)S(1)} %get-tuple-element.215), channel_id=1, source_target_pairs={{0,2},{1,3},{2,0},{3,1},{4,6},{5,7},{6,4},{7,5},{8,10},{9,11},{10,... | collective-permute-start | bytes 516104 | tf_op jit(solution)/shard_map/ppermute | solution.py:355
  225.3 8.0 %collective-permute-start.28 = (f32[56,768]{1,0:T(8,128)S(1)}, f32[56,768]{1,0:T(8,128)S(1)}, u32[]{:S(2)}, u32[]{:S(2)}) collective-permute-start(f32[56,768]{1,0:T(8,128)S(1)} %get-tuple-element.214), channel_id=1, source_target_pairs={{0,3},{1,2},{2,1},{3,0},{4,7},{5,6},{6,5},{7,4},{8,11},{9,10},{10,... | collective-permute-start | bytes 516104 | tf_op jit(solution)/shard_map/ppermute | solution.py:355
  237.5 32.7 %collective-permute-start.21 = (f32[624,768]{1,0:T(8,128)}, f32[624,768]{1,0:T(8,128)}, u32[]{:S(2)}, u32[]{:S(2)}) collective-permute-start(f32[624,768]{1,0:T(8,128)} %get-tuple-element.125), channel_id=1, source_target_pairs={{0,1},{1,0},{2,3},{3,2},{4,5},{5,4},{6,7},{7,6},{8,9},{9,8},{10,11... | collective-permute-start | bytes 5750792 | tf_op jit(solution)/shard_map/ppermute | solution.py:355
  240.0 30.3 %collective-permute-start.18 = (f32[624,768]{1,0:T(8,128)}, f32[624,768]{1,0:T(8,128)}, u32[]{:S(2)}, u32[]{:S(2)}) collective-permute-start(f32[624,768]{1,0:T(8,128)} %get-tuple-element.122), channel_id=1, source_target_pairs={{0,1},{1,0},{2,3},{3,2},{4,5},{5,4},{6,7},{7,6},{8,9},{9,8},{10,11... | collective-permute-start | bytes 5750792 | tf_op jit(solution)/shard_map/ppermute | solution.py:355
  240.4 31.8 %collective-permute-start.19 = (f32[624,768]{1,0:T(8,128)}, f32[624,768]{1,0:T(8,128)}, u32[]{:S(2)}, u32[]{:S(2)}) collective-permute-start(f32[624,768]{1,0:T(8,128)} %get-tuple-element.123), channel_id=1, source_target_pairs={{0,1},{1,0},{2,3},{3,2},{4,5},{5,4},{6,7},{7,6},{8,9},{9,8},{10,11... | collective-permute-start | bytes 5750792 | tf_op jit(solution)/shard_map/ppermute | solution.py:355
  240.5 62.7 %collective-permute-start.24 = (f32[624,768]{1,0:T(8,128)}, f32[624,768]{1,0:T(8,128)S(1)}, u32[]{:S(2)}, u32[]{:S(2)}) collective-permute-start(f32[624,768]{1,0:T(8,128)} %get-tuple-element.124), channel_id=1, source_target_pairs={{0,2},{1,3},{2,0},{3,1},{4,6},{5,7},{6,4},{7,5},{8,10},{9,11},{10,... | collective-permute-start | bytes 5750792 | tf_op jit(solution)/shard_map/ppermute | solution.py:355
  241.3 61.9 %collective-permute-start.25 = (f32[624,768]{1,0:T(8,128)}, f32[624,768]{1,0:T(8,128)}, u32[]{:S(2)}, u32[]{:S(2)}) collective-permute-start(f32[624,768]{1,0:T(8,128)} %get-tuple-element.125), channel_id=1, source_target_pairs={{0,4},{1,5},{2,6},{3,7},{4,0},{5,1},{6,2},{7,3},{8,12},{9,13},{10,... | collective-permute-start | bytes 5750792 | tf_op jit(solution)/shard_map/ppermute | solution.py:355
  270.2 71.6 %collective-permute-start.40 = (f32[624,768]{1,0:T(8,128)}, f32[624,768]{1,0:T(8,128)}, u32[]{:S(2)}, u32[]{:S(2)}) collective-permute-start(f32[624,768]{1,0:T(8,128)} %get-tuple-element.161), channel_id=1, source_target_pairs={{0,1},{1,0},{2,3},{3,2},{4,5},{5,4},{6,7},{7,6},{8,9},{9,8},{10,11... | collective-permute-start | bytes 5750792 | tf_op jit(solution)/shard_map/ppermute | solution.py:355
  270.3 32.6 %collective-permute-start.31 = (f32[56,768]{1,0:T(8,128)}, f32[56,768]{1,0:T(8,128)}, u32[]{:S(2)}, u32[]{:S(2)}) collective-permute-start(f32[56,768]{1,0:T(8,128)} %get-tuple-element.211), channel_id=1, source_target_pairs={{0,6},{1,7},{2,4},{3,5},{4,2},{5,3},{6,0},{7,1},{8,14},{9,15},{10,... | collective-permute-start | bytes 516104 | tf_op jit(solution)/shard_map/ppermute | solution.py:355
  272.2 31.0 %collective-permute-start.32 = (f32[56,768]{1,0:T(8,128)S(1)}, f32[56,768]{1,0:T(8,128)}, u32[]{:S(2)}, u32[]{:S(2)}) collective-permute-start(f32[56,768]{1,0:T(8,128)S(1)} %get-tuple-element.210), channel_id=1, source_target_pairs={{0,7},{1,6},{2,5},{3,4},{4,3},{5,2},{6,1},{7,0},{8,15},{9,14},{10,... | collective-permute-start | bytes 516104 | tf_op jit(solution)/shard_map/ppermute | solution.py:355
  302.9 39.8 %collective-permute-start.41 = (f32[624,768]{1,0:T(8,128)}, f32[624,768]{1,0:T(8,128)S(1)}, u32[]{:S(2)}, u32[]{:S(2)}) collective-permute-start(f32[624,768]{1,0:T(8,128)} %copy-done.14), channel_id=1, source_target_pairs={{0,1},{1,0},{2,3},{3,2},{4,5},{5,4},{6,7},{7,6},{8,9},{9,8},{10,11... | collective-permute-start | bytes 5750792 | tf_op jit(solution)/shard_map/ppermute | solution.py:355
  304.7 11.0 %collective-permute-start.33 = (f32[56,768]{1,0:T(8,128)S(1)}, f32[56,768]{1,0:T(8,128)S(1)}, u32[]{:S(2)}, u32[]{:S(2)}) collective-permute-start(f32[56,768]{1,0:T(8,128)S(1)} %fusion.9.refs_0_), channel_id=1, source_target_pairs={{0,1},{1,0},{2,3},{3,2},{4,5},{5,4},{6,7},{7,6},{8,9},{9,8},{10,11... | collective-permute-start | bytes 516104 | tf_op jit(solution)/shard_map/ppermute | solution.py:355
  305.0 11.7 %collective-permute-start.34 = (f32[56,768]{1,0:T(8,128)S(1)}, f32[56,768]{1,0:T(8,128)S(1)}, u32[]{:S(2)}, u32[]{:S(2)}) collective-permute-start(f32[56,768]{1,0:T(8,128)S(1)} %fusion.9.refs_0_), channel_id=1, source_target_pairs={{0,2},{1,3},{2,0},{3,1},{4,6},{5,7},{6,4},{7,5},{8,10},{9,11},{10,... | collective-permute-start | bytes 516104 | tf_op jit(solution)/shard_map/ppermute | solution.py:355
  315.7 7.1 %collective-permute-start.36 = (f32[56,768]{1,0:T(8,128)S(1)}, f32[56,768]{1,0:T(8,128)S(1)}, u32[]{:S(2)}, u32[]{:S(2)}) collective-permute-start(f32[56,768]{1,0:T(8,128)S(1)} %fusion.9.refs_0_), channel_id=1, source_target_pairs={{0,4},{1,5},{2,6},{3,7},{4,0},{5,1},{6,2},{7,3},{8,12},{9,13},{10,... | collective-permute-start | bytes 516104 | tf_op jit(solution)/shard_map/ppermute | solution.py:355
  316.7 10.0 %collective-permute-start.37 = (f32[56,768]{1,0:T(8,128)S(1)}, f32[56,768]{1,0:T(8,128)S(1)}, u32[]{:S(2)}, u32[]{:S(2)}) collective-permute-start(f32[56,768]{1,0:T(8,128)S(1)} %fusion.9.refs_0_), channel_id=1, source_target_pairs={{0,5},{1,4},{2,7},{3,6},{4,1},{5,0},{6,3},{7,2},{8,13},{9,12},{10,... | collective-permute-start | bytes 516104 | tf_op jit(solution)/shard_map/ppermute | solution.py:355
  321.9 22.1 %collective-permute-start.42 = (f32[624,768]{1,0:T(8,128)}, f32[624,768]{1,0:T(8,128)S(1)}, u32[]{:S(2)}, u32[]{:S(2)}) collective-permute-start(f32[624,768]{1,0:T(8,128)} %collective-permute-done.22.refs_2_), channel_id=1, source_target_pairs={{0,1},{1,0},{2,3},{3,2},{4,5},{5,4},{6,7},{7,6},{8,9},{9,8},{10,11... | collective-permute-start | bytes 5750792 | tf_op jit(solution)/shard_map/ppermute | solution.py:355
  322.9 22.9 %collective-permute-start.43 = (f32[624,768]{1,0:T(8,128)}, f32[624,768]{1,0:T(8,128)}, u32[]{:S(2)}, u32[]{:S(2)}) collective-permute-start(f32[624,768]{1,0:T(8,128)} %collective-permute-done.23.refs_3_), channel_id=1, source_target_pairs={{0,1},{1,0},{2,3},{3,2},{4,5},{5,4},{6,7},{7,6},{8,9},{9,8},{10,11... | collective-permute-start | bytes 5750792 | tf_op jit(solution)/shard_map/ppermute | solution.py:355
  326.7 7.2 %collective-permute-start.38 = (f32[56,768]{1,0:T(8,128)S(1)}, f32[56,768]{1,0:T(8,128)S(1)}, u32[]{:S(2)}, u32[]{:S(2)}) collective-permute-start(f32[56,768]{1,0:T(8,128)S(1)} %fusion.9.refs_0_), channel_id=1, source_target_pairs={{0,6},{1,7},{2,4},{3,5},{4,2},{5,3},{6,0},{7,1},{8,14},{9,15},{10,... | collective-permute-start | bytes 516104 | tf_op jit(solution)/shard_map/ppermute | solution.py:355
  340.7 43.4 %collective-permute-start.44 = (f32[624,768]{1,0:T(8,128)}, f32[624,768]{1,0:T(8,128)}, u32[]{:S(2)}, u32[]{:S(2)}) collective-permute-start(f32[624,768]{1,0:T(8,128)} %get-tuple-element.161), channel_id=1, source_target_pairs={{0,2},{1,3},{2,0},{3,1},{4,6},{5,7},{6,4},{7,5},{8,10},{9,11},{10,... | collective-permute-start | bytes 5750792 | tf_op jit(solution)/shard_map/ppermute | solution.py:355
  341.8 43.5 %collective-permute-start.45 = (f32[624,768]{1,0:T(8,128)}, f32[624,768]{1,0:T(8,128)}, u32[]{:S(2)}, u32[]{:S(2)}) collective-permute-start(f32[624,768]{1,0:T(8,128)} %copy-done.14), channel_id=1, source_target_pairs={{0,4},{1,5},{2,6},{3,7},{4,0},{5,1},{6,2},{7,3},{8,12},{9,13},{10,... | collective-permute-start | bytes 5750792 | tf_op jit(solution)/shard_map/ppermute | solution.py:355
  344.0 42.3 %collective-permute-start.52 = (f32[624,768]{1,0:T(8,128)S(1)}, f32[624,768]{1,0:T(8,128)}, u32[]{:S(2)}, u32[]{:S(2)}) collective-permute-start(f32[624,768]{1,0:T(8,128)S(1)} %collective-permute-done.24.refs_2_), channel_id=1, source_target_pairs={{0,1},{1,0},{2,3},{3,2},{4,5},{5,4},{6,7},{7,6},{8,9},{9,8},{10,11... | collective-permute-start | bytes 5750792 | tf_op jit(solution)/shard_map/ppermute | solution.py:355
  345.3 79.9 %collective-permute-start.53 = (f32[624,768]{1,0:T(8,128)}, f32[624,768]{1,0:T(8,128)}, u32[]{:S(2)}, u32[]{:S(2)}) collective-permute-start(f32[624,768]{1,0:T(8,128)} %collective-permute-done.25.refs_3_), channel_id=1, source_target_pairs={{0,1},{1,0},{2,3},{3,2},{4,5},{5,4},{6,7},{7,6},{8,9},{9,8},{10,11... | collective-permute-start | bytes 5750792 | tf_op jit(solution)/shard_map/ppermute | solution.py:355
  345.8 79.3 %collective-permute-start.50 = (f32[624,768]{1,0:T(8,128)}, f32[624,768]{1,0:T(8,128)}, u32[]{:S(2)}, u32[]{:S(2)}) collective-permute-start(f32[624,768]{1,0:T(8,128)} %copy-done.13), channel_id=1, source_target_pairs={{0,1},{1,0},{2,3},{3,2},{4,5},{5,4},{6,7},{7,6},{8,9},{9,8},{10,11... | collective-permute-start | bytes 5750792 | tf_op jit(solution)/shard_map/ppermute | solution.py:355
  384.2 41.7 %collective-permute-start.51 = (f32[624,768]{1,0:T(8,128)}, f32[624,768]{1,0:T(8,128)}, u32[]{:S(2)}, u32[]{:S(2)}) collective-permute-start(f32[624,768]{1,0:T(8,128)} %copy-done.12), channel_id=1, source_target_pairs={{0,1},{1,0},{2,3},{3,2},{4,5},{5,4},{6,7},{7,6},{8,9},{9,8},{10,11... | collective-permute-start | bytes 5750792 | tf_op jit(solution)/shard_map/ppermute | solution.py:355
  385.4 69.1 %collective-permute-start.55 = (f32[624,768]{1,0:T(8,128)}, f32[624,768]{1,0:T(8,128)}, u32[]{:S(2)}, u32[]{:S(2)}) collective-permute-start(f32[624,768]{1,0:T(8,128)} %copy-done.13), channel_id=1, source_target_pairs={{0,2},{1,3},{2,0},{3,1},{4,6},{5,7},{6,4},{7,5},{8,10},{9,11},{10,... | collective-permute-start | bytes 5750792 | tf_op jit(solution)/shard_map/ppermute | solution.py:355
  386.3 70.2 %collective-permute-start.56 = (f32[624,768]{1,0:T(8,128)}, f32[624,768]{1,0:T(8,128)}, u32[]{:S(2)}, u32[]{:S(2)}) collective-permute-start(f32[624,768]{1,0:T(8,128)} %copy-done.12), channel_id=1, source_target_pairs={{0,4},{1,5},{2,6},{3,7},{4,0},{5,1},{6,2},{7,3},{8,12},{9,13},{10,... | collective-permute-start | bytes 5750792 | tf_op jit(solution)/shard_map/ppermute | solution.py:355
  425.1 57.9 %collective-permute-start.59 = (f32[624,768]{1,0:T(8,128)}, f32[624,768]{1,0:T(8,128)}, u32[]{:S(2)}, u32[]{:S(2)}) collective-permute-start(f32[624,768]{1,0:T(8,128)} %collective-permute-done.44.refs_6_), channel_id=1, source_target_pairs={{0,1},{1,0},{2,3},{3,2},{4,5},{5,4},{6,7},{7,6},{8,9},{9,8},{10,11... | collective-permute-start | bytes 5750792 | tf_op jit(solution)/shard_map/ppermute | solution.py:355
  425.2 72.4 %collective-permute-start.61 = (f32[1296,768]{1,0:T(8,128)}, f32[1296,768]{1,0:T(8,128)}, u32[]{:S(2)}, u32[]{:S(2)}) collective-permute-start(f32[1296,768]{1,0:T(8,128)} %get-tuple-element.178), channel_id=1, source_target_pairs={{0,1},{1,0},{2,3},{3,2},{4,5},{5,4},{6,7},{7,6},{8,9},{9,8},{10,11... | collective-permute-start | bytes 11943944 | tf_op jit(solution)/shard_map/ppermute | solution.py:355
  454.4 51.6 %collective-permute-start.54 = (f32[1296,768]{1,0:T(8,128)}, f32[1296,768]{1,0:T(8,128)}, u32[]{:S(2)}, u32[]{:S(2)}) collective-permute-start(f32[1296,768]{1,0:T(8,128)} %get-tuple-element.172), channel_id=1, source_target_pairs={{0,1},{1,0},{2,3},{3,2},{4,5},{5,4},{6,7},{7,6},{8,9},{9,8},{10,11... | collective-permute-start | bytes 11943944 | tf_op jit(solution)/shard_map/ppermute | solution.py:355
  454.5 28.6 %collective-permute-start.49 = (f32[384,768]{1,0:T(8,128)}, f32[384,768]{1,0:T(8,128)S(1)}, u32[]{:S(2)}, u32[]{:S(2)}) collective-permute-start(f32[384,768]{1,0:T(8,128)} %slice.99.refs_0_), channel_id=1, source_target_pairs={{0,8},{8,0},{1,9},{9,1},{2,10},{10,2},{3,11},{11,3},{4,12},{12,4},... | collective-permute-start | bytes 3538952 | tf_op jit(solution)/shard_map/ppermute | solution.py:355
  461.7 35.9 %collective-permute-start.60 = (f32[624,768]{1,0:T(8,128)}, f32[624,768]{1,0:T(8,128)}, u32[]{:S(2)}, u32[]{:S(2)}) collective-permute-start(f32[624,768]{1,0:T(8,128)} %collective-permute-done.45.refs_7_), channel_id=1, source_target_pairs={{0,1},{1,0},{2,3},{3,2},{4,5},{5,4},{6,7},{7,6},{8,9},{9,8},{10,11... | collective-permute-start | bytes 5750792 | tf_op jit(solution)/shard_map/ppermute | solution.py:355
  483.1 23.0 %collective-permute-start.57 = (f32[624,768]{1,0:T(8,128)}, f32[624,768]{1,0:T(8,128)S(1)}, u32[]{:S(2)}, u32[]{:S(2)}) collective-permute-start(f32[624,768]{1,0:T(8,128)} %collective-permute-done.55.refs_3_), channel_id=1, source_target_pairs={{0,1},{1,0},{2,3},{3,2},{4,5},{5,4},{6,7},{7,6},{8,9},{9,8},{10,11... | collective-permute-start | bytes 5750792 | tf_op jit(solution)/shard_map/ppermute | solution.py:355
  483.1 23.0 %collective-permute-start.58 = (f32[624,768]{1,0:T(8,128)}, f32[624,768]{1,0:T(8,128)}, u32[]{:S(2)}, u32[]{:S(2)}) collective-permute-start(f32[624,768]{1,0:T(8,128)} %collective-permute-done.56.refs_4_), channel_id=1, source_target_pairs={{0,1},{1,0},{2,3},{3,2},{4,5},{5,4},{6,7},{7,6},{8,9},{9,8},{10,11... | collective-permute-start | bytes 5750792 | tf_op jit(solution)/shard_map/ppermute | solution.py:355
  (65 other events, 725.5 us)

commit v3 on v2

--- a/solution.py
+++ b/solution.py
@@ -1,4 +1,5 @@
 import functools
+import math
 
 import jax
 import jax.numpy as jnp
@@ -22,15 +23,60 @@
 VMEM_ROWS = 44
 COST_SCALE = 4
 OFF = 1e30
-MIB = 2 ** 20
-
-
-def head_norm(pre_act, ln_gain, ln_bias):
-    gelu_out = jax.nn.gelu(pre_act, approximate=False)
-    row_mean = jnp.mean(gelu_out, axis=-1, keepdims=True)
-    centered = gelu_out - row_mean
-    row_var = jnp.mean(centered * centered, axis=-1, keepdims=True)
-    return centered * lax.rsqrt(row_var + LN_EPS) * ln_gain + ln_bias
+SHORT = 10 ** 9
+MIB, LANES, UNIT = 2 ** 20, 128, 16
+SQRT_HALF, GAUSS = 0.5 ** 0.5, (2.0 * math.pi) ** -0.5
+
+
+ANY_SPACE = pl.BlockSpec(memory_space=pl.ANY)
+
+
+def fixed(shape):
+    return pl.BlockSpec(shape, lambda *_: (0,) * len(shape))
+
+
+def stepped(shape, base=0):
+    return pl.BlockSpec(shape, lambda i, *_: (i + base,) + (0,) * (len(shape) - 1))
+
+
+def row(x, k):
+    return x[k:k + 1, :]
+
+
+def lanes_of(x, k):
+    return x[:, k * LANES:(k + 1) * LANES]
+
+
+def fold(x):
+    return functools.reduce(jnp.add, [lanes_of(x, k) for k in range(x.shape[1] // LANES)])
+
+
+def wide(x, n):
+    return jnp.concatenate([x] * (n // LANES), axis=1)
+
+
+def row_sum(x):
+    return jnp.sum(x, axis=1, keepdims=True)
+
+
+def col_sum(x):
+    return jnp.sum(x, axis=0, keepdims=True)
+
+
+def row_mean(x):
+    return jnp.mean(x, axis=1, keepdims=True)
+
+
+def units(start, size):
+    return pl.ds(pl.multiple_of(start * UNIT, UNIT), size)
+
+
+def vmem_mib(n):
+    return pltpu.CompilerParams(vmem_limit_bytes=n * MIB)
+
+
+def cost(flops, bytes_accessed, transcendentals=0):
+    return pl.CostEstimate(flops=flops, bytes_accessed=bytes_accessed, transcendentals=transcendentals)
 
 
 def dot_nt(a, b):
@@ -51,14 +97,40 @@
 
     @pl.when(step == n_steps - 1)
     def _():
-        pre = jnp.dot(z_ref[...], w_ref[...], preferred_element_type=F32) + vec_ref[0:1, :]
+        pre = jnp.dot(z_ref[...], w_ref[...], preferred_element_type=F32) + row(vec_ref, 0)
         pre_ref[...] = pre
-        act = 0.5 * pre * (1.0 + lax.erf(pre * 0.7071067811865476))
-        cen = act - jnp.mean(act, axis=1, keepdims=True)
-        var = jnp.mean(cen * cen, axis=1, keepdims=True)
-        u = (cen * lax.rsqrt(var + LN_EPS) * vec_ref[1:2, :] + vec_ref[2:3, :]).astype(BF16)
+        act = 0.5 * pre * (1.0 + lax.erf(pre * SQRT_HALF))
+        cen = act - row_mean(act)
+        var = row_mean(cen * cen)
+        u = (cen * lax.rsqrt(var + LN_EPS) * row(vec_ref, 1) + row(vec_ref, 2)).astype(BF16)
         u_ref[...] = u
         uf_ref[...] = u.astype(F32)
+
+
+def head_kernel(n_pieces, where_ref, pre_ref, mine_ref, other_ref, z_ref, w_ref, vec_ref, loss_ref, *refs):
+    pieces, dz_ref, sum_ref = refs[:n_pieces], refs[n_pieces], refs[-1]
+    pre = pre_ref[...]
+    cdf = 0.5 * (1.0 + lax.erf(pre * SQRT_HALF))
+    act = pre * cdf
+    cen = act - row_mean(act)
+    rstd = lax.rsqrt(row_mean(cen * cen) + LN_EPS)
+    unit = cen * rstd
+    du = mine_ref[...] + other_ref[...]
+    dunit = du * row(vec_ref, 1)
+    dact = rstd * (dunit - row_mean(dunit) - unit * row_mean(dunit * unit))
+    dpre = dact * (cdf + pre * (jnp.exp(-0.5 * pre * pre) * GAUSS))
+    dab = dpre.astype(BF16)
+    dz_ref[...] = dot_nt(dab, w_ref[...]).astype(BF16)
+    half = z_ref.shape[1] // 2
+    z_half = z_ref[:, pl.ds(pl.multiple_of(where_ref[n_pieces] * half, 128), half)]
+    sum_ref[...] = jnp.zeros_like(sum_ref)
+    sum_ref[:half, :] = lax.dot_general(z_half, dab, (((0,), (0,)), ((), ())), preferred_element_type=F32)
+    rows = [col_sum(dpre), col_sum(du * unit), col_sum(du), loss_ref[...]]
+    for k, value in enumerate(rows):
+        sum_ref[half + k:half + k + 1, :] = value
+    size = sum_ref.shape[0] // n_pieces
+    for k in range(n_pieces):
+        pieces[k][...] = sum_ref[pl.ds(pl.multiple_of(where_ref[k] * size, 8), size), :]
 
 
 def own_kernel(n_steps, first, u_ref, emb_ref, bias_ref, col_ref, lab_row_ref, *refs):
@@ -75,11 +147,10 @@
             t_ref[...] = jnp.zeros_like(t_ref)
             acc_ref[...] = jnp.zeros_like(acc_ref)
         else:
-            m_ref[...], s_ref[...], t_ref[...] = state_in[0], state_in[1], state_in[2]
+            for k, ref in enumerate((m_ref, s_ref, t_ref)):
+                ref[...] = state_in[k]
             acc_ref[...] = acc_in[...]
 
-    wide = lambda x, n: jnp.concatenate([x] * (n // 128), axis=1)
-    fold = lambda x: functools.reduce(jnp.add, [x[:, k * 128:(k + 1) * 128] for k in range(CHUNK // 128)])
     logit = lambda q: dot_nt(u_ref[...], emb_ref[q * CHUNK:(q + 1) * CHUNK, :]) + bias_ref[0, :, q * CHUNK:(q + 1) * CHUNK]
     following = logit(0)
     for q in range(VT // CHUNK):
@@ -103,8 +174,8 @@
             for k, ref in enumerate((m_ref, s_ref, t_ref)):
                 stat_ref[k] = ref[...]
             return
-        mass = jnp.sum(s_ref[...], axis=1, keepdims=True)
-        target = jnp.sum(t_ref[...], axis=1, keepdims=True)
+        mass = row_sum(s_ref[...])
+        target = row_sum(t_ref[...])
         lane = lax.broadcasted_iota(I32, m_ref.shape, 1)
         stat_ref[...] = jnp.where(lane == 0, m_ref[...], jnp.where(lane == 1, mass, target)).T[:8]
 
@@ -113,24 +184,24 @@
     low = plane_ref[0] == 0
     mine, other = mine_ref[...], other_ref[...]
     lo, hi = jnp.where(low, mine, other), jnp.where(low, other, mine)
-    top = jnp.maximum(lo[0:1], hi[0:1])
-    log_norm = top + jnp.log(lo[1:2] * jnp.exp(lo[0:1] - top) + hi[1:2] * jnp.exp(hi[0:1] - top))
+    top = jnp.maximum(row(lo, 0), row(hi, 0))
+    log_norm = top + jnp.log(row(lo, 1) * jnp.exp(row(lo, 0) - top) + row(hi, 1) * jnp.exp(row(hi, 0) - top))
     valid = lax.rem(lax.broadcasted_iota(I32, log_norm.shape, 1), SLOTS) < n_masks
     norm = jnp.where(valid, log_norm, OFF)
     lab = lab_ref[...]
     tok_ref[0:1, :] = norm
     tok_ref[1:2, :] = lab
     here = (lab >= 0.0) & (lab < shard_rows)
-    coef_ref[0:1, :] = jnp.exp(mine[0:1] - norm) * inv_n
-    coef_ref[1:2, :] = jnp.where(here, (jnp.exp(mine[2:3] - norm) - 1.0) * inv_n, 0.0)
-    loss = jnp.sum(jnp.where(valid, log_norm - (lo[2:3] + hi[2:3]), 0.0), axis=1, keepdims=True) * inv_n
+    coef_ref[0:1, :] = jnp.exp(row(mine, 0) - norm) * inv_n
+    coef_ref[1:2, :] = jnp.where(here, (jnp.exp(row(mine, 2) - norm) - 1.0) * inv_n, 0.0)
+    loss = jnp.sum(jnp.where(valid, log_norm - (row(lo, 2) + row(hi, 2)), 0.0), axis=1, keepdims=True) * inv_n
     loss_ref[...] = jnp.broadcast_to(loss, loss_ref.shape)
 
 
 def du_kernel(acc_ref, row_ref, coef_ref, du_ref):
-    wide = lambda x: jnp.concatenate([x] * (acc_ref.shape[1] // 128), axis=1)
-    hot = to_lanes(coef_ref[1:2, :]).astype(BF16).astype(F32)
-    du = acc_ref[...] * wide(to_lanes(coef_ref[0:1, :])) + row_ref[...].astype(F32) * wide(hot)
+    width = acc_ref.shape[1]
+    hot = to_lanes(row(coef_ref, 1)).astype(BF16).astype(F32)
+    du = acc_ref[...] * wide(to_lanes(row(coef_ref, 0)), width) + row_ref[...].astype(F32) * wide(hot, width)
     du_ref[...] = du.astype(BF16).astype(F32)
 
 
@@ -141,7 +212,7 @@
         load.start()
     for k in range(n):
         loads[k].wait()
-        out_ref[pl.ds(pl.multiple_of(start_ref[k] * 16, 16), pieces[k].shape[0]), :] = bufs[k][...].astype(BF16)
+        out_ref[units(start_ref[k], pieces[k].shape[0]), :] = bufs[k][...].astype(BF16)
 
 
 def place(pieces, starts, n_all):
@@ -151,21 +222,21 @@
         grid_spec=pltpu.PrefetchScalarGridSpec(
             num_scalar_prefetch=1,
             grid=(1,),
-            in_specs=[pl.BlockSpec(memory_space=pl.ANY)] * n,
+            in_specs=[ANY_SPACE] * n,
             out_specs=pl.BlockSpec(memory_space=pltpu.VMEM),
             scratch_shapes=[pltpu.VMEM(p.shape, F32) for p in pieces] + [pltpu.SemaphoreType.DMA((n,))],
         ),
         out_shape=jax.ShapeDtypeStruct((n_all, width), BF16),
-        compiler_params=pltpu.CompilerParams(vmem_limit_bytes=40 * MIB),
-        cost_estimate=pl.CostEstimate(flops=5 * 10 ** 9, bytes_accessed=6 * n_all * width, transcendentals=0),
+        compiler_params=vmem_mib(40),
+        cost_estimate=cost(SHORT, 6 * n_all * width),
     )(starts, *pieces)
 
 
 def tok_kernel(n, start_ref, *refs):
     for k in range(n):
-        row = pl.ds(start_ref[k], 1)
-        refs[n][row, :] = refs[k][0:1, :]
-        refs[n + 1][row, :] = refs[k][1:2, :]
+        place_at = pl.ds(start_ref[k], 1)
+        refs[n][place_at, :] = row(refs[k], 0)
+        refs[n + 1][place_at, :] = row(refs[k], 1)
 
 
 def place_toks(toks, ranks):
@@ -175,8 +246,8 @@
         grid_spec=pltpu.PrefetchScalarGridSpec(
             num_scalar_prefetch=1,
             grid=(1,),
-            in_specs=[pl.BlockSpec(t.shape, lambda i, s: (0, 0)) for t in toks],
-            out_specs=[pl.BlockSpec((n, width), lambda i, s: (0, 0))] * 2,
+            in_specs=[fixed(t.shape) for t in toks],
+            out_specs=[fixed((n, width))] * 2,
         ),
         out_shape=[jax.ShapeDtypeStruct((n, width), F32)] * 2,
     )(ranks, *toks)
@@ -195,19 +266,46 @@
         grid_spec=pltpu.PrefetchScalarGridSpec(
             num_scalar_prefetch=1,
             grid=(1,),
-            in_specs=[pl.BlockSpec(p.shape, lambda i, s: (0, 0)) for p in pieces],
-            out_specs=pl.BlockSpec(shape, lambda i, s: (0, 0, 0)),
+            in_specs=[fixed(p.shape) for p in pieces],
+            out_specs=fixed(shape),
         ),
         out_shape=jax.ShapeDtypeStruct(shape, F32),
     )(ranks, *pieces)
 
 
+def join_kernel(n, start_ref, *refs):
+    head, rest, buf = refs[n:]
+    size = refs[0].shape[0]
+    for k in range(n):
+        buf[pl.ds(pl.multiple_of(start_ref[k] * size, 8), size), :] = refs[k][...]
+    cut = head.shape[0]
+    head[...] = buf[:cut, :]
+    rest[...] = buf[cut:, :]
+
+
+def join_pieces(pieces, ranks, cut):
+    n, (size, width) = len(pieces), pieces[0].shape
+    shapes = [(cut, width), (n * size - cut, width)]
+    return pl.pallas_call(
+        functools.partial(join_kernel, n),
+        grid_spec=pltpu.PrefetchScalarGridSpec(
+            num_scalar_prefetch=1,
+            grid=(1,),
+            in_specs=[fixed(p.shape) for p in pieces],
+            out_specs=[fixed(shape) for shape in shapes],
+            scratch_shapes=[pltpu.VMEM((n * size, width), F32)],
+        ),
+        out_shape=[jax.ShapeDtypeStruct(shape, F32) for shape in shapes],
+    )(ranks, *pieces)
+
+
 def rows_kernel(cfg, start_ref, emb_ref, bias_ref, u_ref, norm_ref, lab_ref, *refs):
     n_steps, tile, inv_n, n_send, n_copy, aliased = cfg
     arrived, refs = refs[:n_copy], refs[n_copy + (1 if aliased else 0):]
-    out_ref, db_ref, sends, refs = refs[0], refs[1], refs[2:2 + n_send], refs[2 + n_send:]
+    out_ref, db_ref, *refs = refs
+    sends, refs = refs[:n_send], refs[n_send:]
     acc_ref, out_sem, send_sem = refs[:3]
-    stage, load_sem, store_sem = (refs[3:3 + n_copy], refs[3 + n_copy], refs[4 + n_copy]) if n_copy else ((), None, None)
+    stage, (load_sem, store_sem) = (refs[3:-2], refs[-2:]) if n_copy else ((), (None, None))
     step = pl.program_id(0)
     slot = lax.rem(step, 2)
     n_tok = u_ref.shape[0]
@@ -216,7 +314,7 @@
         return pltpu.make_async_copy(arrived[k], stage[k], load_sem.at[k])
 
     def store(k):
-        rows = pl.ds(pl.multiple_of(start_ref[2 * n_steps + k] * 16, 16), arrived[k].shape[0])
+        rows = units(start_ref[2 * n_steps + k], arrived[k].shape[0])
         return pltpu.make_async_copy(stage[k], out_ref.at[rows, :], store_sem.at[k])
 
     @pl.when(step == 0)
@@ -231,7 +329,7 @@
             store(k).start()
 
     def out_copy(t, which):
-        rows = pl.ds(pl.multiple_of(start_ref[t] * 16, 16), tile)
+        rows = units(start_ref[t], tile)
         return pltpu.make_async_copy(acc_ref.at[which], out_ref.at[rows, :], out_sem.at[which])
 
     def send_copy(t, which):
@@ -245,25 +343,24 @@
         pltpu.make_async_copy(acc_ref.at[slot], sends[0].at[pl.ds(0, tile), :], send_sem.at[slot]).wait()
 
     row_id = lax.broadcasted_iota(I32, (tile, 1), 0).astype(F32) + (start_ref[step] * 16).astype(F32)
-    bias = jnp.concatenate([to_lanes(bias_ref[0])[:tile]] * (TOK_CHUNK // 128), axis=1)
+    bias = wide(to_lanes(bias_ref[0])[:tile], TOK_CHUNK)
     per = TOK_CHUNK // norm_ref.shape[1]
     for j in range(n_tok // TOK_CHUNK):
         s = slice(j * TOK_CHUNK, (j + 1) * TOK_CHUNK)
-        norm = jnp.concatenate([norm_ref[i:i + 1, :] for i in range(j * per, (j + 1) * per)], axis=1)
-        lab = jnp.concatenate([lab_ref[i:i + 1, :] for i in range(j * per, (j + 1) * per)], axis=1)
+        norm = jnp.concatenate([row(norm_ref, i) for i in range(j * per, (j + 1) * per)], axis=1)
+        lab = jnp.concatenate([row(lab_ref, i) for i in range(j * per, (j + 1) * per)], axis=1)
         logit = dot_nt(emb_ref[...], u_ref[s, :]) + bias
         prob = jnp.exp(logit - norm)
         grad = (prob - jnp.where(lab == row_id, 1.0, 0.0)) * inv_n
         part = jnp.dot(grad.astype(BF16), u_ref[s, :], preferred_element_type=F32)
-        lanes = functools.reduce(jnp.add, [grad[:, k * 128:(k + 1) * 128] for k in range(TOK_CHUNK // 128)])
-        db = lanes if j == 0 else db + lanes
+        db = fold(grad) if j == 0 else db + fold(grad)
         if j == 0:
             acc_ref[slot] = part
         else:
             acc_ref[slot] += part
 
     db = jnp.concatenate([db, jnp.zeros((db_ref.shape[2] - tile, 128), F32)])
-    db_ref[0] = jnp.sum(db.T, axis=0, keepdims=True)
+    db_ref[0] = col_sum(db.T)
     out_copy(step, slot).start()
     if n_send == 1:
         send_copy(step, slot).start()
@@ -289,8 +386,8 @@
     aliased = out is not None
     cfg = (n_steps, tile, inv_n, n_send, n_copy, aliased)
     table = jnp.concatenate([starts, blocks] + list(copy_starts)).astype(I32)
-    any_space = pl.BlockSpec(memory_space=pl.ANY)
-    whole = lambda a: pl.BlockSpec(a.shape, lambda i, s: (0, 0))
+    any_space = ANY_SPACE
+    whole = lambda a: fixed(a.shape)
     send_rows = n_steps * tile if n_send == 1 else tile
     scratch = [pltpu.VMEM((2, tile, width), F32), pltpu.SemaphoreType.DMA((2,)), pltpu.SemaphoreType.DMA((2,))]
     if n_copy:
@@ -305,12 +402,12 @@
                 pl.BlockSpec((1, 1, bias.shape[2]), lambda i, s: (s[n_steps + i], 0, 0)),
                 pl.BlockSpec(memory_space=pltpu.VMEM), whole(norm), whole(lab),
             ] + [any_space] * (n_copy + aliased),
-            out_specs=[any_space, pl.BlockSpec((1, 1, bias.shape[2]), lambda i, s: (i, 0, 0))] + [any_space] * n_send,
+            out_specs=[any_space, stepped((1, 1, bias.shape[2]))] + [any_space] * n_send,
             scratch_shapes=scratch,
         ),
         out_shape=[jax.ShapeDtypeStruct((n_rows, width), F32), jax.ShapeDtypeStruct((n_steps, 1, bias.shape[2]), F32)] + [jax.ShapeDtypeStruct((send_rows, width), F32)] * n_send,
         input_output_aliases={6 + n_copy: 0} if aliased else {},
-        compiler_params=pltpu.CompilerParams(vmem_limit_bytes=VMEM_ROWS * MIB),
+        compiler_params=vmem_mib(VMEM_ROWS),
         cost_estimate=pl.CostEstimate(
             flops=n_steps * tile * n_tok * width // COST_SCALE, bytes_accessed=n_steps * tile * width * 10, transcendentals=n_steps * tile * n_tok
         ),
@@ -318,14 +415,14 @@
 
 
 def copy_kernel(n, start_ref, *refs):
-    arrived, out_ref, stage, load_sem, store_sem = refs[:n], refs[n + 1], refs[n + 2:-2], refs[-2], refs[-1]
+    arrived, (_, out_ref, *stage, load_sem, store_sem) = refs[:n], refs[n:]
     loads = [pltpu.make_async_copy(arrived[k], stage[k], load_sem.at[k]) for k in range(n)]
     for load in loads:
         load.start()
     stores = []
     for k in range(n):
         loads[k].wait()
-        rows = pl.ds(pl.multiple_of(start_ref[k] * 16, 16), arrived[k].shape[0])
+        rows = units(start_ref[k], arrived[k].shape[0])
         stores.append(pltpu.make_async_copy(stage[k], out_ref.at[rows, :], store_sem.at[k]))
         stores[-1].start()
     for store in stores:
@@ -339,14 +436,14 @@
         grid_spec=pltpu.PrefetchScalarGridSpec(
             num_scalar_prefetch=1,
             grid=(1,),
-            in_specs=[pl.BlockSpec(memory_space=pl.ANY)] * (n + 1),
-            out_specs=pl.BlockSpec(memory_space=pl.ANY),
+            in_specs=[ANY_SPACE] * (n + 1),
+            out_specs=ANY_SPACE,
             scratch_shapes=[pltpu.VMEM(a.shape, F32) for a in arrived] + [pltpu.SemaphoreType.DMA((n,))] * 2,
         ),
         out_shape=jax.ShapeDtypeStruct(out.shape, F32),
         input_output_aliases={n + 1: 0},
-        compiler_params=pltpu.CompilerParams(vmem_limit_bytes=48 * MIB),
-        cost_estimate=pl.CostEstimate(flops=5 * 10 ** 9, bytes_accessed=8 * sum(a.size for a in arrived), transcendentals=0),
+        compiler_params=vmem_mib(48),
+        cost_estimate=cost(SHORT, 8 * sum(a.size for a in arrived)),
     )(jnp.concatenate(starts).astype(I32), *arrived, out)
 
 
@@ -373,26 +470,24 @@
         pos_onehot = (pos[:, :, None] == jnp.arange(seq_len)[None, None, :]).astype(BF16)
         pos_row = jnp.pad(mask_pos, ((0, 0), (0, 128 - n_masks)), constant_values=-1).astype(F32)[:, None, :]
         tok_f32, tok_bf16 = jax.ShapeDtypeStruct((n_own, width), F32), jax.ShapeDtypeStruct((n_own, width), BF16)
-        own_block = pl.BlockSpec((n_own, width), lambda i: (0, 0))
+        own_block = fixed((n_own, width))
+        vectors = jnp.stack([b_trans, ln_gain, ln_bias])
         masked_h, pre_act, u_own, u_f = pl.pallas_call(
             functools.partial(front_kernel, n_rows),
             grid=(n_rows,),
             in_specs=[
-                pl.BlockSpec((1, seq_len, width), lambda i: (i, 0, 0)), pl.BlockSpec((1, 1, 128), lambda i: (i, 0, 0)),
-                pl.BlockSpec((width, width), lambda i: (0, 0)), pl.BlockSpec((3, width), lambda i: (0, 0)),
+                stepped((1, seq_len, width)), stepped((1, 1, 128)),
+                fixed((width, width)), fixed((3, width)),
             ],
             out_specs=[own_block] * 4,
             out_shape=[tok_bf16, tok_f32, tok_bf16, tok_f32],
-            compiler_params=pltpu.CompilerParams(vmem_limit_bytes=48 * MIB),
-            cost_estimate=pl.CostEstimate(flops=2 * n_own * width * (width + seq_len), bytes_accessed=2 * hidden.size, transcendentals=0),
-        )(hidden, pos_row, w_trans, jnp.stack([b_trans, ln_gain, ln_bias]))
-
-        _, head_vjp = jax.vjp(head_norm, pre_act, ln_gain, ln_bias)
+            compiler_params=vmem_mib(48),
+            cost_estimate=cost(2 * n_own * width * (width + seq_len), 2 * hidden.size),
+        )(hidden, pos_row, w_trans, vectors)
 
         half = n_own // 2
         u_sib, u_x, u_y = swap(u_f, 1), swap(u_f, 2), swap(u_f, 4)
         blk = n_own // 16
-        at = lambda m, o=0: ((me ^ m) * blk + o)[None]
 
         n_steps = -(-shard_rows // VT)
         last = shard_rows - VT
@@ -403,11 +498,9 @@
         lab_pad = jnp.pad(labels, ((0, 0), (0, SLOTS - n_masks)), constant_values=-1000000).reshape(n_own)
         lab_rel = (lab_pad - row_start).astype(F32)
         lab_row = lab_rel[None]
-        row_block = pl.BlockSpec((1, n_own), lambda i: (0, 0))
-        emb_block = pl.BlockSpec((pl.Element(VT), pl.Element(width)), lambda i: (pl.multiple_of(jnp.minimum(i * (VT // 16), last // 16) * 16, 16), 0))
-        col_block = pl.BlockSpec((1, 1, VT), lambda i: (i, 0, 0))
+        row_block = fixed((1, n_own))
         state = jax.ShapeDtypeStruct((3, n_own, 128), F32)
-        state_block = pl.BlockSpec(state.shape, lambda i: (0, 0, 0))
+        state_block = fixed(state.shape)
 
         def own_call(begin, end, carry):
             first = not carry
@@ -419,12 +512,12 @@
                 in_specs=[
                     own_block,
                     pl.BlockSpec((pl.Element(VT), pl.Element(width)), lambda i: (pl.multiple_of(jnp.minimum(skip(i) * (VT // 16), last // 16) * 16, 16), 0)),
-                    pl.BlockSpec((1, 1, VT), lambda i: (skip(i), 0, 0)), pl.BlockSpec((1, 1, VT), lambda i: (skip(i), 0, 0)), row_block,
+                    stepped((1, 1, VT), begin), stepped((1, 1, VT), begin), row_block,
                 ] + ([] if first else [own_block, state_block]),
-                out_specs=[own_block, state_block if first else pl.BlockSpec((8, n_own), lambda i: (0, 0))],
+                out_specs=[own_block, state_block if first else fixed((8, n_own))],
                 out_shape=[tok_f32, last_shape],
                 scratch_shapes=[pltpu.VMEM((n_own, 128), F32)] * 4,
-                compiler_params=pltpu.CompilerParams(vmem_limit_bytes=56 * MIB),
+                compiler_params=vmem_mib(56),
                 cost_estimate=pl.CostEstimate(
                     flops=4 * n_own * (end - begin) * VT * width // COST_SCALE, bytes_accessed=2 * (end - begin) * VT * width, transcendentals=n_own * shard_rows),
             )(u_own, emb_table, b_pad, cols, lab_row, *carry)
@@ -441,9 +534,12 @@
         (u_d0, u_d1), du_sum = lax.optimization_barrier(((u_d0, u_d1), du_sum))
         u_ds0, u_ds1 = swap(u_d0, 1), swap(u_d1, 1)
 
+        ranks = jnp.stack([me ^ m for m in range(n_groups)]).astype(I32)
+        split = jnp.repeat(ranks[6:], 2) * blk + jnp.tile(jnp.array([0, blk // 2], I32), 2)
+        u_starts = jnp.concatenate([ranks[:6] * blk, split])
         u_all = place(
-            [u_f, u_sib, u_x, u_y, u_xs, u_ys, u_d0, u_d1, u_ds0, u_ds1],
-            jnp.concatenate([at(0), at(1), at(2), at(4), at(3), at(5), at(6), at(6, blk // 2), at(7), at(7, blk // 2)]).astype(I32), n_all)
+            [u_f, u_sib, u_x, u_xs, u_y, u_ys, u_d0, u_d1, u_ds0, u_ds1],
+            u_starts, n_all)
         tok, coef, loss_row = pl.pallas_call(
             functools.partial(norm_kernel, n_masks, inv_n, shard_rows),
             in_specs=[pl.BlockSpec(memory_space=pltpu.SMEM)] + [pl.BlockSpec(memory_space=pltpu.VMEM)] * 3,
@@ -451,11 +547,10 @@
         )(plane[None], stats, other, lab_row)
         toks = [tok] + [swap(tok, m) for m in range(1, n_groups)]
         du_part = pl.pallas_call(
-            du_kernel, out_shape=tok_f32, compiler_params=pltpu.CompilerParams(vmem_limit_bytes=32 * MIB),
-            cost_estimate=pl.CostEstimate(flops=10 ** 9, bytes_accessed=10 * n_own * width, transcendentals=0),
+            du_kernel, out_shape=tok_f32, compiler_params=vmem_mib(32),
+            cost_estimate=cost(SHORT, 10 * n_own * width),
         )(du_sum, label_rows, coef)
         du_other = swap(du_part, 1, "vp")
-        ranks = jnp.stack([me ^ m for m in range(n_groups)]).astype(I32)
         norm_all, lab_all = place_toks(toks, ranks)
 
         nx, nl = SHARE_CHUNKS * SHARE_TILE // 16, LOCAL_TILES * LOCAL_TILE // 16
@@ -502,19 +597,20 @@
         near1 = near(1, sx1, sy1)
 
         du_other, out = after((du_other, out))
-        d_pre, d_ln_gain, d_ln_bias = head_vjp(du_part + du_other)
-        d_pre_bf = d_pre.astype(BF16)
-        d_w_part = lax.dot_general(masked_h, d_pre_bf, (((0,), (0,)), ((), ())), preferred_element_type=F32)
         hw = width // 2
-        small = jnp.concatenate([jnp.sum(d_pre, axis=0), d_ln_gain, d_ln_bias, loss_row[0]]).reshape(4, width)
-        total = hw + 4
-        padded = -(-total // 64) * 64
-        part = padded // n_groups
-        mine = jnp.concatenate([lax.dynamic_slice(d_w_part, (plane * hw, 0), (hw, width)), small, jnp.zeros((padded - total, width), F32)])
-        mine = mine.reshape(n_groups, part, width)
-        mine, out, d_pre_bf = after((mine, out, d_pre_bf))
-        piece = lambda a, m: lax.dynamic_index_in_dim(a, me ^ m, 0, keepdims=False)
-        got = [swap(piece(mine, m), m) for m in range(1, n_groups)]
+        padded = -(-(hw + 4) // 64) * 64
+        part = jax.ShapeDtypeStruct((padded // n_groups, width), F32)
+        vmem = pl.BlockSpec(memory_space=pltpu.VMEM)
+        *parts, d_masked = pl.pallas_call(
+            functools.partial(head_kernel, n_groups),
+            in_specs=[pl.BlockSpec(memory_space=pltpu.SMEM)] + [vmem] * 7,
+            out_shape=[part] * n_groups + [tok_bf16],
+            scratch_shapes=[pltpu.VMEM((padded, width), F32)],
+            compiler_params=vmem_mib(40),
+            cost_estimate=pl.CostEstimate(flops=3 * n_own * width * width, bytes_accessed=20 * n_own * width, transcendentals=2 * n_own * width),
+        )(jnp.concatenate([ranks, plane[None]]), pre_act, du_part, du_other, masked_h, w_trans, vectors, loss_row)
+        parts, out, d_masked = after((parts, out, d_masked))
+        got = [swap(parts[m], m) for m in range(1, n_groups)]
 
         out, db2, sx2, sy2 = shared_rows(out, 2, [])
         near2 = near(2, sx2, sy2)
@@ -526,7 +622,7 @@
         out, rx1, ry1, sx3, sy3, got = after((out, rx1, ry1, sx3, sy3, got))
         rx3, ry3 = swap(sx3, 2), swap(sy3, 4)
         far1 = far(1, rx1, ry1)
-        parts = [piece(mine, 0)] + got
+        parts = parts[:1] + got
         level = lambda v: [v[i] + v[i + 1] for i in range(0, len(v), 2)]
         acc = level(level(level(parts)))[0]
         db_mine = jnp.stack([jnp.concatenate([d[i, 0, :SHARE_TILE] for d in (db0, db1, db2, db3)]) for i in range(2)])
@@ -535,31 +631,29 @@
         db_rel = [db_mine] + [swap(db_mine, m) for m in (1, 2, 3)]
         out, got0, dl0 = local_rows(out, 0, near2 + far0)
         sums, out = after((sums, out))
-        grads = gather_pieces(sums, ranks).reshape(padded, width)
-        w_half, out = after((grads[:hw], out))
+        w_half, small = join_pieces(sums, ranks, hw)
+        w_half, out = after((w_half, out))
         w_other = swap(w_half, 1, "vp")
-        d_masked = dot_nt(d_pre_bf, w_trans).astype(BF16).reshape(n_rows, SLOTS, width)
         out, rx2, ry2, d_masked, db_rel = after((out, rx2, ry2, d_masked, db_rel))
         far2 = far(2, rx2, ry2)
         db_sh = jnp.stack(db_rel, 1).reshape(2, 2, 2, 16 * nx)
         db_sh = jnp.where(par == 1, jnp.flip(db_sh, 1), db_sh)
         db_sh = jnp.where(core == 1, jnp.flip(db_sh, 2), db_sh).reshape(2 * 4 * 16 * nx)
-        out, got1, dl1 = local_rows(out, 1, near3 + far1 + far2[:2])
+        out, got1, dl1 = local_rows(out, 1, near3 + far1 + far2[:2] + [got0])
         out, rx3, ry3 = after((out, rx3, ry3))
         far3 = far(3, rx3, ry3)
         dl_mine = jnp.concatenate([dl0, dl1]).reshape(16 * nl)
         dl_other = swap(dl_mine, 1)
-        d_hidden = jnp.einsum("clt,cle->cte", pos_onehot, d_masked, preferred_element_type=F32).astype(BF16)
+        d_hidden = jnp.einsum("clt,cle->cte", pos_onehot, d_masked.reshape(n_rows, SLOTS, width), preferred_element_type=F32).astype(BF16)
         put = lambda out, items: copy_rows(out, [a for a, _ in items], [s[:1] for _, s in items])
-        out = put(out, far2[2:] + [got0] + far3[:2])
+        out = put(out, far2[2:] + far3[:2])
         d_emb_table = put(out, [got1] + far3[2:])
         d_w_trans = gather_pieces([w_half, w_other], jnp.stack([plane, 1 - plane]).astype(I32)).reshape(width, width)
-        vec = grads[hw:hw + 3]
-        mlm_loss = grads[hw + 3, 0]
+        mlm_loss = small[3, 0]
         d_b_vocab = jnp.concatenate([db_sh, jnp.where(core == 0, dl_mine, dl_other), jnp.where(core == 0, dl_other, dl_mine)])
-        return mlm_loss, d_hidden, d_w_trans, vec[0], vec[1], vec[2], d_emb_table, d_b_vocab
-
-    in_specs = (P("dp", None, None), P("dp", None), P("dp", None), P(None, None), P(None), P(None), P(None), P("vp", None), P("vp"))
-    out_specs = (P(), P("dp", None, None), P(None, None), P(None), P(None), P(None), P("vp", None), P("vp"))
+        return mlm_loss, d_hidden, d_w_trans, small[0], small[1], small[2], d_emb_table, d_b_vocab
+
+    in_specs = (P("dp"), P("dp"), P("dp"), P(), P(), P(), P(), P("vp"), P("vp"))
+    out_specs = (P(), P("dp"), P(), P(), P(), P(), P("vp"), P("vp"))
 
     return jax.shard_map(local_step, mesh=mesh, in_specs=in_specs, out_specs=out_specs, check_vma=False)

time: 521 us -> 530 us (1.017)
  waiting for transfers between devices: 112 us -> 139 us
  other arithmetic: 18.4 us -> 5.54 us
  matrix products: 10.2 us -> 4.64 us
    ppermute x63, waiting for transfers between devices: 112 us -> 139 us  [swap(): return lax.ppermute(x, axis, [(i, i ^ mask) for i in range(n)])]
    reduce_sum x4 -> x0, other arithmetic: 11.6 us -> none  [the longest x1 5.85 us: head_norm(): row_mean = jnp.mean(gelu_out, axis=-1, keepdims=True)]
    pallas_call x1 -> x3, Pallas kernels: 1.74 us -> 8.99 us  [the longest x1 5.06 us: local_step(): pl.pallas_call(functools.partial(head_kernel, n_groups), in_specs=[pl.Blo...]
    dot_general x3 -> x1, matrix products: 10.2 us -> 4.64 us  [local_step(): jnp.einsum('clt,cle->cte', pos_onehot, d_masked.reshape(n_rows, SLOTS, wi...]
    unnamed x97 -> x91, local copies, waits for them, and re-layouts: 14.5 us -> 15.2 us
  transfers between devices with their start and end apart: 63 -> 63, of which waited for: 20 -> 27; matrix products, arithmetic and copies ran while one was open for 11% -> 6% of each run, Pallas kernels for 53% -> 47%
where the time goes in v3:
time: 530 us; the launch traced here: 523 us
  Pallas kernels  288 us (54%)
  waiting for transfers between devices  139 us (26%)
  starting transfers between devices  43.3 us (8%)
  local copies, waits for them, and re-layouts  40.4 us (8%)
  other arithmetic  5.54 us (1%)
    pallas_call x6, Pallas kernels, emb_rows(): pl.pallas_call(functools.partial(rows_kernel, cfg), grid_spec=pltpu.Prefe...  167 us
    ppermute x63, waiting for transfers between devices, swap(): return lax.ppermute(x, axis, [(i, i ^ mask) for i in range(n)])  139 us
    pallas_call x2, Pallas kernels, own_call(): pl.pallas_call(functools.partial(own_kernel, end - begin, first), grid=(e...  75 us
    ppermute x63, starting transfers between devices, swap(): return lax.ppermute(x, axis, [(i, i ^ mask) for i in range(n)])  43.3 us
    unnamed x91, local copies, waits for them, and re-layouts  15.2 us
    pallas_call x2, Pallas kernels, copy_rows(): pl.pallas_call(functools.partial(copy_kernel, n), grid_spec=pltpu.Prefetc...  11.8 us
    gather x1, local copies, waits for them, and re-layouts, local_step(): jnp.take(emb_table, jnp.where((lab_local >= 0) & (lab_local < shard_rows)...  11 us
  transfers between devices with their start and end apart: 63, of which 27 were waited for; matrix products, arithmetic and copies ran while one was open for 6% of the time, Pallas kernels for 47%

profile of v3, /device:TPU:0, one launch (start us, length us, event | category | flops | bytes accessed | tf_op | source)
XLA Modules:
  0.0 522.9 jit_solution(3327512948589429799)
XLA Ops:
  4.7 9.3 %shard_map.161 = (bf16[640,768]{1,0:T(8,128)(2,1)S(1)}, f32[640,768]{1,0:T(8,128)S(1)}, bf16[640,768]{1,0:T(8,128)(2,1)S(1)}, f32[640,768]{1,0:T(8,128)}) custom-call(bf16[8,512,768]{2,1,0:T(8,128)(2,1)} %hid_ref.1, f32[8,1,128]{2,1,0:T(1,128)S(1)} %bitcast.65, bf16[768,768]{1,0:T(8,128)(2,1)S(1)} %copy-done, f32[3,768]{1,0:T(4,128)S(1)} %pad_maximum_fusion.3.vec_ref), custom_call_target="tpu_custom_call" | custom-call | flops 1258291200 | bytes 6291456 | tf_op jit(solution)/shard_map/pallas_call | solution.py:475
  17.2 3.2 collective-permute-start
  24.3 45.9 %shard_map.162 = (f32[640,768]{1,0:T(8,128)}, f32[3,640,128]{2,1,0:T(8,128)}) custom-call(bf16[640,768]{1,0:T(8,128)(2,1)} %copy-done.2, bf16[25152,768]{1,0:T(8,128)(2,1)} %emb_ref.15, f32[11,1,2304]{2,1,0:T(1,128)} %reshape.115.bias_ref, f32[11,1,2304]{2,1,0:T(1,128)} %reshape.116.col_ref, f32[1,640]{1,0:T(1,128)} %convert_element_type.26.lab_row_ref.lab_ref), custom_call_target="tpu_custom_call" | custom-call | flops 7927234560 | bytes 24772608 | tf_op jit(solution)/shard_map/pallas_call | solution.py:509
  70.2 2.2 slice.74
  74.3 29.0 %shard_map.163 = (f32[640,768]{1,0:T(8,128)}, f32[8,640]{1,0:T(8,128)}) custom-call(bf16[640,768]{1,0:T(8,128)(2,1)} %copy-done.2, bf16[25152,768]{1,0:T(8,128)(2,1)} %emb_ref.15, f32[11,1,2304]{2,1,0:T(1,128)} %reshape.115.bias_ref, f32[11,1,2304]{2,1,0:T(1,128)} %reshape.116.col_ref, f32[1,640]{1,0:T(1,128)} %convert_element_type.26.lab_row_ref.lab_ref, ...), custom_call_target="tpu_custom_call" | custom-call | flops 4529848320 | bytes 14155776 | tf_op jit(solution)/shard_map/pallas_call | solution.py:509
  103.3 2.1 collective-permute-start.4
  105.4 2.0 collective-permute-done.4.other_ref
  109.5 3.0 collective-permute-done.11.refs_1_
  114.0 11.0 %gather_fusion = bf16[640,768]{1,0:T(8,128)(2,1)} fusion(bf16[25152,768]{1,0:T(8,128)(2,1)} %emb_ref.15, s32[1024]{0:T(1024)S(1)} %pad_clamp_fusion), kind=kCustom, calls=%fused_computation | custom fusion | bytes 1968640 | tf_op jit(solution)/shard_map/jit(_take)/gather | solution.py:532
  125.1 1.9 collective-permute-start.14
  128.4 2.9 collective-permute-start.16
  133.9 1.5 copy-done.6
  138.7 2.1 shard_map.167
  140.8 1.5 copy-done.3
  142.3 1.5 copy-done.5
  143.9 8.8 %shard_map.166.u_ref = bf16[5120,768]{1,0:T(8,128)(2,1)} custom-call(s32[10]{0:T(128)S(1)} %pad_add_fusion.2.start_ref, f32[640,768]{1,0:T(8,128)S(1)} %copy-done.3, f32[640,768]{1,0:T(8,128)S(1)} %copy-done.5, f32[640,768]{1,0:T(8,128)} %collective-permute-done.refs_2_, f32[640,768]{1,0:T(8,128)} %collective-permute-done.7.refs_3_, ...), custom_call_target="tpu_custom_call" | custom-call | flops 1000000000 | bytes 23592960 | tf_op jit(solution)/shard_map/pallas_call | solution.py:220
  152.7 27.3 %shard_map.168 = (f32[25152,768]{1,0:T(8,128)}, f32[2,1,640]{2,1,0:T(1,128)S(1)}, f32[624,768]{1,0:T(8,128)}, f32[624,768]{1,0:T(8,128)}) custom-call(s32[4]{0:T(128)S(1)} %pad_add_fusion.4.start_ref, bf16[25152,768]{1,0:T(8,128)(2,1)} %emb_ref.15, f32[32,1,640]{2,1,0:T(1,128)S(1)} %broadcast_in_dim.139.bias_ref, bf16[5120,768]{1,0:T(8,128)(2,1)} %shard_map.166.u_ref, ...), custom_call_target="tpu_custom_call" | custom-call | flops 1226833920 | bytes 9584640 | tf_op jit(solution)/shard_map/pallas_call | solution.py:395
  183.4 27.8 %shard_map.169 = (f32[25152,768]{1,0:T(8,128)}, f32[2,1,640]{2,1,0:T(1,128)S(1)}, f32[624,768]{1,0:T(8,128)}, f32[624,768]{1,0:T(8,128)}) custom-call(s32[4]{0:T(128)S(1)} %pad_add_fusion.1.start_ref, bf16[25152,768]{1,0:T(8,128)(2,1)} %emb_ref.15, f32[32,1,640]{2,1,0:T(1,128)S(1)} %broadcast_in_dim.139.bias_ref, ...), custom_call_target="tpu_custom_call", output_to_operand_aliasing={{0}: (6, {})} | custom-call | flops 1226833920 | bytes 9584640 | tf_op jit(solution)/shard_map/pallas_call | solution.py:395
  211.2 5.1 shard_map.170
  218.2 10.4 %collective-permute-done.27 = f32[56,768]{1,0:T(8,128)S(1)} collective-permute-done((f32[56,768]{1,0:T(8,128)S(1)}, f32[56,768]{1,0:T(8,128)S(1)}, u32[]{:S(2)}, u32[]{:S(2)}) %collective-permute-start.27) | collective-permute-done | bytes 172064 | tf_op jit(solution)/shard_map/ppermute | solution.py:452
  230.1 1.8 collective-permute-done.28
  231.9 2.7 collective-permute-done.29
  234.6 4.8 collective-permute-start.31
  241.0 3.0 collective-permute-done.31
  244.0 4.0 collective-permute-done.32
  251.3 27.3 %shard_map.171 = (f32[25152,768]{1,0:T(8,128)}, f32[2,1,640]{2,1,0:T(1,128)S(1)}, f32[624,768]{1,0:T(8,128)}, f32[624,768]{1,0:T(8,128)}) custom-call(s32[4]{0:T(128)S(1)} %pad_add_fusion.7.start_ref, bf16[25152,768]{1,0:T(8,128)(2,1)} %emb_ref.15, f32[32,1,640]{2,1,0:T(1,128)S(1)} %broadcast_in_dim.139.bias_ref, ...), custom_call_target="tpu_custom_call", output_to_operand_aliasing={{0}: (6, {})} | custom-call | flops 1226833920 | bytes 9584640 | tf_op jit(solution)/shard_map/pallas_call | solution.py:395
  279.2 13.3 %collective-permute-done.24.refs_2_ = f32[624,768]{1,0:T(8,128)S(1)} collective-permute-done((f32[624,768]{1,0:T(8,128)}, f32[624,768]{1,0:T(8,128)S(1)}, u32[]{:S(2)}, u32[]{:S(2)}) %collective-permute-start.24) | collective-permute-done | bytes 1916960 | tf_op jit(solution)/shard_map/ppermute | solution.py:452
  294.6 27.7 %shard_map.172 = (f32[25152,768]{1,0:T(8,128)}, f32[2,1,640]{2,1,0:T(1,128)S(1)}, f32[624,768]{1,0:T(8,128)}, f32[624,768]{1,0:T(8,128)}) custom-call(s32[8]{0:T(128)S(1)} %concatenate.78.start_ref, bf16[25152,768]{1,0:T(8,128)(2,1)} %emb_ref.15, f32[32,1,640]{2,1,0:T(1,128)S(1)} %broadcast_in_dim.139.bias_ref, ...), custom_call_target="tpu_custom_call", output_to_operand_aliasing={{0}: (10, {})} | custom-call | flops 1226833920 | bytes 9584640 | tf_op jit(solution)/shard_map/pallas_call | solution.py:395
  324.0 28.4 %shard_map.173 = (f32[25152,768]{1,0:T(8,128)}, f32[3,1,512]{2,1,0:T(1,128)S(1)}, f32[1296,768]{1,0:T(8,128)}) custom-call(s32[12]{0:T(128)S(1)} %concatenate.83.start_ref, bf16[25152,768]{1,0:T(8,128)(2,1)} %emb_ref.15, f32[12,1,512]{2,1,0:T(1,128)S(1)} %broadcast_in_dim.157.bias_ref, ...), custom_call_target="tpu_custom_call", output_to_operand_aliasing={{0}: (12, {})} | custom-call | flops 1274019840 | bytes 9953280 | tf_op jit(solution)/shard_map/pallas_call | solution.py:395
  355.2 4.8 collective-permute-done.46
  360.5 36.9 %collective-permute-done.47 = f32[2,2496]{1,0:T(2,128)S(1)} collective-permute-done((f32[2,2496]{1,0:T(2,128)S(1)}, f32[2,2496]{1,0:T(2,128)S(1)}, u32[]{:S(2)}, u32[]{:S(2)}) %collective-permute-start.47) | collective-permute-done | bytes 20000 | tf_op jit(solution)/shard_map/ppermute | solution.py:452
  397.4 3.2 collective-permute-done.48
  401.3 6.5 %collective-permute-done.34.refs_2_ = f32[56,768]{1,0:T(8,128)S(1)} collective-permute-done((f32[56,768]{1,0:T(8,128)S(1)}, f32[56,768]{1,0:T(8,128)S(1)}, u32[]{:S(2)}, u32[]{:S(2)}) %collective-permute-start.34) | collective-permute-done | bytes 172064 | tf_op jit(solution)/shard_map/ppermute | solution.py:452
  410.1 6.4 %collective-permute-done.36.refs_4_ = f32[56,768]{1,0:T(8,128)S(1)} collective-permute-done((f32[56,768]{1,0:T(8,128)S(1)}, f32[56,768]{1,0:T(8,128)S(1)}, u32[]{:S(2)}, u32[]{:S(2)}) %collective-permute-start.36) | collective-permute-done | bytes 172064 | tf_op jit(solution)/shard_map/ppermute | solution.py:452
  417.4 1.9 collective-permute-start.39
  419.4 4.9 collective-permute-done.38.refs_6_
  429.4 1.6 collective-permute-done.53.refs_5_
  431.3 3.5 shard_map.174
  434.8 1.8 collective-permute-done.51.refs_1_
  438.1 28.8 %shard_map.176 = (f32[25152,768]{1,0:T(8,128)}, f32[3,1,512]{2,1,0:T(1,128)S(1)}, f32[1296,768]{1,0:T(8,128)}) custom-call(s32[15]{0:T(128)S(1)} %concatenate.85.start_ref, bf16[25152,768]{1,0:T(8,128)(2,1)} %emb_ref.15, f32[12,1,512]{2,1,0:T(1,128)S(1)} %broadcast_in_dim.157.bias_ref, ...), custom_call_target="tpu_custom_call", output_to_operand_aliasing={{0}: (15, {})} | custom-call | flops 1274019840 | bytes 9953280 | tf_op jit(solution)/shard_map/pallas_call | solution.py:395
  467.0 3.4 collective-permute-start.49
  471.6 2.0 collective-permute-done.56.refs_2_
  473.6 1.6 collective-permute-done.57.refs_3_
  475.2 22.1 %collective-permute-done.49.refs_1_ = f32[384,768]{1,0:T(8,128)} collective-permute-done((f32[384,768]{1,0:T(8,128)}, f32[384,768]{1,0:T(8,128)}, u32[]{:S(2)}, u32[]{:S(2)}) %collective-permute-start.49) | collective-permute-done | bytes 1179680 | tf_op jit(solution)/shard_map/ppermute | solution.py:452
  500.9 4.6 convolution_convert_fusion
  505.6 3.8 shard_map.175
  510.1 5.9 %shard_map.177.refs_3_ = f32[25152,768]{1,0:T(8,128)} custom-call(s32[4]{0:T(128)S(1)} %pad_add_fusion.10.start_ref, f32[624,768]{1,0:T(8,128)S(1)} %collective-permute-done.60.refs_0_, f32[624,768]{1,0:T(8,128)} %collective-permute-done.61.refs_1_, f32[624,768]{1,0:T(8,128)} %collective-permute-done.56.refs_2_, ...), custom_call_target="tpu_custom_call", output_to_operand_aliasing={{}: (5, {})} | custom-call | flops 1000000000 | bytes 15335424 | tf_op jit(solution)/shard_map/pallas_call | solution.py:434
  516.7 5.9 %shard_map.178 = f32[25152,768]{1,0:T(8,128)} custom-call(s32[3]{0:T(128)S(1)} %pad_add_fusion.9.start_ref, f32[1296,768]{1,0:T(8,128)} %collective-permute-done.55.refs_0_, f32[624,768]{1,0:T(8,128)} %collective-permute-done.58.refs_1_, f32[624,768]{1,0:T(8,128)} %collective-permute-done.59.refs_2_, ...), custom_call_target="tpu_custom_call", output_to_operand_aliasing={{}: (4, {})} | custom-call | flops 1000000000 | bytes 15630336 | tf_op jit(solution)/shard_map/pallas_call | solution.py:434
  (276 shorter events, 60.1 us)
Async XLA Ops:
  17.2 53.1 %collective-permute-start = (f32[640,768]{1,0:T(8,128)}, f32[640,768]{1,0:T(8,128)}, u32[]{:S(2)}, u32[]{:S(2)}) collective-permute-start(f32[640,768]{1,0:T(8,128)} %get-tuple-element.116.refs_0_), channel_id=1, source_target_pairs={{0,2},{1,3},{2,0},{3,1},{4,6},{5,7},{6,4},{7,5},{8,10},{9,11},{10,... | collective-permute-start | bytes 5898248 | tf_op jit(solution)/shard_map/ppermute | solution.py:452
  20.4 49.9 %collective-permute-start.1 = (f32[640,768]{1,0:T(8,128)}, f32[640,768]{1,0:T(8,128)}, u32[]{:S(2)}, u32[]{:S(2)}) collective-permute-start(f32[640,768]{1,0:T(8,128)} %get-tuple-element.116.refs_0_), channel_id=1, source_target_pairs={{0,4},{1,5},{2,6},{3,7},{4,0},{5,1},{6,2},{7,3},{8,12},{9,13},{10,... | collective-permute-start | bytes 5898248 | tf_op jit(solution)/shard_map/ppermute | solution.py:452
  21.9 87.5 %collective-permute-start.6 = (f32[640,768]{1,0:T(8,128)}, f32[640,768]{1,0:T(8,128)S(1)}, u32[]{:S(2)}, u32[]{:S(2)}) collective-permute-start(f32[640,768]{1,0:T(8,128)} %get-tuple-element.116.refs_0_), channel_id=1, source_target_pairs={{0,1},{1,0},{2,3},{3,2},{4,5},{5,4},{6,7},{7,6},{8,9},{9,8},{10,11... | collective-permute-start | bytes 5898248 | tf_op jit(solution)/shard_map/ppermute | solution.py:452
  72.4 52.6 %collective-permute-start.2 = (f32[320,768]{1,0:T(8,128)}, f32[320,768]{1,0:T(8,128)}, u32[]{:S(2)}, u32[]{:S(2)}) collective-permute-start(f32[320,768]{1,0:T(8,128)} %slice.74), channel_id=1, source_target_pairs={{0,4},{1,5},{2,6},{3,7},{4,0},{5,1},{6,2},{7,3},{8,12},{9,13},{10,... | collective-permute-start | bytes 2949128 | tf_op jit(solution)/shard_map/ppermute | solution.py:452
  74.2 52.8 %collective-permute-start.3 = (f32[320,768]{1,0:T(8,128)S(1)}, f32[320,768]{1,0:T(8,128)}, u32[]{:S(2)}, u32[]{:S(2)}) collective-permute-start(f32[320,768]{1,0:T(8,128)S(1)} %slice.75), channel_id=1, source_target_pairs={{0,2},{1,3},{2,0},{3,1},{4,6},{5,7},{6,4},{7,5},{8,10},{9,11},{10,... | collective-permute-start | bytes 2949128 | tf_op jit(solution)/shard_map/ppermute | solution.py:452
  105.4 35.4 %collective-permute-start.7 = (f32[640,768]{1,0:T(8,128)}, f32[640,768]{1,0:T(8,128)}, u32[]{:S(2)}, u32[]{:S(2)}) collective-permute-start(f32[640,768]{1,0:T(8,128)} %collective-permute-done.refs_2_), channel_id=1, source_target_pairs={{0,1},{1,0},{2,3},{3,2},{4,5},{5,4},{6,7},{7,6},{8,9},{9,8},{10,11... | collective-permute-start | bytes 5898248 | tf_op jit(solution)/shard_map/ppermute | solution.py:452
  107.4 33.4 %collective-permute-start.8 = (f32[640,768]{1,0:T(8,128)}, f32[640,768]{1,0:T(8,128)}, u32[]{:S(2)}, u32[]{:S(2)}) collective-permute-start(f32[640,768]{1,0:T(8,128)} %collective-permute-done.1.refs_4_), channel_id=1, source_target_pairs={{0,1},{1,0},{2,3},{3,2},{4,5},{5,4},{6,7},{7,6},{8,9},{9,8},{10,11... | collective-permute-start | bytes 5898248 | tf_op jit(solution)/shard_map/ppermute | solution.py:452
  112.5 12.5 %collective-permute-start.12 = (f32[2,640]{1,0:T(2,128)}, f32[2,640]{1,0:T(2,128)S(1)}, u32[]{:S(2)}, u32[]{:S(2)}) collective-permute-start(f32[2,640]{1,0:T(2,128)} %get-tuple-element.130.refs_0_), channel_id=1, source_target_pairs={{0,2},{1,3},{2,0},{3,1},{4,6},{5,7},{6,4},{7,5},{8,10},{9,11},{10,... | collective-permute-start | bytes 15368 | tf_op jit(solution)/shard_map/ppermute | solution.py:452
  131.3 9.4 %collective-permute-start.10 = (f32[320,768]{1,0:T(8,128)}, f32[320,768]{1,0:T(8,128)}, u32[]{:S(2)}, u32[]{:S(2)}) collective-permute-start(f32[320,768]{1,0:T(8,128)} %collective-permute-done.3.refs_7_), channel_id=1, source_target_pairs={{0,1},{1,0},{2,3},{3,2},{4,5},{5,4},{6,7},{7,6},{8,9},{9,8},{10,11... | collective-permute-start | bytes 2949128 | tf_op jit(solution)/shard_map/ppermute | solution.py:452
  131.4 9.4 %collective-permute-start.9 = (f32[320,768]{1,0:T(8,128)}, f32[320,768]{1,0:T(8,128)}, u32[]{:S(2)}, u32[]{:S(2)}) collective-permute-start(f32[320,768]{1,0:T(8,128)} %collective-permute-done.2.refs_6_), channel_id=1, source_target_pairs={{0,1},{1,0},{2,3},{3,2},{4,5},{5,4},{6,7},{7,6},{8,9},{9,8},{10,11... | collective-permute-start | bytes 2949128 | tf_op jit(solution)/shard_map/ppermute | solution.py:452
  136.9 74.2 %collective-permute-start.5 = (f32[640,768]{1,0:T(8,128)S(1)}, f32[640,768]{1,0:T(8,128)}, u32[]{:S(2)}, u32[]{:S(2)}) collective-permute-start(f32[640,768]{1,0:T(8,128)S(1)} %shard_map.165.mine_ref), channel_id=1, source_target_pairs={{0,8},{8,0},{1,9},{9,1},{2,10},{10,2},{3,11},{11,3},{4,12},{12,4},... | collective-permute-start | bytes 5898248 | tf_op jit(solution)/shard_map/ppermute | solution.py:452
  180.0 68.0 %collective-permute-start.22 = (f32[624,768]{1,0:T(8,128)}, f32[624,768]{1,0:T(8,128)}, u32[]{:S(2)}, u32[]{:S(2)}) collective-permute-start(f32[624,768]{1,0:T(8,128)} %get-tuple-element.149), channel_id=1, source_target_pairs={{0,2},{1,3},{2,0},{3,1},{4,6},{5,7},{6,4},{7,5},{8,10},{9,11},{10,... | collective-permute-start | bytes 5750792 | tf_op jit(solution)/shard_map/ppermute | solution.py:452
  181.6 66.9 %collective-permute-start.23 = (f32[624,768]{1,0:T(8,128)}, f32[624,768]{1,0:T(8,128)}, u32[]{:S(2)}, u32[]{:S(2)}) collective-permute-start(f32[624,768]{1,0:T(8,128)} %get-tuple-element.150), channel_id=1, source_target_pairs={{0,4},{1,5},{2,6},{3,7},{4,0},{5,1},{6,2},{7,3},{8,12},{9,13},{10,... | collective-permute-start | bytes 5750792 | tf_op jit(solution)/shard_map/ppermute | solution.py:452
  216.3 32.4 %collective-permute-start.20 = (f32[624,768]{1,0:T(8,128)}, f32[624,768]{1,0:T(8,128)S(1)}, u32[]{:S(2)}, u32[]{:S(2)}) collective-permute-start(f32[624,768]{1,0:T(8,128)} %get-tuple-element.151), channel_id=1, source_target_pairs={{0,1},{1,0},{2,3},{3,2},{4,5},{5,4},{6,7},{7,6},{8,9},{9,8},{10,11... | collective-permute-start | bytes 5750792 | tf_op jit(solution)/shard_map/ppermute | solution.py:452
  216.8 11.8 %collective-permute-start.27 = (f32[56,768]{1,0:T(8,128)S(1)}, f32[56,768]{1,0:T(8,128)S(1)}, u32[]{:S(2)}, u32[]{:S(2)}) collective-permute-start(f32[56,768]{1,0:T(8,128)S(1)} %get-tuple-element.162), channel_id=1, source_target_pairs={{0,2},{1,3},{2,0},{3,1},{4,6},{5,7},{6,4},{7,5},{8,10},{9,11},{10,... | collective-permute-start | bytes 516104 | tf_op jit(solution)/shard_map/ppermute | solution.py:452
  217.7 14.2 %collective-permute-start.28 = (f32[56,768]{1,0:T(8,128)S(1)}, f32[56,768]{1,0:T(8,128)S(1)}, u32[]{:S(2)}, u32[]{:S(2)}) collective-permute-start(f32[56,768]{1,0:T(8,128)S(1)} %get-tuple-element.163), channel_id=1, source_target_pairs={{0,3},{1,2},{2,1},{3,0},{4,7},{5,6},{6,5},{7,4},{8,11},{9,10},{10,... | collective-permute-start | bytes 516104 | tf_op jit(solution)/shard_map/ppermute | solution.py:452
  231.9 8.6 %collective-permute-start.30 = (f32[56,768]{1,0:T(8,128)S(1)}, f32[56,768]{1,0:T(8,128)S(1)}, u32[]{:S(2)}, u32[]{:S(2)}) collective-permute-start(f32[56,768]{1,0:T(8,128)S(1)} %get-tuple-element.165), channel_id=1, source_target_pairs={{0,5},{1,4},{2,7},{3,6},{4,1},{5,0},{6,3},{7,2},{8,13},{9,12},{10,... | collective-permute-start | bytes 516104 | tf_op jit(solution)/shard_map/ppermute | solution.py:452
  234.6 9.4 %collective-permute-start.31 = (f32[56,768]{1,0:T(8,128)S(1)}, f32[56,768]{1,0:T(8,128)S(1)}, u32[]{:S(2)}, u32[]{:S(2)}) collective-permute-start(f32[56,768]{1,0:T(8,128)S(1)} %get-tuple-element.166), channel_id=1, source_target_pairs={{0,6},{1,7},{2,4},{3,5},{4,2},{5,3},{6,0},{7,1},{8,14},{9,15},{10,... | collective-permute-start | bytes 516104 | tf_op jit(solution)/shard_map/ppermute | solution.py:452
  240.5 7.5 %collective-permute-start.32 = (f32[56,768]{1,0:T(8,128)S(1)}, f32[56,768]{1,0:T(8,128)S(1)}, u32[]{:S(2)}, u32[]{:S(2)}) collective-permute-start(f32[56,768]{1,0:T(8,128)S(1)} %get-tuple-element.167), channel_id=1, source_target_pairs={{0,7},{1,6},{2,5},{3,4},{4,3},{5,2},{6,1},{7,0},{8,15},{9,14},{10,... | collective-permute-start | bytes 516104 | tf_op jit(solution)/shard_map/ppermute | solution.py:452
  244.0 34.6 %collective-permute-start.21 = (f32[624,768]{1,0:T(8,128)}, f32[624,768]{1,0:T(8,128)}, u32[]{:S(2)}, u32[]{:S(2)}) collective-permute-start(f32[624,768]{1,0:T(8,128)} %get-tuple-element.152), channel_id=1, source_target_pairs={{0,1},{1,0},{2,3},{3,2},{4,5},{5,4},{6,7},{7,6},{8,9},{9,8},{10,11... | collective-permute-start | bytes 5750792 | tf_op jit(solution)/shard_map/ppermute | solution.py:452
  248.0 30.7 %collective-permute-start.18 = (f32[624,768]{1,0:T(8,128)}, f32[624,768]{1,0:T(8,128)}, u32[]{:S(2)}, u32[]{:S(2)}) collective-permute-start(f32[624,768]{1,0:T(8,128)} %get-tuple-element.149), channel_id=1, source_target_pairs={{0,1},{1,0},{2,3},{3,2},{4,5},{5,4},{6,7},{7,6},{8,9},{9,8},{10,11... | collective-permute-start | bytes 5750792 | tf_op jit(solution)/shard_map/ppermute | solution.py:452
  248.1 31.1 %collective-permute-start.19 = (f32[624,768]{1,0:T(8,128)}, f32[624,768]{1,0:T(8,128)}, u32[]{:S(2)}, u32[]{:S(2)}) collective-permute-start(f32[624,768]{1,0:T(8,128)} %get-tuple-element.150), channel_id=1, source_target_pairs={{0,1},{1,0},{2,3},{3,2},{4,5},{5,4},{6,7},{7,6},{8,9},{9,8},{10,11... | collective-permute-start | bytes 5750792 | tf_op jit(solution)/shard_map/ppermute | solution.py:452
  248.5 43.9 %collective-permute-start.24 = (f32[624,768]{1,0:T(8,128)}, f32[624,768]{1,0:T(8,128)S(1)}, u32[]{:S(2)}, u32[]{:S(2)}) collective-permute-start(f32[624,768]{1,0:T(8,128)} %get-tuple-element.151), channel_id=1, source_target_pairs={{0,2},{1,3},{2,0},{3,1},{4,6},{5,7},{6,4},{7,5},{8,10},{9,11},{10,... | collective-permute-start | bytes 5750792 | tf_op jit(solution)/shard_map/ppermute | solution.py:452
  250.0 72.5 %collective-permute-start.25 = (f32[624,768]{1,0:T(8,128)}, f32[624,768]{1,0:T(8,128)}, u32[]{:S(2)}, u32[]{:S(2)}) collective-permute-start(f32[624,768]{1,0:T(8,128)} %get-tuple-element.152), channel_id=1, source_target_pairs={{0,4},{1,5},{2,6},{3,7},{4,0},{5,1},{6,2},{7,3},{8,12},{9,13},{10,... | collective-permute-start | bytes 5750792 | tf_op jit(solution)/shard_map/ppermute | solution.py:452
  278.6 45.4 %collective-permute-start.40 = (f32[624,768]{1,0:T(8,128)}, f32[624,768]{1,0:T(8,128)}, u32[]{:S(2)}, u32[]{:S(2)}) collective-permute-start(f32[624,768]{1,0:T(8,128)} %get-tuple-element.197), channel_id=1, source_target_pairs={{0,1},{1,0},{2,3},{3,2},{4,5},{5,4},{6,7},{7,6},{8,9},{9,8},{10,11... | collective-permute-start | bytes 5750792 | tf_op jit(solution)/shard_map/ppermute | solution.py:452
  278.6 45.4 %collective-permute-start.41 = (f32[624,768]{1,0:T(8,128)}, f32[624,768]{1,0:T(8,128)}, u32[]{:S(2)}, u32[]{:S(2)}) collective-permute-start(f32[624,768]{1,0:T(8,128)} %get-tuple-element.198), channel_id=1, source_target_pairs={{0,1},{1,0},{2,3},{3,2},{4,5},{5,4},{6,7},{7,6},{8,9},{9,8},{10,11... | collective-permute-start | bytes 5750792 | tf_op jit(solution)/shard_map/ppermute | solution.py:452
  279.1 44.9 %collective-permute-start.42 = (f32[624,768]{1,0:T(8,128)}, f32[624,768]{1,0:T(8,128)}, u32[]{:S(2)}, u32[]{:S(2)}) collective-permute-start(f32[624,768]{1,0:T(8,128)} %collective-permute-done.22.refs_2_), channel_id=1, source_target_pairs={{0,1},{1,0},{2,3},{3,2},{4,5},{5,4},{6,7},{7,6},{8,9},{9,8},{10,11... | collective-permute-start | bytes 5750792 | tf_op jit(solution)/shard_map/ppermute | solution.py:452
  292.5 31.6 %collective-permute-start.43 = (f32[624,768]{1,0:T(8,128)}, f32[624,768]{1,0:T(8,128)}, u32[]{:S(2)}, u32[]{:S(2)}) collective-permute-start(f32[624,768]{1,0:T(8,128)} %collective-permute-done.23.refs_3_), channel_id=1, source_target_pairs={{0,1},{1,0},{2,3},{3,2},{4,5},{5,4},{6,7},{7,6},{8,9},{9,8},{10,11... | collective-permute-start | bytes 5750792 | tf_op jit(solution)/shard_map/ppermute | solution.py:452
  352.5 84.1 %collective-permute-start.54 = (f32[1296,768]{1,0:T(8,128)}, f32[1296,768]{1,0:T(8,128)}, u32[]{:S(2)}, u32[]{:S(2)}) collective-permute-start(f32[1296,768]{1,0:T(8,128)} %get-tuple-element.207), channel_id=1, source_target_pairs={{0,1},{1,0},{2,3},{3,2},{4,5},{5,4},{6,7},{7,6},{8,9},{9,8},{10,11... | collective-permute-start | bytes 11943944 | tf_op jit(solution)/shard_map/ppermute | solution.py:452
  353.0 73.3 %collective-permute-start.44 = (f32[624,768]{1,0:T(8,128)}, f32[624,768]{1,0:T(8,128)}, u32[]{:S(2)}, u32[]{:S(2)}) collective-permute-start(f32[624,768]{1,0:T(8,128)} %get-tuple-element.197), channel_id=1, source_target_pairs={{0,2},{1,3},{2,0},{3,1},{4,6},{5,7},{6,4},{7,5},{8,10},{9,11},{10,... | collective-permute-start | bytes 5750792 | tf_op jit(solution)/shard_map/ppermute | solution.py:452
  353.5 72.8 %collective-permute-start.45 = (f32[624,768]{1,0:T(8,128)}, f32[624,768]{1,0:T(8,128)}, u32[]{:S(2)}, u32[]{:S(2)}) collective-permute-start(f32[624,768]{1,0:T(8,128)} %get-tuple-element.198), channel_id=1, source_target_pairs={{0,4},{1,5},{2,6},{3,7},{4,0},{5,1},{6,2},{7,3},{8,12},{9,13},{10,... | collective-permute-start | bytes 5750792 | tf_op jit(solution)/shard_map/ppermute | solution.py:452
  354.7 46.6 %collective-permute-start.33 = (f32[56,768]{1,0:T(8,128)S(1)}, f32[56,768]{1,0:T(8,128)S(1)}, u32[]{:S(2)}, u32[]{:S(2)}) collective-permute-start(f32[56,768]{1,0:T(8,128)S(1)} %add_add_fusion.refs_0_), channel_id=1, source_target_pairs={{0,1},{1,0},{2,3},{3,2},{4,5},{5,4},{6,7},{7,6},{8,9},{9,8},{10,11... | collective-permute-start | bytes 516104 | tf_op jit(solution)/shard_map/ppermute | solution.py:452
  360.0 37.4 %collective-permute-start.47 = (f32[2,2496]{1,0:T(2,128)S(1)}, f32[2,2496]{1,0:T(2,128)S(1)}, u32[]{:S(2)}, u32[]{:S(2)}) collective-permute-start(f32[2,2496]{1,0:T(2,128)S(1)} %pad_maximum_fusion.1), channel_id=1, source_target_pairs={{0,2},{1,3},{2,0},{3,1},{4,6},{5,7},{6,4},{7,5},{8,10},{9,11},{10,... | collective-permute-start | bytes 59912 | tf_op jit(solution)/shard_map/ppermute | solution.py:452
  401.3 7.6 %collective-permute-start.35 = (f32[56,768]{1,0:T(8,128)S(1)}, f32[56,768]{1,0:T(8,128)S(1)}, u32[]{:S(2)}, u32[]{:S(2)}) collective-permute-start(f32[56,768]{1,0:T(8,128)S(1)} %add_add_fusion.refs_0_), channel_id=1, source_target_pairs={{0,3},{1,2},{2,1},{3,0},{4,7},{5,6},{6,5},{7,4},{8,11},{9,10},{10,... | collective-permute-start | bytes 516104 | tf_op jit(solution)/shard_map/ppermute | solution.py:452
  407.8 8.6 %collective-permute-start.36 = (f32[56,768]{1,0:T(8,128)S(1)}, f32[56,768]{1,0:T(8,128)S(1)}, u32[]{:S(2)}, u32[]{:S(2)}) collective-permute-start(f32[56,768]{1,0:T(8,128)S(1)} %add_add_fusion.refs_0_), channel_id=1, source_target_pairs={{0,4},{1,5},{2,6},{3,7},{4,0},{5,1},{6,2},{7,3},{8,12},{9,13},{10,... | collective-permute-start | bytes 516104 | tf_op jit(solution)/shard_map/ppermute | solution.py:452
  408.9 8.5 %collective-permute-start.37 = (f32[56,768]{1,0:T(8,128)S(1)}, f32[56,768]{1,0:T(8,128)S(1)}, u32[]{:S(2)}, u32[]{:S(2)}) collective-permute-start(f32[56,768]{1,0:T(8,128)S(1)} %add_add_fusion.refs_0_), channel_id=1, source_target_pairs={{0,5},{1,4},{2,7},{3,6},{4,1},{5,0},{6,3},{7,2},{8,13},{9,12},{10,... | collective-permute-start | bytes 516104 | tf_op jit(solution)/shard_map/ppermute | solution.py:452
  416.4 7.8 %collective-permute-start.38 = (f32[56,768]{1,0:T(8,128)S(1)}, f32[56,768]{1,0:T(8,128)}, u32[]{:S(2)}, u32[]{:S(2)}) collective-permute-start(f32[56,768]{1,0:T(8,128)S(1)} %add_add_fusion.refs_0_), channel_id=1, source_target_pairs={{0,6},{1,7},{2,4},{3,5},{4,2},{5,3},{6,0},{7,1},{8,14},{9,15},{10,... | collective-permute-start | bytes 516104 | tf_op jit(solution)/shard_map/ppermute | solution.py:452
  417.4 7.6 %collective-permute-start.39 = (f32[56,768]{1,0:T(8,128)S(1)}, f32[56,768]{1,0:T(8,128)S(1)}, u32[]{:S(2)}, u32[]{:S(2)}) collective-permute-start(f32[56,768]{1,0:T(8,128)S(1)} %add_add_fusion.refs_0_), channel_id=1, source_target_pairs={{0,7},{1,6},{2,5},{3,4},{4,3},{5,2},{6,1},{7,0},{8,15},{9,14},{10,... | collective-permute-start | bytes 516104 | tf_op jit(solution)/shard_map/ppermute | solution.py:452
  426.3 8.5 %collective-permute-start.50 = (f32[624,768]{1,0:T(8,128)}, f32[624,768]{1,0:T(8,128)}, u32[]{:S(2)}, u32[]{:S(2)}) collective-permute-start(f32[624,768]{1,0:T(8,128)} %get-tuple-element.211), channel_id=1, source_target_pairs={{0,1},{1,0},{2,3},{3,2},{4,5},{5,4},{6,7},{7,6},{8,9},{9,8},{10,11... | collective-permute-start | bytes 5750792 | tf_op jit(solution)/shard_map/ppermute | solution.py:452
  426.3 10.2 %collective-permute-start.51 = (f32[624,768]{1,0:T(8,128)}, f32[624,768]{1,0:T(8,128)}, u32[]{:S(2)}, u32[]{:S(2)}) collective-permute-start(f32[624,768]{1,0:T(8,128)} %get-tuple-element.212), channel_id=1, source_target_pairs={{0,1},{1,0},{2,3},{3,2},{4,5},{5,4},{6,7},{7,6},{8,9},{9,8},{10,11... | collective-permute-start | bytes 5750792 | tf_op jit(solution)/shard_map/ppermute | solution.py:452
  429.4 44.1 %collective-permute-start.56 = (f32[624,768]{1,0:T(8,128)}, f32[624,768]{1,0:T(8,128)}, u32[]{:S(2)}, u32[]{:S(2)}) collective-permute-start(f32[624,768]{1,0:T(8,128)} %get-tuple-element.211), channel_id=1, source_target_pairs={{0,2},{1,3},{2,0},{3,1},{4,6},{5,7},{6,4},{7,5},{8,10},{9,11},{10,... | collective-permute-start | bytes 5750792 | tf_op jit(solution)/shard_map/ppermute | solution.py:452
  431.1 44.1 %collective-permute-start.57 = (f32[624,768]{1,0:T(8,128)}, f32[624,768]{1,0:T(8,128)}, u32[]{:S(2)}, u32[]{:S(2)}) collective-permute-start(f32[624,768]{1,0:T(8,128)} %get-tuple-element.212), channel_id=1, source_target_pairs={{0,4},{1,5},{2,6},{3,7},{4,0},{5,1},{6,2},{7,3},{8,12},{9,13},{10,... | collective-permute-start | bytes 5750792 | tf_op jit(solution)/shard_map/ppermute | solution.py:452
  466.9 49.8 %collective-permute-start.55 = (f32[1296,768]{1,0:T(8,128)}, f32[1296,768]{1,0:T(8,128)}, u32[]{:S(2)}, u32[]{:S(2)}) collective-permute-start(f32[1296,768]{1,0:T(8,128)} %get-tuple-element.209), channel_id=1, source_target_pairs={{0,1},{1,0},{2,3},{3,2},{4,5},{5,4},{6,7},{7,6},{8,9},{9,8},{10,11... | collective-permute-start | bytes 11943944 | tf_op jit(solution)/shard_map/ppermute | solution.py:452
  467.0 30.3 %collective-permute-start.49 = (f32[384,768]{1,0:T(8,128)}, f32[384,768]{1,0:T(8,128)}, u32[]{:S(2)}, u32[]{:S(2)}) collective-permute-start(f32[384,768]{1,0:T(8,128)} %get-tuple-element.202.refs_0_), channel_id=1, source_target_pairs={{0,8},{8,0},{1,9},{9,1},{2,10},{10,2},{3,11},{11,3},{4,12},{12,4},... | collective-permute-start | bytes 3538952 | tf_op jit(solution)/shard_map/ppermute | solution.py:452
  471.2 38.3 %collective-permute-start.60 = (f32[624,768]{1,0:T(8,128)}, f32[624,768]{1,0:T(8,128)S(1)}, u32[]{:S(2)}, u32[]{:S(2)}) collective-permute-start(f32[624,768]{1,0:T(8,128)} %collective-permute-done.44.refs_6_), channel_id=1, source_target_pairs={{0,1},{1,0},{2,3},{3,2},{4,5},{5,4},{6,7},{7,6},{8,9},{9,8},{10,11... | collective-permute-start | bytes 5750792 | tf_op jit(solution)/shard_map/ppermute | solution.py:452
  473.6 36.5 %collective-permute-start.61 = (f32[624,768]{1,0:T(8,128)}, f32[624,768]{1,0:T(8,128)}, u32[]{:S(2)}, u32[]{:S(2)}) collective-permute-start(f32[624,768]{1,0:T(8,128)} %collective-permute-done.45.refs_7_), channel_id=1, source_target_pairs={{0,1},{1,0},{2,3},{3,2},{4,5},{5,4},{6,7},{7,6},{8,9},{9,8},{10,11... | collective-permute-start | bytes 5750792 | tf_op jit(solution)/shard_map/ppermute | solution.py:452
  475.2 41.5 %collective-permute-start.58 = (f32[624,768]{1,0:T(8,128)}, f32[624,768]{1,0:T(8,128)}, u32[]{:S(2)}, u32[]{:S(2)}) collective-permute-start(f32[624,768]{1,0:T(8,128)} %collective-permute-done.56.refs_2_), channel_id=1, source_target_pairs={{0,1},{1,0},{2,3},{3,2},{4,5},{5,4},{6,7},{7,6},{8,9},{9,8},{10,11... | collective-permute-start | bytes 5750792 | tf_op jit(solution)/shard_map/ppermute | solution.py:452
  497.3 19.4 %collective-permute-start.59 = (f32[624,768]{1,0:T(8,128)}, f32[624,768]{1,0:T(8,128)}, u32[]{:S(2)}, u32[]{:S(2)}) collective-permute-start(f32[624,768]{1,0:T(8,128)} %collective-permute-done.57.refs_3_), channel_id=1, source_target_pairs={{0,1},{1,0},{2,3},{3,2},{4,5},{5,4},{6,7},{7,6},{8,9},{9,8},{10,11... | collective-permute-start | bytes 5750792 | tf_op jit(solution)/shard_map/ppermute | solution.py:452
  (62 other events, 636.9 us)

commit v4 on v3

--- a/solution.py
+++ b/solution.py
@@ -630,25 +630,25 @@
         sums = [acc] + [swap(acc, m) for m in range(1, n_groups)]
         db_rel = [db_mine] + [swap(db_mine, m) for m in (1, 2, 3)]
         out, got0, dl0 = local_rows(out, 0, near2 + far0)
-        sums, out = after((sums, out))
+        d_hidden = jnp.einsum("clt,cle->cte", pos_onehot, d_masked.reshape(n_rows, SLOTS, width), preferred_element_type=F32).astype(BF16)
+        sums, out, d_hidden = after((sums, out, d_hidden))
         w_half, small = join_pieces(sums, ranks, hw)
         w_half, out = after((w_half, out))
         w_other = swap(w_half, 1, "vp")
-        out, rx2, ry2, d_masked, db_rel = after((out, rx2, ry2, d_masked, db_rel))
+        out, rx2, ry2, db_rel = after((out, rx2, ry2, db_rel))
         far2 = far(2, rx2, ry2)
         db_sh = jnp.stack(db_rel, 1).reshape(2, 2, 2, 16 * nx)
         db_sh = jnp.where(par == 1, jnp.flip(db_sh, 1), db_sh)
         db_sh = jnp.where(core == 1, jnp.flip(db_sh, 2), db_sh).reshape(2 * 4 * 16 * nx)
         out, got1, dl1 = local_rows(out, 1, near3 + far1 + far2[:2] + [got0])
-        out, rx3, ry3 = after((out, rx3, ry3))
+        d_w_trans = gather_pieces([w_half, w_other], jnp.stack([plane, 1 - plane]).astype(I32)).reshape(width, width)
+        out, rx3, ry3, d_w_trans = after((out, rx3, ry3, d_w_trans))
         far3 = far(3, rx3, ry3)
         dl_mine = jnp.concatenate([dl0, dl1]).reshape(16 * nl)
         dl_other = swap(dl_mine, 1)
-        d_hidden = jnp.einsum("clt,cle->cte", pos_onehot, d_masked.reshape(n_rows, SLOTS, width), preferred_element_type=F32).astype(BF16)
         put = lambda out, items: copy_rows(out, [a for a, _ in items], [s[:1] for _, s in items])
         out = put(out, far2[2:] + far3[:2])
         d_emb_table = put(out, [got1] + far3[2:])
-        d_w_trans = gather_pieces([w_half, w_other], jnp.stack([plane, 1 - plane]).astype(I32)).reshape(width, width)
         mlm_loss = small[3, 0]
         d_b_vocab = jnp.concatenate([db_sh, jnp.where(core == 0, dl_mine, dl_other), jnp.where(core == 0, dl_other, dl_mine)])
         return mlm_loss, d_hidden, d_w_trans, small[0], small[1], small[2], d_emb_table, d_b_vocab

time: 530 us -> 525 us (level)
  transfers between devices with their start and end apart: 63 -> 63, of which waited for: 27 -> 23; matrix products, arithmetic and copies ran while one was open for 6% -> 6% of each run, Pallas kernels for 47% -> 47%
where the time goes in v4:
time: 525 us; the launch traced here: 517 us
  Pallas kernels  288 us (55%)
  waiting for transfers between devices  134 us (26%)
  starting transfers between devices  44.6 us (8%)
  local copies, waits for them, and re-layouts  38.4 us (7%)
  other arithmetic  5.53 us (1%)
    pallas_call x6, Pallas kernels, emb_rows(): pl.pallas_call(functools.partial(rows_kernel, cfg), grid_spec=pltpu.Prefe...  167 us
    ppermute x63, waiting for transfers between devices, swap(): return lax.ppermute(x, axis, [(i, i ^ mask) for i in range(n)])  134 us
    pallas_call x2, Pallas kernels, own_call(): pl.pallas_call(functools.partial(own_kernel, end - begin, first), grid=(e...  74.9 us
    ppermute x63, starting transfers between devices, swap(): return lax.ppermute(x, axis, [(i, i ^ mask) for i in range(n)])  44.6 us
    unnamed x91, local copies, waits for them, and re-layouts  13.3 us
    pallas_call x2, Pallas kernels, copy_rows(): pl.pallas_call(functools.partial(copy_kernel, n), grid_spec=pltpu.Prefetc...  11.8 us
    gather x1, local copies, waits for them, and re-layouts, local_step(): jnp.take(emb_table, jnp.where((lab_local >= 0) & (lab_local < shard_rows)...  11 us
  transfers between devices with their start and end apart: 63, of which 23 were waited for; matrix products, arithmetic and copies ran while one was open for 6% of the time, Pallas kernels for 47%

profile of v4, /device:TPU:0, one launch (start us, length us, event | category | flops | bytes accessed | tf_op | source)
XLA Modules:
  0.0 517.4 jit_solution(16091933325030865711)
XLA Ops:
  4.7 9.3 %shard_map.161 = (bf16[640,768]{1,0:T(8,128)(2,1)S(1)}, f32[640,768]{1,0:T(8,128)S(1)}, bf16[640,768]{1,0:T(8,128)(2,1)S(1)}, f32[640,768]{1,0:T(8,128)}) custom-call(bf16[8,512,768]{2,1,0:T(8,128)(2,1)} %hid_ref.1, f32[8,1,128]{2,1,0:T(1,128)S(1)} %bitcast.65, bf16[768,768]{1,0:T(8,128)(2,1)S(1)} %copy-done, f32[3,768]{1,0:T(4,128)S(1)} %pad_maximum_fusion.3.vec_ref), custom_call_target="tpu_custom_call" | custom-call | flops 1258291200 | bytes 6291456 | tf_op jit(solution)/shard_map/pallas_call | solution.py:475
  17.2 3.2 collective-permute-start
  20.4 1.5 collective-permute-start.1
  24.3 45.9 %shard_map.162 = (f32[640,768]{1,0:T(8,128)}, f32[3,640,128]{2,1,0:T(8,128)}) custom-call(bf16[640,768]{1,0:T(8,128)(2,1)} %copy-done.2, bf16[25152,768]{1,0:T(8,128)(2,1)} %emb_ref.15, f32[11,1,2304]{2,1,0:T(1,128)} %reshape.115.bias_ref, f32[11,1,2304]{2,1,0:T(1,128)} %reshape.116.col_ref, f32[1,640]{1,0:T(1,128)} %convert_element_type.26.lab_row_ref.lab_ref), custom_call_target="tpu_custom_call" | custom-call | flops 7927234560 | bytes 24772608 | tf_op jit(solution)/shard_map/pallas_call | solution.py:509
  70.3 2.2 slice.74
  74.3 29.0 %shard_map.163 = (f32[640,768]{1,0:T(8,128)}, f32[8,640]{1,0:T(8,128)}) custom-call(bf16[640,768]{1,0:T(8,128)(2,1)} %copy-done.2, bf16[25152,768]{1,0:T(8,128)(2,1)} %emb_ref.15, f32[11,1,2304]{2,1,0:T(1,128)} %reshape.115.bias_ref, f32[11,1,2304]{2,1,0:T(1,128)} %reshape.116.col_ref, f32[1,640]{1,0:T(1,128)} %convert_element_type.26.lab_row_ref.lab_ref, ...), custom_call_target="tpu_custom_call" | custom-call | flops 4529848320 | bytes 14155776 | tf_op jit(solution)/shard_map/pallas_call | solution.py:509
  103.3 2.1 collective-permute-start.4
  105.4 2.0 collective-permute-done.4.other_ref
  109.5 3.0 collective-permute-done.11.refs_1_
  114.0 11.0 %gather_fusion = bf16[640,768]{1,0:T(8,128)(2,1)} fusion(bf16[25152,768]{1,0:T(8,128)(2,1)} %emb_ref.15, s32[1024]{0:T(1024)S(1)} %pad_clamp_fusion), kind=kCustom, calls=%fused_computation | custom fusion | bytes 1968640 | tf_op jit(solution)/shard_map/jit(_take)/gather | solution.py:532
  125.1 1.9 collective-permute-start.14
  128.4 2.9 collective-permute-start.16
  133.9 1.5 copy-done.6
  138.6 2.1 shard_map.167
  140.8 1.5 copy-done.3
  142.3 1.5 copy-done.5
  143.8 8.8 %shard_map.166.u_ref = bf16[5120,768]{1,0:T(8,128)(2,1)} custom-call(s32[10]{0:T(128)S(1)} %pad_add_fusion.2.start_ref, f32[640,768]{1,0:T(8,128)S(1)} %copy-done.3, f32[640,768]{1,0:T(8,128)S(1)} %copy-done.5, f32[640,768]{1,0:T(8,128)} %collective-permute-done.refs_2_, f32[640,768]{1,0:T(8,128)} %collective-permute-done.7.refs_3_, ...), custom_call_target="tpu_custom_call" | custom-call | flops 1000000000 | bytes 23592960 | tf_op jit(solution)/shard_map/pallas_call | solution.py:220
  152.6 27.3 %shard_map.168 = (f32[25152,768]{1,0:T(8,128)}, f32[2,1,640]{2,1,0:T(1,128)S(1)}, f32[624,768]{1,0:T(8,128)}, f32[624,768]{1,0:T(8,128)}) custom-call(s32[4]{0:T(128)S(1)} %pad_add_fusion.4.start_ref, bf16[25152,768]{1,0:T(8,128)(2,1)} %emb_ref.15, f32[32,1,640]{2,1,0:T(1,128)S(1)} %broadcast_in_dim.139.bias_ref, bf16[5120,768]{1,0:T(8,128)(2,1)} %shard_map.166.u_ref, ...), custom_call_target="tpu_custom_call" | custom-call | flops 1226833920 | bytes 9584640 | tf_op jit(solution)/shard_map/pallas_call | solution.py:395
  180.0 1.5 collective-permute-start.22
  181.5 1.5 collective-permute-start.23
  183.3 27.8 %shard_map.169 = (f32[25152,768]{1,0:T(8,128)}, f32[2,1,640]{2,1,0:T(1,128)S(1)}, f32[624,768]{1,0:T(8,128)}, f32[624,768]{1,0:T(8,128)}) custom-call(s32[4]{0:T(128)S(1)} %pad_add_fusion.1.start_ref, bf16[25152,768]{1,0:T(8,128)(2,1)} %emb_ref.15, f32[32,1,640]{2,1,0:T(1,128)S(1)} %broadcast_in_dim.139.bias_ref, ...), custom_call_target="tpu_custom_call", output_to_operand_aliasing={{0}: (6, {})} | custom-call | flops 1226833920 | bytes 9584640 | tf_op jit(solution)/shard_map/pallas_call | solution.py:395
  211.2 5.1 shard_map.170
  218.2 10.4 %collective-permute-done.27 = f32[56,768]{1,0:T(8,128)S(1)} collective-permute-done((f32[56,768]{1,0:T(8,128)S(1)}, f32[56,768]{1,0:T(8,128)S(1)}, u32[]{:S(2)}, u32[]{:S(2)}) %collective-permute-start.27) | collective-permute-done | bytes 172064 | tf_op jit(solution)/shard_map/ppermute | solution.py:452
  230.1 1.8 collective-permute-done.28
  231.8 2.7 collective-permute-done.29
  234.5 4.8 collective-permute-start.31
  241.0 3.0 collective-permute-done.31
  243.9 4.0 collective-permute-done.32
  251.2 27.3 %shard_map.171 = (f32[25152,768]{1,0:T(8,128)}, f32[2,1,640]{2,1,0:T(1,128)S(1)}, f32[624,768]{1,0:T(8,128)}, f32[624,768]{1,0:T(8,128)}) custom-call(s32[4]{0:T(128)S(1)} %pad_add_fusion.7.start_ref, bf16[25152,768]{1,0:T(8,128)(2,1)} %emb_ref.15, f32[32,1,640]{2,1,0:T(1,128)S(1)} %broadcast_in_dim.139.bias_ref, ...), custom_call_target="tpu_custom_call", output_to_operand_aliasing={{0}: (6, {})} | custom-call | flops 1226833920 | bytes 9584640 | tf_op jit(solution)/shard_map/pallas_call | solution.py:395
  279.1 13.3 %collective-permute-done.24.refs_2_ = f32[624,768]{1,0:T(8,128)S(1)} collective-permute-done((f32[624,768]{1,0:T(8,128)}, f32[624,768]{1,0:T(8,128)S(1)}, u32[]{:S(2)}, u32[]{:S(2)}) %collective-permute-start.24) | collective-permute-done | bytes 1916960 | tf_op jit(solution)/shard_map/ppermute | solution.py:452
  293.0 1.5 copy-done.10
  294.5 27.7 %shard_map.172 = (f32[25152,768]{1,0:T(8,128)}, f32[2,1,640]{2,1,0:T(1,128)S(1)}, f32[624,768]{1,0:T(8,128)}, f32[624,768]{1,0:T(8,128)}) custom-call(s32[8]{0:T(128)S(1)} %concatenate.78.start_ref, bf16[25152,768]{1,0:T(8,128)(2,1)} %emb_ref.15, f32[32,1,640]{2,1,0:T(1,128)S(1)} %broadcast_in_dim.139.bias_ref, ...), custom_call_target="tpu_custom_call", output_to_operand_aliasing={{0}: (10, {})} | custom-call | flops 1226833920 | bytes 9584640 | tf_op jit(solution)/shard_map/pallas_call | solution.py:395
  324.0 28.5 %shard_map.173 = (f32[25152,768]{1,0:T(8,128)}, f32[3,1,512]{2,1,0:T(1,128)S(1)}, f32[1296,768]{1,0:T(8,128)}) custom-call(s32[12]{0:T(128)S(1)} %concatenate.83.start_ref, bf16[25152,768]{1,0:T(8,128)(2,1)} %emb_ref.15, f32[12,1,512]{2,1,0:T(1,128)S(1)} %broadcast_in_dim.157.bias_ref, ...), custom_call_target="tpu_custom_call", output_to_operand_aliasing={{0}: (12, {})} | custom-call | flops 1274019840 | bytes 9953280 | tf_op jit(solution)/shard_map/pallas_call | solution.py:395
  355.2 4.8 collective-permute-done.50
  360.5 36.9 %collective-permute-done.51 = f32[2,2496]{1,0:T(2,128)S(1)} collective-permute-done((f32[2,2496]{1,0:T(2,128)S(1)}, f32[2,2496]{1,0:T(2,128)S(1)}, u32[]{:S(2)}, u32[]{:S(2)}) %collective-permute-start.51) | collective-permute-done | bytes 20000 | tf_op jit(solution)/shard_map/ppermute | solution.py:452
  397.4 3.2 collective-permute-done.52
  401.3 6.5 %collective-permute-done.34.refs_2_ = f32[56,768]{1,0:T(8,128)S(1)} collective-permute-done((f32[56,768]{1,0:T(8,128)S(1)}, f32[56,768]{1,0:T(8,128)S(1)}, u32[]{:S(2)}, u32[]{:S(2)}) %collective-permute-start.34) | collective-permute-done | bytes 172064 | tf_op jit(solution)/shard_map/ppermute | solution.py:452
  410.1 6.4 %collective-permute-done.36.refs_4_ = f32[56,768]{1,0:T(8,128)S(1)} collective-permute-done((f32[56,768]{1,0:T(8,128)S(1)}, f32[56,768]{1,0:T(8,128)S(1)}, u32[]{:S(2)}, u32[]{:S(2)}) %collective-permute-start.36) | collective-permute-done | bytes 172064 | tf_op jit(solution)/shard_map/ppermute | solution.py:452
  417.4 1.9 collective-permute-start.39
  419.4 4.8 collective-permute-done.38.refs_6_
  427.1 4.6 convolution_convert_fusion
  431.8 3.4 shard_map.174
  436.5 28.6 %shard_map.175 = (f32[25152,768]{1,0:T(8,128)}, f32[3,1,512]{2,1,0:T(1,128)S(1)}, f32[1296,768]{1,0:T(8,128)}) custom-call(s32[15]{0:T(128)S(1)} %concatenate.84.start_ref, bf16[25152,768]{1,0:T(8,128)(2,1)} %emb_ref.15, f32[12,1,512]{2,1,0:T(1,128)S(1)} %broadcast_in_dim.157.bias_ref, ...), custom_call_target="tpu_custom_call", output_to_operand_aliasing={{0}: (15, {})} | custom-call | flops 1274019840 | bytes 9953280 | tf_op jit(solution)/shard_map/pallas_call | solution.py:395
  465.3 3.4 collective-permute-start.56
  469.7 25.8 %collective-permute-done.56.refs_1_ = f32[384,768]{1,0:T(8,128)S(1)} collective-permute-done((f32[384,768]{1,0:T(8,128)}, f32[384,768]{1,0:T(8,128)S(1)}, u32[]{:S(2)}, u32[]{:S(2)}) %collective-permute-start.56) | collective-permute-done | bytes 1179680 | tf_op jit(solution)/shard_map/ppermute | solution.py:452
  496.5 3.8 shard_map.176
  504.6 5.9 %shard_map.177.refs_3_ = f32[25152,768]{1,0:T(8,128)} custom-call(s32[4]{0:T(128)S(1)} %pad_add_fusion.10.start_ref, f32[624,768]{1,0:T(8,128)S(1)} %collective-permute-done.60.refs_0_, f32[624,768]{1,0:T(8,128)} %collective-permute-done.61.refs_1_, f32[624,768]{1,0:T(8,128)} %collective-permute-done.54.refs_2_, ...), custom_call_target="tpu_custom_call", output_to_operand_aliasing={{}: (5, {})} | custom-call | flops 1000000000 | bytes 15335424 | tf_op jit(solution)/shard_map/pallas_call | solution.py:434
  511.3 5.9 %shard_map.178 = f32[25152,768]{1,0:T(8,128)} custom-call(s32[3]{0:T(128)S(1)} %pad_add_fusion.9.start_ref, f32[1296,768]{1,0:T(8,128)} %collective-permute-done.57.refs_0_, f32[624,768]{1,0:T(8,128)} %collective-permute-done.58.refs_1_, f32[624,768]{1,0:T(8,128)} %collective-permute-done.59.refs_2_, ...), custom_call_target="tpu_custom_call", output_to_operand_aliasing={{}: (4, {})} | custom-call | flops 1000000000 | bytes 15630336 | tf_op jit(solution)/shard_map/pallas_call | solution.py:434
  (276 shorter events, 52.2 us)
Async XLA Ops:
  17.2 53.1 %collective-permute-start = (f32[640,768]{1,0:T(8,128)}, f32[640,768]{1,0:T(8,128)}, u32[]{:S(2)}, u32[]{:S(2)}) collective-permute-start(f32[640,768]{1,0:T(8,128)} %get-tuple-element.117.refs_0_), channel_id=1, source_target_pairs={{0,2},{1,3},{2,0},{3,1},{4,6},{5,7},{6,4},{7,5},{8,10},{9,11},{10,... | collective-permute-start | bytes 5898248 | tf_op jit(solution)/shard_map/ppermute | solution.py:452
  20.4 49.9 %collective-permute-start.1 = (f32[640,768]{1,0:T(8,128)}, f32[640,768]{1,0:T(8,128)}, u32[]{:S(2)}, u32[]{:S(2)}) collective-permute-start(f32[640,768]{1,0:T(8,128)} %get-tuple-element.117.refs_0_), channel_id=1, source_target_pairs={{0,4},{1,5},{2,6},{3,7},{4,0},{5,1},{6,2},{7,3},{8,12},{9,13},{10,... | collective-permute-start | bytes 5898248 | tf_op jit(solution)/shard_map/ppermute | solution.py:452
  21.9 87.5 %collective-permute-start.6 = (f32[640,768]{1,0:T(8,128)}, f32[640,768]{1,0:T(8,128)S(1)}, u32[]{:S(2)}, u32[]{:S(2)}) collective-permute-start(f32[640,768]{1,0:T(8,128)} %get-tuple-element.117.refs_0_), channel_id=1, source_target_pairs={{0,1},{1,0},{2,3},{3,2},{4,5},{5,4},{6,7},{7,6},{8,9},{9,8},{10,11... | collective-permute-start | bytes 5898248 | tf_op jit(solution)/shard_map/ppermute | solution.py:452
  72.5 52.6 %collective-permute-start.2 = (f32[320,768]{1,0:T(8,128)}, f32[320,768]{1,0:T(8,128)}, u32[]{:S(2)}, u32[]{:S(2)}) collective-permute-start(f32[320,768]{1,0:T(8,128)} %slice.74), channel_id=1, source_target_pairs={{0,4},{1,5},{2,6},{3,7},{4,0},{5,1},{6,2},{7,3},{8,12},{9,13},{10,... | collective-permute-start | bytes 2949128 | tf_op jit(solution)/shard_map/ppermute | solution.py:452
  74.2 52.8 %collective-permute-start.3 = (f32[320,768]{1,0:T(8,128)S(1)}, f32[320,768]{1,0:T(8,128)}, u32[]{:S(2)}, u32[]{:S(2)}) collective-permute-start(f32[320,768]{1,0:T(8,128)S(1)} %slice.75), channel_id=1, source_target_pairs={{0,2},{1,3},{2,0},{3,1},{4,6},{5,7},{6,4},{7,5},{8,10},{9,11},{10,... | collective-permute-start | bytes 2949128 | tf_op jit(solution)/shard_map/ppermute | solution.py:452
  105.4 35.3 %collective-permute-start.7 = (f32[640,768]{1,0:T(8,128)}, f32[640,768]{1,0:T(8,128)}, u32[]{:S(2)}, u32[]{:S(2)}) collective-permute-start(f32[640,768]{1,0:T(8,128)} %collective-permute-done.refs_2_), channel_id=1, source_target_pairs={{0,1},{1,0},{2,3},{3,2},{4,5},{5,4},{6,7},{7,6},{8,9},{9,8},{10,11... | collective-permute-start | bytes 5898248 | tf_op jit(solution)/shard_map/ppermute | solution.py:452
  107.4 33.4 %collective-permute-start.8 = (f32[640,768]{1,0:T(8,128)}, f32[640,768]{1,0:T(8,128)}, u32[]{:S(2)}, u32[]{:S(2)}) collective-permute-start(f32[640,768]{1,0:T(8,128)} %collective-permute-done.1.refs_4_), channel_id=1, source_target_pairs={{0,1},{1,0},{2,3},{3,2},{4,5},{5,4},{6,7},{7,6},{8,9},{9,8},{10,11... | collective-permute-start | bytes 5898248 | tf_op jit(solution)/shard_map/ppermute | solution.py:452
  112.5 12.5 %collective-permute-start.12 = (f32[2,640]{1,0:T(2,128)}, f32[2,640]{1,0:T(2,128)S(1)}, u32[]{:S(2)}, u32[]{:S(2)}) collective-permute-start(f32[2,640]{1,0:T(2,128)} %get-tuple-element.131.refs_0_), channel_id=1, source_target_pairs={{0,2},{1,3},{2,0},{3,1},{4,6},{5,7},{6,4},{7,5},{8,10},{9,11},{10,... | collective-permute-start | bytes 15368 | tf_op jit(solution)/shard_map/ppermute | solution.py:452
  131.3 9.4 %collective-permute-start.10 = (f32[320,768]{1,0:T(8,128)}, f32[320,768]{1,0:T(8,128)}, u32[]{:S(2)}, u32[]{:S(2)}) collective-permute-start(f32[320,768]{1,0:T(8,128)} %collective-permute-done.3.refs_7_), channel_id=1, source_target_pairs={{0,1},{1,0},{2,3},{3,2},{4,5},{5,4},{6,7},{7,6},{8,9},{9,8},{10,11... | collective-permute-start | bytes 2949128 | tf_op jit(solution)/shard_map/ppermute | solution.py:452
  131.4 9.3 %collective-permute-start.9 = (f32[320,768]{1,0:T(8,128)}, f32[320,768]{1,0:T(8,128)}, u32[]{:S(2)}, u32[]{:S(2)}) collective-permute-start(f32[320,768]{1,0:T(8,128)} %collective-permute-done.2.refs_6_), channel_id=1, source_target_pairs={{0,1},{1,0},{2,3},{3,2},{4,5},{5,4},{6,7},{7,6},{8,9},{9,8},{10,11... | collective-permute-start | bytes 2949128 | tf_op jit(solution)/shard_map/ppermute | solution.py:452
  136.9 74.2 %collective-permute-start.5 = (f32[640,768]{1,0:T(8,128)S(1)}, f32[640,768]{1,0:T(8,128)}, u32[]{:S(2)}, u32[]{:S(2)}) collective-permute-start(f32[640,768]{1,0:T(8,128)S(1)} %shard_map.165.mine_ref), channel_id=1, source_target_pairs={{0,8},{8,0},{1,9},{9,1},{2,10},{10,2},{3,11},{11,3},{4,12},{12,4},... | collective-permute-start | bytes 5898248 | tf_op jit(solution)/shard_map/ppermute | solution.py:452
  180.0 68.0 %collective-permute-start.22 = (f32[624,768]{1,0:T(8,128)}, f32[624,768]{1,0:T(8,128)}, u32[]{:S(2)}, u32[]{:S(2)}) collective-permute-start(f32[624,768]{1,0:T(8,128)} %get-tuple-element.150), channel_id=1, source_target_pairs={{0,2},{1,3},{2,0},{3,1},{4,6},{5,7},{6,4},{7,5},{8,10},{9,11},{10,... | collective-permute-start | bytes 5750792 | tf_op jit(solution)/shard_map/ppermute | solution.py:452
  181.5 66.9 %collective-permute-start.23 = (f32[624,768]{1,0:T(8,128)}, f32[624,768]{1,0:T(8,128)}, u32[]{:S(2)}, u32[]{:S(2)}) collective-permute-start(f32[624,768]{1,0:T(8,128)} %get-tuple-element.151), channel_id=1, source_target_pairs={{0,4},{1,5},{2,6},{3,7},{4,0},{5,1},{6,2},{7,3},{8,12},{9,13},{10,... | collective-permute-start | bytes 5750792 | tf_op jit(solution)/shard_map/ppermute | solution.py:452
  216.3 32.3 %collective-permute-start.20 = (f32[624,768]{1,0:T(8,128)}, f32[624,768]{1,0:T(8,128)S(1)}, u32[]{:S(2)}, u32[]{:S(2)}) collective-permute-start(f32[624,768]{1,0:T(8,128)} %get-tuple-element.152), channel_id=1, source_target_pairs={{0,1},{1,0},{2,3},{3,2},{4,5},{5,4},{6,7},{7,6},{8,9},{9,8},{10,11... | collective-permute-start | bytes 5750792 | tf_op jit(solution)/shard_map/ppermute | solution.py:452
  216.8 11.8 %collective-permute-start.27 = (f32[56,768]{1,0:T(8,128)S(1)}, f32[56,768]{1,0:T(8,128)S(1)}, u32[]{:S(2)}, u32[]{:S(2)}) collective-permute-start(f32[56,768]{1,0:T(8,128)S(1)} %get-tuple-element.163), channel_id=1, source_target_pairs={{0,2},{1,3},{2,0},{3,1},{4,6},{5,7},{6,4},{7,5},{8,10},{9,11},{10,... | collective-permute-start | bytes 516104 | tf_op jit(solution)/shard_map/ppermute | solution.py:452
  217.7 14.2 %collective-permute-start.28 = (f32[56,768]{1,0:T(8,128)S(1)}, f32[56,768]{1,0:T(8,128)S(1)}, u32[]{:S(2)}, u32[]{:S(2)}) collective-permute-start(f32[56,768]{1,0:T(8,128)S(1)} %get-tuple-element.164), channel_id=1, source_target_pairs={{0,3},{1,2},{2,1},{3,0},{4,7},{5,6},{6,5},{7,4},{8,11},{9,10},{10,... | collective-permute-start | bytes 516104 | tf_op jit(solution)/shard_map/ppermute | solution.py:452
  231.8 8.6 %collective-permute-start.30 = (f32[56,768]{1,0:T(8,128)S(1)}, f32[56,768]{1,0:T(8,128)S(1)}, u32[]{:S(2)}, u32[]{:S(2)}) collective-permute-start(f32[56,768]{1,0:T(8,128)S(1)} %get-tuple-element.166), channel_id=1, source_target_pairs={{0,5},{1,4},{2,7},{3,6},{4,1},{5,0},{6,3},{7,2},{8,13},{9,12},{10,... | collective-permute-start | bytes 516104 | tf_op jit(solution)/shard_map/ppermute | solution.py:452
  234.5 9.4 %collective-permute-start.31 = (f32[56,768]{1,0:T(8,128)S(1)}, f32[56,768]{1,0:T(8,128)S(1)}, u32[]{:S(2)}, u32[]{:S(2)}) collective-permute-start(f32[56,768]{1,0:T(8,128)S(1)} %get-tuple-element.167), channel_id=1, source_target_pairs={{0,6},{1,7},{2,4},{3,5},{4,2},{5,3},{6,0},{7,1},{8,14},{9,15},{10,... | collective-permute-start | bytes 516104 | tf_op jit(solution)/shard_map/ppermute | solution.py:452
  243.9 34.6 %collective-permute-start.21 = (f32[624,768]{1,0:T(8,128)}, f32[624,768]{1,0:T(8,128)}, u32[]{:S(2)}, u32[]{:S(2)}) collective-permute-start(f32[624,768]{1,0:T(8,128)} %get-tuple-element.153), channel_id=1, source_target_pairs={{0,1},{1,0},{2,3},{3,2},{4,5},{5,4},{6,7},{7,6},{8,9},{9,8},{10,11... | collective-permute-start | bytes 5750792 | tf_op jit(solution)/shard_map/ppermute | solution.py:452
  247.9 30.6 %collective-permute-start.18 = (f32[624,768]{1,0:T(8,128)}, f32[624,768]{1,0:T(8,128)}, u32[]{:S(2)}, u32[]{:S(2)}) collective-permute-start(f32[624,768]{1,0:T(8,128)} %get-tuple-element.150), channel_id=1, source_target_pairs={{0,1},{1,0},{2,3},{3,2},{4,5},{5,4},{6,7},{7,6},{8,9},{9,8},{10,11... | collective-permute-start | bytes 5750792 | tf_op jit(solution)/shard_map/ppermute | solution.py:452
  248.0 31.1 %collective-permute-start.19 = (f32[624,768]{1,0:T(8,128)}, f32[624,768]{1,0:T(8,128)}, u32[]{:S(2)}, u32[]{:S(2)}) collective-permute-start(f32[624,768]{1,0:T(8,128)} %get-tuple-element.151), channel_id=1, source_target_pairs={{0,1},{1,0},{2,3},{3,2},{4,5},{5,4},{6,7},{7,6},{8,9},{9,8},{10,11... | collective-permute-start | bytes 5750792 | tf_op jit(solution)/shard_map/ppermute | solution.py:452
  248.5 44.0 %collective-permute-start.24 = (f32[624,768]{1,0:T(8,128)}, f32[624,768]{1,0:T(8,128)S(1)}, u32[]{:S(2)}, u32[]{:S(2)}) collective-permute-start(f32[624,768]{1,0:T(8,128)} %get-tuple-element.152), channel_id=1, source_target_pairs={{0,2},{1,3},{2,0},{3,1},{4,6},{5,7},{6,4},{7,5},{8,10},{9,11},{10,... | collective-permute-start | bytes 5750792 | tf_op jit(solution)/shard_map/ppermute | solution.py:452
  249.9 72.5 %collective-permute-start.25 = (f32[624,768]{1,0:T(8,128)}, f32[624,768]{1,0:T(8,128)}, u32[]{:S(2)}, u32[]{:S(2)}) collective-permute-start(f32[624,768]{1,0:T(8,128)} %get-tuple-element.153), channel_id=1, source_target_pairs={{0,4},{1,5},{2,6},{3,7},{4,0},{5,1},{6,2},{7,3},{8,12},{9,13},{10,... | collective-permute-start | bytes 5750792 | tf_op jit(solution)/shard_map/ppermute | solution.py:452
  278.5 45.4 %collective-permute-start.40 = (f32[624,768]{1,0:T(8,128)}, f32[624,768]{1,0:T(8,128)}, u32[]{:S(2)}, u32[]{:S(2)}) collective-permute-start(f32[624,768]{1,0:T(8,128)} %get-tuple-element.202), channel_id=1, source_target_pairs={{0,1},{1,0},{2,3},{3,2},{4,5},{5,4},{6,7},{7,6},{8,9},{9,8},{10,11... | collective-permute-start | bytes 5750792 | tf_op jit(solution)/shard_map/ppermute | solution.py:452
  278.6 45.4 %collective-permute-start.41 = (f32[624,768]{1,0:T(8,128)}, f32[624,768]{1,0:T(8,128)}, u32[]{:S(2)}, u32[]{:S(2)}) collective-permute-start(f32[624,768]{1,0:T(8,128)} %get-tuple-element.203), channel_id=1, source_target_pairs={{0,1},{1,0},{2,3},{3,2},{4,5},{5,4},{6,7},{7,6},{8,9},{9,8},{10,11... | collective-permute-start | bytes 5750792 | tf_op jit(solution)/shard_map/ppermute | solution.py:452
  279.1 44.9 %collective-permute-start.42 = (f32[624,768]{1,0:T(8,128)}, f32[624,768]{1,0:T(8,128)}, u32[]{:S(2)}, u32[]{:S(2)}) collective-permute-start(f32[624,768]{1,0:T(8,128)} %collective-permute-done.22.refs_2_), channel_id=1, source_target_pairs={{0,1},{1,0},{2,3},{3,2},{4,5},{5,4},{6,7},{7,6},{8,9},{9,8},{10,11... | collective-permute-start | bytes 5750792 | tf_op jit(solution)/shard_map/ppermute | solution.py:452
  292.4 31.6 %collective-permute-start.43 = (f32[624,768]{1,0:T(8,128)}, f32[624,768]{1,0:T(8,128)}, u32[]{:S(2)}, u32[]{:S(2)}) collective-permute-start(f32[624,768]{1,0:T(8,128)} %collective-permute-done.23.refs_3_), channel_id=1, source_target_pairs={{0,1},{1,0},{2,3},{3,2},{4,5},{5,4},{6,7},{7,6},{8,9},{9,8},{10,11... | collective-permute-start | bytes 5750792 | tf_op jit(solution)/shard_map/ppermute | solution.py:452
  352.5 84.0 %collective-permute-start.53 = (f32[1296,768]{1,0:T(8,128)}, f32[1296,768]{1,0:T(8,128)}, u32[]{:S(2)}, u32[]{:S(2)}) collective-permute-start(f32[1296,768]{1,0:T(8,128)} %get-tuple-element.207), channel_id=1, source_target_pairs={{0,1},{1,0},{2,3},{3,2},{4,5},{5,4},{6,7},{7,6},{8,9},{9,8},{10,11... | collective-permute-start | bytes 11943944 | tf_op jit(solution)/shard_map/ppermute | solution.py:452
  353.0 73.3 %collective-permute-start.48 = (f32[624,768]{1,0:T(8,128)}, f32[624,768]{1,0:T(8,128)}, u32[]{:S(2)}, u32[]{:S(2)}) collective-permute-start(f32[624,768]{1,0:T(8,128)} %get-tuple-element.202), channel_id=1, source_target_pairs={{0,2},{1,3},{2,0},{3,1},{4,6},{5,7},{6,4},{7,5},{8,10},{9,11},{10,... | collective-permute-start | bytes 5750792 | tf_op jit(solution)/shard_map/ppermute | solution.py:452
  353.6 72.8 %collective-permute-start.49 = (f32[624,768]{1,0:T(8,128)}, f32[624,768]{1,0:T(8,128)}, u32[]{:S(2)}, u32[]{:S(2)}) collective-permute-start(f32[624,768]{1,0:T(8,128)} %get-tuple-element.203), channel_id=1, source_target_pairs={{0,4},{1,5},{2,6},{3,7},{4,0},{5,1},{6,2},{7,3},{8,12},{9,13},{10,... | collective-permute-start | bytes 5750792 | tf_op jit(solution)/shard_map/ppermute | solution.py:452
  354.7 46.6 %collective-permute-start.33 = (f32[56,768]{1,0:T(8,128)S(1)}, f32[56,768]{1,0:T(8,128)S(1)}, u32[]{:S(2)}, u32[]{:S(2)}) collective-permute-start(f32[56,768]{1,0:T(8,128)S(1)} %add_add_fusion.refs_0_), channel_id=1, source_target_pairs={{0,1},{1,0},{2,3},{3,2},{4,5},{5,4},{6,7},{7,6},{8,9},{9,8},{10,11... | collective-permute-start | bytes 516104 | tf_op jit(solution)/shard_map/ppermute | solution.py:452
  360.0 37.4 %collective-permute-start.51 = (f32[2,2496]{1,0:T(2,128)S(1)}, f32[2,2496]{1,0:T(2,128)S(1)}, u32[]{:S(2)}, u32[]{:S(2)}) collective-permute-start(f32[2,2496]{1,0:T(2,128)S(1)} %pad_maximum_fusion.1), channel_id=1, source_target_pairs={{0,2},{1,3},{2,0},{3,1},{4,6},{5,7},{6,4},{7,5},{8,10},{9,11},{10,... | collective-permute-start | bytes 59912 | tf_op jit(solution)/shard_map/ppermute | solution.py:452
  401.3 7.6 %collective-permute-start.35 = (f32[56,768]{1,0:T(8,128)S(1)}, f32[56,768]{1,0:T(8,128)S(1)}, u32[]{:S(2)}, u32[]{:S(2)}) collective-permute-start(f32[56,768]{1,0:T(8,128)S(1)} %add_add_fusion.refs_0_), channel_id=1, source_target_pairs={{0,3},{1,2},{2,1},{3,0},{4,7},{5,6},{6,5},{7,4},{8,11},{9,10},{10,... | collective-permute-start | bytes 516104 | tf_op jit(solution)/shard_map/ppermute | solution.py:452
  407.9 8.6 %collective-permute-start.36 = (f32[56,768]{1,0:T(8,128)S(1)}, f32[56,768]{1,0:T(8,128)S(1)}, u32[]{:S(2)}, u32[]{:S(2)}) collective-permute-start(f32[56,768]{1,0:T(8,128)S(1)} %add_add_fusion.refs_0_), channel_id=1, source_target_pairs={{0,4},{1,5},{2,6},{3,7},{4,0},{5,1},{6,2},{7,3},{8,12},{9,13},{10,... | collective-permute-start | bytes 516104 | tf_op jit(solution)/shard_map/ppermute | solution.py:452
  408.9 8.5 %collective-permute-start.37 = (f32[56,768]{1,0:T(8,128)S(1)}, f32[56,768]{1,0:T(8,128)S(1)}, u32[]{:S(2)}, u32[]{:S(2)}) collective-permute-start(f32[56,768]{1,0:T(8,128)S(1)} %add_add_fusion.refs_0_), channel_id=1, source_target_pairs={{0,5},{1,4},{2,7},{3,6},{4,1},{5,0},{6,3},{7,2},{8,13},{9,12},{10,... | collective-permute-start | bytes 516104 | tf_op jit(solution)/shard_map/ppermute | solution.py:452
  416.5 7.7 %collective-permute-start.38 = (f32[56,768]{1,0:T(8,128)S(1)}, f32[56,768]{1,0:T(8,128)S(1)}, u32[]{:S(2)}, u32[]{:S(2)}) collective-permute-start(f32[56,768]{1,0:T(8,128)S(1)} %add_add_fusion.refs_0_), channel_id=1, source_target_pairs={{0,6},{1,7},{2,4},{3,5},{4,2},{5,3},{6,0},{7,1},{8,14},{9,15},{10,... | collective-permute-start | bytes 516104 | tf_op jit(solution)/shard_map/ppermute | solution.py:452
  424.2 11.0 %collective-permute-start.46 = (f32[624,768]{1,0:T(8,128)S(1)}, f32[624,768]{1,0:T(8,128)}, u32[]{:S(2)}, u32[]{:S(2)}) collective-permute-start(f32[624,768]{1,0:T(8,128)S(1)} %collective-permute-done.24.refs_2_), channel_id=1, source_target_pairs={{0,1},{1,0},{2,3},{3,2},{4,5},{5,4},{6,7},{7,6},{8,9},{9,8},{10,11... | collective-permute-start | bytes 5750792 | tf_op jit(solution)/shard_map/ppermute | solution.py:452
  425.0 10.3 %collective-permute-start.47 = (f32[624,768]{1,0:T(8,128)}, f32[624,768]{1,0:T(8,128)}, u32[]{:S(2)}, u32[]{:S(2)}) collective-permute-start(f32[624,768]{1,0:T(8,128)} %collective-permute-done.25.refs_3_), channel_id=1, source_target_pairs={{0,1},{1,0},{2,3},{3,2},{4,5},{5,4},{6,7},{7,6},{8,9},{9,8},{10,11... | collective-permute-start | bytes 5750792 | tf_op jit(solution)/shard_map/ppermute | solution.py:452
  426.3 10.0 %collective-permute-start.44 = (f32[624,768]{1,0:T(8,128)}, f32[624,768]{1,0:T(8,128)}, u32[]{:S(2)}, u32[]{:S(2)}) collective-permute-start(f32[624,768]{1,0:T(8,128)} %get-tuple-element.210), channel_id=1, source_target_pairs={{0,1},{1,0},{2,3},{3,2},{4,5},{5,4},{6,7},{7,6},{8,9},{9,8},{10,11... | collective-permute-start | bytes 5750792 | tf_op jit(solution)/shard_map/ppermute | solution.py:452
  426.4 10.1 %collective-permute-start.45 = (f32[624,768]{1,0:T(8,128)}, f32[624,768]{1,0:T(8,128)}, u32[]{:S(2)}, u32[]{:S(2)}) collective-permute-start(f32[624,768]{1,0:T(8,128)} %get-tuple-element.211), channel_id=1, source_target_pairs={{0,1},{1,0},{2,3},{3,2},{4,5},{5,4},{6,7},{7,6},{8,9},{9,8},{10,11... | collective-permute-start | bytes 5750792 | tf_op jit(solution)/shard_map/ppermute | solution.py:452
  435.1 65.2 %collective-permute-start.54 = (f32[624,768]{1,0:T(8,128)}, f32[624,768]{1,0:T(8,128)}, u32[]{:S(2)}, u32[]{:S(2)}) collective-permute-start(f32[624,768]{1,0:T(8,128)} %get-tuple-element.210), channel_id=1, source_target_pairs={{0,2},{1,3},{2,0},{3,1},{4,6},{5,7},{6,4},{7,5},{8,10},{9,11},{10,... | collective-permute-start | bytes 5750792 | tf_op jit(solution)/shard_map/ppermute | solution.py:452
  435.3 65.0 %collective-permute-start.55 = (f32[624,768]{1,0:T(8,128)}, f32[624,768]{1,0:T(8,128)}, u32[]{:S(2)}, u32[]{:S(2)}) collective-permute-start(f32[624,768]{1,0:T(8,128)} %get-tuple-element.211), channel_id=1, source_target_pairs={{0,4},{1,5},{2,6},{3,7},{4,0},{5,1},{6,2},{7,3},{8,12},{9,13},{10,... | collective-permute-start | bytes 5750792 | tf_op jit(solution)/shard_map/ppermute | solution.py:452
  465.1 46.2 %collective-permute-start.57 = (f32[1296,768]{1,0:T(8,128)}, f32[1296,768]{1,0:T(8,128)}, u32[]{:S(2)}, u32[]{:S(2)}) collective-permute-start(f32[1296,768]{1,0:T(8,128)} %get-tuple-element.214), channel_id=1, source_target_pairs={{0,1},{1,0},{2,3},{3,2},{4,5},{5,4},{6,7},{7,6},{8,9},{9,8},{10,11... | collective-permute-start | bytes 11943944 | tf_op jit(solution)/shard_map/ppermute | solution.py:452
  465.3 30.2 %collective-permute-start.56 = (f32[384,768]{1,0:T(8,128)}, f32[384,768]{1,0:T(8,128)S(1)}, u32[]{:S(2)}, u32[]{:S(2)}) collective-permute-start(f32[384,768]{1,0:T(8,128)} %get-tuple-element.212.refs_0_), channel_id=1, source_target_pairs={{0,8},{8,0},{1,9},{9,1},{2,10},{10,2},{3,11},{11,3},{4,12},{12,4},... | collective-permute-start | bytes 3538952 | tf_op jit(solution)/shard_map/ppermute | solution.py:452
  469.5 35.0 %collective-permute-start.60 = (f32[624,768]{1,0:T(8,128)}, f32[624,768]{1,0:T(8,128)S(1)}, u32[]{:S(2)}, u32[]{:S(2)}) collective-permute-start(f32[624,768]{1,0:T(8,128)} %collective-permute-done.48.refs_6_), channel_id=1, source_target_pairs={{0,1},{1,0},{2,3},{3,2},{4,5},{5,4},{6,7},{7,6},{8,9},{9,8},{10,11... | collective-permute-start | bytes 5750792 | tf_op jit(solution)/shard_map/ppermute | solution.py:452
  495.4 9.2 %collective-permute-start.61 = (f32[624,768]{1,0:T(8,128)}, f32[624,768]{1,0:T(8,128)}, u32[]{:S(2)}, u32[]{:S(2)}) collective-permute-start(f32[624,768]{1,0:T(8,128)} %collective-permute-done.49.refs_7_), channel_id=1, source_target_pairs={{0,1},{1,0},{2,3},{3,2},{4,5},{5,4},{6,7},{7,6},{8,9},{9,8},{10,11... | collective-permute-start | bytes 5750792 | tf_op jit(solution)/shard_map/ppermute | solution.py:452
  500.3 10.9 %collective-permute-start.58 = (f32[624,768]{1,0:T(8,128)}, f32[624,768]{1,0:T(8,128)}, u32[]{:S(2)}, u32[]{:S(2)}) collective-permute-start(f32[624,768]{1,0:T(8,128)} %collective-permute-done.54.refs_2_), channel_id=1, source_target_pairs={{0,1},{1,0},{2,3},{3,2},{4,5},{5,4},{6,7},{7,6},{8,9},{9,8},{10,11... | collective-permute-start | bytes 5750792 | tf_op jit(solution)/shard_map/ppermute | solution.py:452
  500.3 10.9 %collective-permute-start.59 = (f32[624,768]{1,0:T(8,128)}, f32[624,768]{1,0:T(8,128)}, u32[]{:S(2)}, u32[]{:S(2)}) collective-permute-start(f32[624,768]{1,0:T(8,128)} %collective-permute-done.55.refs_3_), channel_id=1, source_target_pairs={{0,1},{1,0},{2,3},{3,2},{4,5},{5,4},{6,7},{7,6},{8,9},{9,8},{10,11... | collective-permute-start | bytes 5750792 | tf_op jit(solution)/shard_map/ppermute | solution.py:452
  (62 other events, 731.1 us)
